TPU v7x, 32 devices: a whole 2x2x4 slice. The times are simulated.
32 devices in a mesh: dom: 8 (over z, x), sub: 4 (over y, core).
Axes of the slice: x: 2, y: 2, z: 4, core: 2. Of those that a mesh axis runs over, the one named last changes fastest.
Arguments:
- load_vector: float32 [64, 128], P(('dom', 'sub')), may hold values from -38 to 38
- recycled: float32 [40, 64, 128], P(None, ('dom', 'sub')), may hold values from -6 to 6
- images: float32 [40, 64, 128], P(None, ('dom', 'sub')), may hold values from -6 to 6
- matrix_tiles: float32 [64, 8, 128, 128], P(('dom', 'sub')), may hold values from -7 to 7
- tile_columns: int32 [64, 8], P(('dom', 'sub')), may hold values from 0 to 5, as said below
- ghost_list: int32 [32, 4], P(('dom', 'sub')), may hold values from 0 to 23, as said below
- live_counts: int32 [32], P(('dom', 'sub')), may hold values from 1 to 2, as said below
Outputs:
- solution: float32 [64, 128], P(('dom', 'sub'))
- residual: float32 [64, 128], P(('dom', 'sub'))
Inputs may be any that keep to these rules, and one draw needn't show every extreme that they name: `live_counts`: each device's live block rows are its first slots; some device has all 2 live. `tile_columns`: tile 0 of a block row names the row's own slot. Other entries below 2 name a live slot of the same device; entries from 2 on name a ghost slot of that device. `ghost_list`: each entry names a live slot q of a device with sub index s and dom index differing from the owner's by o - 1 (o of 0, 1, 2), coded as o * (size of sub) * 2 + s * 2 + q; it never points outside the dom axis and never to the owner itself.
All inputs are finite; a program needn't handle non-finite values.
Results may differ from a plain program's by a relative error of at most 0.0003.
Values sent between devices are 32-bit elements; how exact they have to be, the bound alone decides.
No kernel may reach another device: no remote copies, remote signals or barrier semaphores. Data moves between devices by JAX's collectives and lax.ppermute only.
A program may use at most 64 MiB of HBM per device.

v0:
```python
import jax
import jax.numpy as jnp
from jax import lax
from jax.sharding import PartitionSpec as P

STEPS = 3


def padded(value, sides, width):
    for axis, dim in sides:
        count, length = (lax.axis_size(axis), value.shape[dim])
        up = [(i, (i + 1) % count) for i in range(count - 1)]
        down = [(j, i) for i, j in up]
        last = lax.slice_in_dim(value, length - width, length, axis=dim)
        first = lax.slice_in_dim(value, 0, width, axis=dim)
        before = lax.ppermute(last, axis, up)
        after = lax.ppermute(first, axis, down)
        value = jnp.concatenate([before, value, after], axis=dim)
    return value


def triangle_solve(factor, values, transpose):
    column = values if values.ndim == 2 else values[:, None]
    solved = lax.linalg.triangular_solve(
        factor, column, left_side=True, lower=True, transpose_a=transpose
    )
    return solved if values.ndim == 2 else solved[:, 0]


def multiply(vector, matrix_tiles, tile_columns, ghost_codes):
    slot_count = vector.shape[0]
    group_size = lax.axis_size("sub") * slot_count
    gathered = lax.all_gather(vector, "sub", axis=0, tiled=True)
    nearby = padded(gathered, (("dom", 0),), group_size)
    ghosts = jnp.take(nearby, ghost_codes, axis=0)
    extended = jnp.concatenate([vector, ghosts], axis=0)
    picked = jnp.take(extended, tile_columns, axis=0)
    return jnp.einsum("stij,stj->si", matrix_tiles, picked, precision=lax.Precision.HIGHEST)


def local(load_vector, recycled, images, matrix_tiles, tile_columns, ghost_list, live_counts):
    highest = lax.Precision.HIGHEST
    slot_count, tile_width = load_vector.shape
    recycled_count = recycled.shape[0]
    live_mask = (jnp.arange(slot_count) < live_counts[0]).astype(jnp.float32)[:, None]
    ghost_codes = ghost_list[0]
    source = (load_vector * live_mask).reshape(-1)
    recycled_flat = (recycled * live_mask[None]).reshape(recycled_count, -1)
    images_flat = (images * live_mask[None]).reshape(recycled_count, -1)
    gram_matrix, projection, source_norm = lax.psum(
        (
            jnp.dot(images_flat, images_flat.T, precision=highest),
            jnp.dot(images_flat, source, precision=highest),
            jnp.sum(source * source),
        ),
        ("dom", "sub"),
    )
    cholesky_low = jnp.linalg.cholesky(gram_matrix)
    reduced = triangle_solve(cholesky_low, projection, False)
    initial_norm = jnp.sqrt(source_norm - jnp.sum(reduced * reduced))
    images_hat = triangle_solve(cholesky_low, images_flat, False)
    recycled_hat = triangle_solve(cholesky_low, recycled_flat, False)
    start_point = jnp.dot(reduced, recycled_hat, precision=highest)
    start_residual = source - jnp.dot(reduced, images_hat, precision=highest)
    basis = [start_residual / initial_norm]
    hessenberg = jnp.zeros((STEPS + 1, STEPS), jnp.float32)
    coupling = jnp.zeros((recycled_count, STEPS), jnp.float32)
    for column in range(STEPS):
        image_now = multiply(
            basis[column].reshape(slot_count, tile_width), matrix_tiles, tile_columns, ghost_codes
        )
        image_now = (image_now * live_mask).reshape(-1)
        stacked = jnp.stack(basis)
        local_images = jnp.dot(images_hat, image_now, precision=highest)
        summed_images, against_basis, image_norm = lax.psum(
            (
                local_images,
                jnp.dot(stacked, image_now, precision=highest),
                jnp.sum(image_now * image_now),
            ),
            ("dom", "sub"),
        )
        correction = jnp.dot(summed_images, images_hat, precision=highest)
        next_norm = jnp.sqrt(
            image_norm
            - jnp.sum(summed_images * summed_images)
            - jnp.sum(against_basis * against_basis)
        )
        remaining = image_now - correction - jnp.dot(against_basis, stacked, precision=highest)
        basis.append(remaining / next_norm)
        hessenberg = hessenberg.at[: column + 1, column].set(against_basis)
        hessenberg = hessenberg.at[column + 1, column].set(next_norm)
        coupling = coupling.at[:, column].set(summed_images)
    normal_matrix = jnp.dot(hessenberg.T, hessenberg, precision=highest)
    target = initial_norm * hessenberg[0]
    small_factor = jnp.linalg.cholesky(normal_matrix)
    least = triangle_solve(small_factor, triangle_solve(small_factor, target, False), True)
    every_basis = jnp.stack(basis)
    coupled = jnp.dot(coupling, least, precision=highest)
    recycled_term = jnp.dot(coupled, recycled_hat, precision=highest)
    solution = start_point + jnp.dot(least, every_basis[:STEPS], precision=highest) - recycled_term
    residual = start_residual - jnp.dot(
        jnp.dot(hessenberg, least, precision=highest), every_basis, precision=highest
    )
    return (solution.reshape(slot_count, tile_width), residual.reshape(slot_count, tile_width))


def solution(mesh):
    return jax.shard_map(
        local,
        mesh=mesh,
        in_specs=(
            P(("dom", "sub"), None),
            P(None, ("dom", "sub"), None),
            P(None, ("dom", "sub"), None),
            P(("dom", "sub"), None, None, None),
            P(("dom", "sub"), None),
            P(("dom", "sub"), None),
            P(("dom", "sub")),
        ),
        out_specs=(P(("dom", "sub"), None), P(("dom", "sub"), None)),
        check_vma=False,
    )
```

profile of v0, /device:TPU:0, one launch (start us, length us, event | category | flops | bytes accessed | tf_op | source)
XLA Modules:
  0.0 252.3 jit_solution(12142202452177539300)
XLA Ops:
  1.4 0.9 broadcast_multiply_fusion
  3.8 42.4 %all-reduce.5 = (f32[40,40]{0,1:T(8,128)S(1)}, f32[]{:T(128)}, f32[40]{0:T(128)S(1)}) all-reduce(f32[40,40]{0,1:T(8,128)S(1)} %convolution_bitcast_fusion, f32[]{:T(128)} %get-tuple-element.131, f32[40]{0:T(128)S(1)} %convolution_bitcast_fusion.5), channel_id=1, replica_groups=mesh['dom'=8,'sub'=4] {'dom','sub'}, use_global_device_ids=true, to_apply=%region_0.0 | all-reduce | flops 1641 | bytes 13128 | tf_op jit(solution)/shard_map/psum | solution.py:50
  46.3 3.6 %cholesky.29 = f32[40,40]{1,0:T(8,128)S(1)} custom-call(f32[40,40]{1,0:T(8,128)S(1)} %fusion.13), custom_call_target="Cholesky" | custom-call | tf_op jit(solution)/shard_map/jit(cholesky)/cholesky | solution.py:58
  51.3 3.1 %custom-call.17 = f32[1,40,40]{1,2,0:T(8,128)S(1)} custom-call(f32[1,40,40]{2,1,0:T(8,128)S(1)} %fusion.8), custom_call_target="InvertDiagBlocksLowerTriangular" | custom-call | tf_op jit(solution)/shard_map/triangular_solve | solution.py:24
  54.6 0.7 fusion.47
  56.8 5.2 %all-gather = f32[4,2,128]{2,1,0:T(2,128)S(1)} all-gather(f32[1,2,128]{2,1,0:T(2,128)S(1)} %bitcast.252), channel_id=1, replica_groups=mesh['dom'=8,'sub'=4] {'sub'}, dimensions={0}, use_global_device_ids=true | all-gather | bytes 5120 | tf_op jit(solution)/shard_map/all_gather | solution.py:33
  62.0 1.4 collective-permute-start.1
  63.4 4.7 %collective-permute-start = (f32[8,128]{1,0:T(8,128)S(1)}, f32[8,128]{1,0:T(8,128)S(1)}, u32[]{:S(2)}, u32[]{:S(2)}) collective-permute-start(f32[8,128]{1,0:T(8,128)S(1)} %bitcast.262), channel_id=1, source_target_pairs={{0,4},{4,8},{8,12},{12,16},{16,20},{20,24},{24,28},{1,5},{5,9},{9,... | collective-permute-start | bytes 12296 | tf_op jit(solution)/shard_map/ppermute | solution.py:16
  69.6 0.7 and_reduce_fusion
  70.7 0.7 compare_reduce_fusion.1
  72.6 1.0 fusion.61
  73.6 0.7 fusion.30
  75.0 40.7 %all-reduce.4 = (f32[40]{0:T(128)S(1)}, f32[]{:T(128)}, f32[1]{0:T(128)}) all-reduce(f32[40]{0:T(128)S(1)} %convolution_bitcast_fusion.4, f32[]{:T(128)} %multiply_reduce_fusion.3, f32[1]{0:T(128)} %bitcast.29), channel_id=1, replica_groups=mesh['dom'=8,'sub'=4] {'dom','sub'}, use_global_device_ids=true, to_apply=%region_10.14 | all-reduce | flops 42 | bytes 336 | tf_op jit(solution)/shard_map/psum | solution.py:75
  115.9 1.3 multiply_reduce_fusion.9
  120.5 5.5 %all-gather.1 = f32[4,2,128]{2,1,0:T(2,128)S(1)} all-gather(f32[1,2,128]{2,1,0:T(2,128)S(1)} %bitcast.270), channel_id=1, replica_groups=mesh['dom'=8,'sub'=4] {'sub'}, dimensions={0}, use_global_device_ids=true | all-gather | bytes 5120 | tf_op jit(solution)/shard_map/all_gather | solution.py:33
  126.0 1.3 collective-permute-start.3
  127.2 4.5 %collective-permute-start.2 = (f32[8,128]{1,0:T(8,128)S(1)}, f32[8,128]{1,0:T(8,128)S(1)}, u32[]{:S(2)}, u32[]{:S(2)}) collective-permute-start(f32[8,128]{1,0:T(8,128)S(1)} %bitcast.268), channel_id=1, source_target_pairs={{0,4},{4,8},{8,12},{12,16},{16,20},{20,24},{24,28},{1,5},{5,9},{9,... | collective-permute-start | bytes 12296 | tf_op jit(solution)/shard_map/ppermute | solution.py:16
  135.8 1.0 fusion.62
  136.8 0.7 multiply_reduce_fusion.2
  137.8 41.0 %all-reduce.3 = (f32[40]{0:T(128)S(1)}, f32[2]{0:T(128)S(1)}, f32[]{:T(128)}) all-reduce(f32[40]{0:T(128)S(1)} %convolution_bitcast_fusion.3, f32[2]{0:T(128)S(1)} %convolution_bitcast_fusion.10, f32[]{:T(128)} %get-tuple-element.127), channel_id=1, replica_groups=mesh['dom'=8,'sub'=4] {'dom','sub'}, use_global_device_ids=true, to_apply=%region_16.20 | all-reduce | flops 43 | bytes 344 | tf_op jit(solution)/shard_map/psum | solution.py:75
  178.7 0.7 multiply_reduce_fusion.7
  179.7 1.2 multiply_reduce_fusion.8
  182.9 5.5 %all-gather.2 = f32[4,2,128]{2,1,0:T(2,128)S(1)} all-gather(f32[1,2,128]{2,1,0:T(2,128)S(1)} %bitcast.278), channel_id=1, replica_groups=mesh['dom'=8,'sub'=4] {'sub'}, dimensions={0}, use_global_device_ids=true | all-gather | bytes 5120 | tf_op jit(solution)/shard_map/all_gather | solution.py:33
  188.4 1.3 collective-permute-start.5
  189.7 4.5 %collective-permute-start.4 = (f32[8,128]{1,0:T(8,128)S(1)}, f32[8,128]{1,0:T(8,128)S(1)}, u32[]{:S(2)}, u32[]{:S(2)}) collective-permute-start(f32[8,128]{1,0:T(8,128)S(1)} %bitcast.265), channel_id=1, source_target_pairs={{0,4},{4,8},{8,12},{12,16},{16,20},{20,24},{24,28},{1,5},{5,9},{9,... | collective-permute-start | bytes 12296 | tf_op jit(solution)/shard_map/ppermute | solution.py:16
  194.2 1.9 broadcast_select_fusion.6
  196.1 1.3 scatter.34
  199.0 1.0 fusion.63
  199.9 0.7 multiply_reduce_fusion.1
  200.9 40.7 %all-reduce.2 = (f32[40]{0:T(128)S(1)}, f32[3]{0:T(128)S(1)}, f32[]{:T(128)}) all-reduce(f32[40]{0:T(128)S(1)} %convolution_bitcast_fusion.1, f32[3]{0:T(128)S(1)} %convolution_bitcast_fusion.2, f32[]{:T(128)} %get-tuple-element.125), channel_id=1, replica_groups=mesh['dom'=8,'sub'=4] {'dom','sub'}, use_global_device_ids=true, to_apply=%region_23.27 | all-reduce | flops 44 | bytes 352 | tf_op jit(solution)/shard_map/psum | solution.py:75
  242.1 2.0 broadcast_select_fusion.5
  244.1 1.4 scatter.36
  (101 shorter events, 19.5 us)
Async XLA Ops:
  0.6 72.0 %copy-start = (f32[2,8,128,128]{3,2,1,0:T(8,128)S(1)}, f32[2,8,128,128]{3,2,1,0:T(8,128)}, u32[]{:S(2)}) copy-start(f32[2,8,128,128]{3,2,1,0:T(8,128)} %param.34) | copy-start | bytes 3145732
  2.3 0.7 copy-start.1
  62.0 6.2 %copy-start.3 = (s32[1,4]{1,0:T(1,128)S(1)}, s32[1,4]{1,0:T(1,128)}, u32[]{:S(2)}) copy-start(s32[1,4]{1,0:T(1,128)} %param.36) | copy-start | bytes 52
  62.0 9.4 %collective-permute-start.1 = (f32[8,128]{1,0:T(8,128)S(1)}, f32[8,128]{1,0:T(8,128)S(1)}, u32[]{:S(2)}, u32[]{:S(2)}) collective-permute-start(f32[8,128]{1,0:T(8,128)S(1)} %bitcast.261), channel_id=1, source_target_pairs={{4,0},{8,4},{12,8},{16,12},{20,16},{24,20},{28,24},{5,1},{9,5},{13... | collective-permute-start | bytes 12296 | tf_op jit(solution)/shard_map/ppermute | solution.py:17
  63.4 8.0 %collective-permute-start = (f32[8,128]{1,0:T(8,128)S(1)}, f32[8,128]{1,0:T(8,128)S(1)}, u32[]{:S(2)}, u32[]{:S(2)}) collective-permute-start(f32[8,128]{1,0:T(8,128)S(1)} %bitcast.262), channel_id=1, source_target_pairs={{0,4},{4,8},{8,12},{12,16},{16,20},{20,24},{24,28},{1,5},{5,9},{9,... | collective-permute-start | bytes 12296 | tf_op jit(solution)/shard_map/ppermute | solution.py:16
  68.1 0.7 copy-start.2
  68.9 0.7 copy-start.4
  126.0 8.6 %collective-permute-start.3 = (f32[8,128]{1,0:T(8,128)S(1)}, f32[8,128]{1,0:T(8,128)S(1)}, u32[]{:S(2)}, u32[]{:S(2)}) collective-permute-start(f32[8,128]{1,0:T(8,128)S(1)} %bitcast.267), channel_id=1, source_target_pairs={{4,0},{8,4},{12,8},{16,12},{20,16},{24,20},{28,24},{5,1},{9,5},{13... | collective-permute-start | bytes 12296 | tf_op jit(solution)/shard_map/ppermute | solution.py:17
  127.2 7.3 %collective-permute-start.2 = (f32[8,128]{1,0:T(8,128)S(1)}, f32[8,128]{1,0:T(8,128)S(1)}, u32[]{:S(2)}, u32[]{:S(2)}) collective-permute-start(f32[8,128]{1,0:T(8,128)S(1)} %bitcast.268), channel_id=1, source_target_pairs={{0,4},{4,8},{8,12},{12,16},{16,20},{20,24},{24,28},{1,5},{5,9},{9,... | collective-permute-start | bytes 12296 | tf_op jit(solution)/shard_map/ppermute | solution.py:16
  188.4 9.2 %collective-permute-start.5 = (f32[8,128]{1,0:T(8,128)S(1)}, f32[8,128]{1,0:T(8,128)S(1)}, u32[]{:S(2)}, u32[]{:S(2)}) collective-permute-start(f32[8,128]{1,0:T(8,128)S(1)} %bitcast.264), channel_id=1, source_target_pairs={{4,0},{8,4},{12,8},{16,12},{20,16},{24,20},{28,24},{5,1},{9,5},{13... | collective-permute-start | bytes 12296 | tf_op jit(solution)/shard_map/ppermute | solution.py:17
  189.7 8.0 %collective-permute-start.4 = (f32[8,128]{1,0:T(8,128)S(1)}, f32[8,128]{1,0:T(8,128)S(1)}, u32[]{:S(2)}, u32[]{:S(2)}) collective-permute-start(f32[8,128]{1,0:T(8,128)S(1)} %bitcast.265), channel_id=1, source_target_pairs={{0,4},{4,8},{8,12},{12,16},{16,20},{20,24},{24,28},{1,5},{5,9},{9,... | collective-permute-start | bytes 12296 | tf_op jit(solution)/shard_map/ppermute | solution.py:16
where the time goes:
time: 254 us; the launch traced here: 252 us
  blocking collectives  181 us (71%)
  other arithmetic  26.9 us (11%)
  starting transfers between devices  17.8 us (7%)
  local copies, waits for them, and re-layouts  9.88 us (4%)
  between operations  9.6 us (4%)
  matrix products  7.11 us (3%)
    psum x3, blocking collectives, local(): lax.psum((local_images, jnp.dot(stacked, image_now, precision=highest), j...  122 us
    psum x1, blocking collectives, local(): lax.psum((jnp.dot(images_flat, images_flat.T, precision=highest), jnp.dot...  42.4 us
    all_gather x3, blocking collectives, multiply(): gathered = lax.all_gather(vector, 'sub', axis=0, tiled=True)  16.2 us
    ppermute x3, starting transfers between devices, padded(): before = lax.ppermute(last, axis, up)  13.8 us
    another operation x7, other arithmetic  6.56 us
  transfers between devices with their start and end apart: 6, of which 0 were waited for; matrix products, arithmetic and copies ran while one was open for 3% of the time, Pallas kernels for 0%

commit v1 on v0

--- a/solution.py
+++ b/solution.py
@@ -4,6 +4,23 @@
 from jax.sharding import PartitionSpec as P
 
 STEPS = 3
+
+
+def total(values):
+    axes = ("dom", "sub")
+    flat = jnp.concatenate([value.reshape(-1) for value in values])
+    lanes = 128
+    rows = -(-flat.shape[0] // lanes)
+    packed = jnp.pad(flat, (0, rows * lanes - flat.shape[0])).reshape(rows, lanes)
+    count = lax.axis_size("dom") * lax.axis_size("sub")
+    every = lax.all_to_all(jnp.broadcast_to(packed[None], (count, rows, lanes)), axes, 0, 0)
+    summed = jnp.sum(every, axis=0).reshape(-1)
+    results = []
+    offset = 0
+    for value in values:
+        results.append(summed[offset : offset + value.size].reshape(value.shape))
+        offset += value.size
+    return results
 
 
 def padded(value, sides, width):
@@ -47,13 +64,12 @@
     source = (load_vector * live_mask).reshape(-1)
     recycled_flat = (recycled * live_mask[None]).reshape(recycled_count, -1)
     images_flat = (images * live_mask[None]).reshape(recycled_count, -1)
-    gram_matrix, projection, source_norm = lax.psum(
+    gram_matrix, projection, source_norm = total(
         (
             jnp.dot(images_flat, images_flat.T, precision=highest),
             jnp.dot(images_flat, source, precision=highest),
             jnp.sum(source * source),
-        ),
-        ("dom", "sub"),
+        )
     )
     cholesky_low = jnp.linalg.cholesky(gram_matrix)
     reduced = triangle_solve(cholesky_low, projection, False)
@@ -72,13 +88,12 @@
         image_now = (image_now * live_mask).reshape(-1)
         stacked = jnp.stack(basis)
         local_images = jnp.dot(images_hat, image_now, precision=highest)
-        summed_images, against_basis, image_norm = lax.psum(
+        summed_images, against_basis, image_norm = total(
             (
                 local_images,
                 jnp.dot(stacked, image_now, precision=highest),
                 jnp.sum(image_now * image_now),
-            ),
-            ("dom", "sub"),
+            )
         )
         correction = jnp.dot(summed_images, images_hat, precision=highest)
         next_norm = jnp.sqrt(

time: 254 us -> 141 us (0.56)
  blocking collectives: 181 us -> 15.2 us
  waiting for transfers between devices: 0.02 us -> 32.9 us
  starting transfers between devices: 17.8 us -> 27.6 us
  local copies, waits for them, and re-layouts: 9.88 us -> 17.2 us
  other arithmetic: 26.9 us -> 30.1 us
    psum x4 -> x0, blocking collectives: 165 us -> none  [the longest x3 122 us: local(): lax.psum((local_images, jnp.dot(stacked, image_now, precision=highest), j...]
    all_to_all x0 -> x4, waiting for transfers between devices: none -> 24.7 us  [total(): lax.all_to_all(jnp.broadcast_to(packed[None], (count, rows, lanes)), axes...]
    all_to_all x0 -> x4, starting transfers between devices: none -> 16 us  [total(): lax.all_to_all(jnp.broadcast_to(packed[None], (count, rows, lanes)), axes...]
    ppermute x3, waiting for transfers between devices: 0.01 us -> 8.18 us  [padded(): after = lax.ppermute(first, axis, down)]
    ppermute x3, starting transfers between devices: 13.8 us -> 7.67 us  [padded(): before = lax.ppermute(last, axis, up)]
    concatenate x0 -> x3, other arithmetic: none -> 2.9 us  [total(): flat = jnp.concatenate([value.reshape(-1) for value in values])]
    broadcast_in_dim x0 -> x5, local copies, waits for them, and re-layouts: none -> 2.55 us  [total(): jnp.broadcast_to(packed[None], (count, rows, lanes))]
    another operation x7 -> x9, other arithmetic: 6.56 us -> 7.76 us
  transfers between devices with their start and end apart: 6 -> 10, of which waited for: 0 -> 7; matrix products, arithmetic and copies ran while one was open for 3% -> 7% of each run, Pallas kernels for 0% -> 0%
where the time goes in v1:
time: 141 us; the launch traced here: 140 us
  waiting for transfers between devices  32.9 us (23%)
  other arithmetic  30.1 us (21%)
  starting transfers between devices  27.6 us (20%)
  local copies, waits for them, and re-layouts  17.2 us (12%)
  blocking collectives  15.2 us (11%)
  between operations  9.81 us (7%)
  matrix products  7.36 us (5%)
    all_to_all x4, waiting for transfers between devices, total(): lax.all_to_all(jnp.broadcast_to(packed[None], (count, rows, lanes)), axes...  24.7 us
    all_to_all x4, starting transfers between devices, total(): lax.all_to_all(jnp.broadcast_to(packed[None], (count, rows, lanes)), axes...  16 us
    all_gather x3, blocking collectives, multiply(): gathered = lax.all_gather(vector, 'sub', axis=0, tiled=True)  15.2 us
    ppermute x3, waiting for transfers between devices, padded(): after = lax.ppermute(first, axis, down)  8.18 us
    another operation x9, other arithmetic  7.76 us
    ppermute x3, starting transfers between devices, padded(): before = lax.ppermute(last, axis, up)  7.67 us
    another operation x4, other arithmetic, triangle_solve(): lax.linalg.triangular_solve(factor, column, left_side=True, lower=True, t...  4.62 us
    another operation x3, other arithmetic, local(): cholesky_low = jnp.linalg.cholesky(gram_matrix)  4.33 us
  transfers between devices with their start and end apart: 10, of which 7 were waited for; matrix products, arithmetic and copies ran while one was open for 7% of the time, Pallas kernels for 0%

profile of v1, /device:TPU:0, one launch (start us, length us, event | category | flops | bytes accessed | tf_op | source)
XLA Modules:
  0.0 140.2 jit_solution(14159245760804955157)
XLA Ops:
  2.7 0.9 broadcast_multiply_fusion
  5.5 7.3 %all-to-all-start = ((f32[32,13,128]{2,1,0:T(8,128)}), f32[32,13,128]{2,1,0:T(8,128)S(1)}, u32[]{:S(2)}, u32[]{:S(2)}) async-start(f32[32,13,128]{2,1,0:T(8,128)} %broadcast_in_dim.47), calls=%async_computation | async-start | bytes 524288 | tf_op jit(solution)/shard_map/all_to_all | solution.py:16
  16.2 7.2 %all-to-all-done = f32[32,13,128]{2,1,0:T(8,128)S(1)} async-done(((f32[32,13,128]{2,1,0:T(8,128)}), f32[32,13,128]{2,1,0:T(8,128)S(1)}, u32[]{:S(2)}, u32[]{:S(2)}) %all-to-all-start) | async-done | bytes 213024 | tf_op jit(solution)/shard_map/all_to_all | solution.py:16
  24.2 3.6 %cholesky.29 = f32[40,40]{1,0:T(8,128)S(1)} custom-call(f32[40,40]{1,0:T(8,128)S(1)} %fusion.13), custom_call_target="Cholesky" | custom-call | tf_op jit(solution)/shard_map/jit(cholesky)/cholesky | solution.py:74
  29.2 3.1 %custom-call.17 = f32[1,40,40]{1,2,0:T(8,128)S(1)} custom-call(f32[1,40,40]{2,1,0:T(8,128)S(1)} %fusion.8), custom_call_target="InvertDiagBlocksLowerTriangular" | custom-call | tf_op jit(solution)/shard_map/triangular_solve | solution.py:41
  32.2 0.8 fusion.50
  34.8 5.1 %all-gather = f32[4,2,128]{2,1,0:T(2,128)S(1)} all-gather(f32[1,2,128]{2,1,0:T(2,128)S(1)} %bitcast.294), channel_id=1, replica_groups=mesh['dom'=8,'sub'=4] {'sub'}, dimensions={0}, use_global_device_ids=true | all-gather | bytes 5120 | tf_op jit(solution)/shard_map/all_gather | solution.py:50
  39.8 2.8 %collective-permute-start = (f32[8,128]{1,0:T(8,128)S(1)}, f32[8,128]{1,0:T(8,128)S(1)}, u32[]{:S(2)}, u32[]{:S(2)}) collective-permute-start(f32[8,128]{1,0:T(8,128)S(1)} %bitcast.306), channel_id=1, source_target_pairs={{0,4},{4,8},{8,12},{12,16},{16,20},{20,24},{24,28},{1,5},{5,9},{9,... | collective-permute-start | bytes 12296 | tf_op jit(solution)/shard_map/ppermute | solution.py:33
  42.6 1.3 collective-permute-start.1
  46.0 2.2 %collective-permute-done.1 = f32[8,128]{1,0:T(8,128)S(1)} collective-permute-done((f32[8,128]{1,0:T(8,128)S(1)}, f32[8,128]{1,0:T(8,128)S(1)}, u32[]{:S(2)}, u32[]{:S(2)}) %collective-permute-start.1) | collective-permute-done | bytes 4128 | tf_op jit(solution)/shard_map/ppermute | solution.py:34
  49.4 1.0 fusion.68
  51.8 1.4 select_maximum_fusion.4
  53.8 3.2 %all-to-all-start.1 = ((f32[32,1,128]{2,1,0:T(1,128)}), f32[32,1,128]{2,1,0:T(1,128)S(1)}, u32[]{:S(2)}, u32[]{:S(2)}) async-start(f32[32,1,128]{2,1,0:T(1,128)} %broadcast_in_dim.48), calls=%async_computation.1 | async-start | bytes 32768 | tf_op jit(solution)/shard_map/all_to_all | solution.py:16
  57.2 6.9 %all-to-all-done.1 = f32[32,1,128]{2,1,0:T(1,128)S(1)} async-done(((f32[32,1,128]{2,1,0:T(1,128)}), f32[32,1,128]{2,1,0:T(1,128)S(1)}, u32[]{:S(2)}, u32[]{:S(2)}) %all-to-all-start.1) | async-done | bytes 16416 | tf_op jit(solution)/shard_map/all_to_all | solution.py:16
  68.9 5.1 %all-gather.1 = f32[4,2,128]{2,1,0:T(2,128)S(1)} all-gather(f32[1,2,128]{2,1,0:T(2,128)S(1)} %bitcast.312), channel_id=1, replica_groups=mesh['dom'=8,'sub'=4] {'sub'}, dimensions={0}, use_global_device_ids=true | all-gather | bytes 5120 | tf_op jit(solution)/shard_map/all_gather | solution.py:50
  74.0 2.4 %collective-permute-start.2 = (f32[8,128]{1,0:T(8,128)S(1)}, f32[8,128]{1,0:T(8,128)S(1)}, u32[]{:S(2)}, u32[]{:S(2)}) collective-permute-start(f32[8,128]{1,0:T(8,128)S(1)} %bitcast.309), channel_id=1, source_target_pairs={{0,4},{4,8},{8,12},{12,16},{16,20},{20,24},{24,28},{1,5},{5,9},{9,... | collective-permute-start | bytes 12296 | tf_op jit(solution)/shard_map/ppermute | solution.py:33
  76.4 1.3 collective-permute-start.3
  77.9 4.1 %collective-permute-done.3 = f32[8,128]{1,0:T(8,128)S(1)} collective-permute-done((f32[8,128]{1,0:T(8,128)S(1)}, f32[8,128]{1,0:T(8,128)S(1)}, u32[]{:S(2)}, u32[]{:S(2)}) %collective-permute-start.3) | collective-permute-done | bytes 4128 | tf_op jit(solution)/shard_map/ppermute | solution.py:34
  83.2 1.0 fusion.69
  86.6 2.8 %all-to-all-start.2 = ((f32[32,1,128]{2,1,0:T(1,128)}), f32[32,1,128]{2,1,0:T(1,128)S(1)}, u32[]{:S(2)}, u32[]{:S(2)}) async-start(f32[32,1,128]{2,1,0:T(1,128)} %broadcast_in_dim.49), calls=%async_computation.2 | async-start | bytes 32768 | tf_op jit(solution)/shard_map/all_to_all | solution.py:16
  90.7 5.8 %all-to-all-done.2 = f32[32,1,128]{2,1,0:T(1,128)S(1)} async-done(((f32[32,1,128]{2,1,0:T(1,128)}), f32[32,1,128]{2,1,0:T(1,128)S(1)}, u32[]{:S(2)}, u32[]{:S(2)}) %all-to-all-start.2) | async-done | bytes 16416 | tf_op jit(solution)/shard_map/all_to_all | solution.py:16
  100.9 5.1 %all-gather.2 = f32[4,2,128]{2,1,0:T(2,128)S(1)} all-gather(f32[1,2,128]{2,1,0:T(2,128)S(1)} %bitcast.320), channel_id=1, replica_groups=mesh['dom'=8,'sub'=4] {'sub'}, dimensions={0}, use_global_device_ids=true | all-gather | bytes 5120 | tf_op jit(solution)/shard_map/all_gather | solution.py:50
  106.0 2.4 %collective-permute-start.4 = (f32[8,128]{1,0:T(8,128)S(1)}, f32[8,128]{1,0:T(8,128)S(1)}, u32[]{:S(2)}, u32[]{:S(2)}) collective-permute-start(f32[8,128]{1,0:T(8,128)S(1)} %bitcast.303), channel_id=1, source_target_pairs={{0,4},{4,8},{8,12},{12,16},{16,20},{20,24},{24,28},{1,5},{5,9},{9,... | collective-permute-start | bytes 12296 | tf_op jit(solution)/shard_map/ppermute | solution.py:33
  108.4 1.3 collective-permute-start.5
  109.9 2.1 %dynamic-slice_select_fusion.1 = f32[2,1]{1,0:T(2,128)S(1)} fusion(f32[2,1]{1,0:T(2,128)S(1)} %copy.43, f32[4,3]{1,0:T(4,128)S(1)} %scatter.31, s32[]{:T(128)} %bitcast.65, s32[]{:T(128)} %bitcast.66, pred[]{:T(512)} %compare_reduce_fusion.3), kind=kLoop, calls=%fused_computation.99 | loop fusion | flops 2 | bytes 33 | tf_op jit(solution)/shard_map/select.30
  112.0 1.9 %collective-permute-done.5 = f32[8,128]{1,0:T(8,128)S(1)} collective-permute-done((f32[8,128]{1,0:T(8,128)S(1)}, f32[8,128]{1,0:T(8,128)S(1)}, u32[]{:S(2)}, u32[]{:S(2)}) %collective-permute-start.5) | collective-permute-done | bytes 4128 | tf_op jit(solution)/shard_map/ppermute | solution.py:34
  115.2 1.0 fusion.70
  118.5 2.8 %all-to-all-start.3 = ((f32[32,1,128]{2,1,0:T(1,128)}), f32[32,1,128]{2,1,0:T(1,128)S(1)}, u32[]{:S(2)}, u32[]{:S(2)}) async-start(f32[32,1,128]{2,1,0:T(1,128)} %broadcast_in_dim.50), calls=%async_computation.3 | async-start | bytes 32768 | tf_op jit(solution)/shard_map/all_to_all | solution.py:16
  121.8 1.7 %scatter.34 = f32[4,3]{1,0:T(4,128)S(1)} dynamic-update-slice(f32[4,3]{1,0:T(4,128)S(1)} %scatter.31, f32[2,1]{1,0:T(2,128)S(1)} %dynamic-slice_select_fusion.1, s32[]{:T(128)} %bitcast.65, s32[]{:T(128)} %bitcast.66) | dynamic-update-slice | bytes 20 | tf_op jit(solution)/shard_map/scatter | solution.py:106
  123.6 4.8 %all-to-all-done.3 = f32[32,1,128]{2,1,0:T(1,128)S(1)} async-done(((f32[32,1,128]{2,1,0:T(1,128)}), f32[32,1,128]{2,1,0:T(1,128)S(1)}, u32[]{:S(2)}, u32[]{:S(2)}) %all-to-all-start.3) | async-done | bytes 16416 | tf_op jit(solution)/shard_map/all_to_all | solution.py:16
  132.9 1.9 %dynamic-slice_select_fusion = f32[3,1]{1,0:T(4,128)S(1)} fusion(f32[3,1]{1,0:T(4,128)S(1)} %copy.45, f32[4,3]{1,0:T(4,128)S(1)} %scatter.35, s32[]{:T(128)} %bitcast.93, s32[]{:T(128)} %bitcast.94, pred[]{:T(512)} %and_reduce_fusion), kind=kLoop, calls=%fused_computation.69 | loop fusion | flops 3 | bytes 45 | tf_op jit(solution)/shard_map/select.32
  134.8 1.5 %scatter.36 = f32[4,3]{1,0:T(4,128)S(1)} dynamic-update-slice(f32[4,3]{1,0:T(4,128)S(1)} %scatter.35, f32[3,1]{1,0:T(4,128)S(1)} %dynamic-slice_select_fusion, s32[]{:T(128)} %bitcast.93, s32[]{:T(128)} %bitcast.94) | dynamic-update-slice | bytes 28 | tf_op jit(solution)/shard_map/scatter | solution.py:106
  (130 shorter events, 34.9 us)
Async XLA Ops:
  0.6 48.8 %copy-start = (f32[2,8,128,128]{3,2,1,0:T(8,128)S(1)}, f32[2,8,128,128]{3,2,1,0:T(8,128)}, u32[]{:S(2)}) copy-start(f32[2,8,128,128]{3,2,1,0:T(8,128)} %param.34) | copy-start | bytes 3145732
  1.4 0.7 copy-start.1
  5.5 17.9 %all-to-all-start = ((f32[32,13,128]{2,1,0:T(8,128)}), f32[32,13,128]{2,1,0:T(8,128)S(1)}, u32[]{:S(2)}, u32[]{:S(2)}) async-start(f32[32,13,128]{2,1,0:T(8,128)} %broadcast_in_dim.47), calls=%async_computation | async-start | bytes 524288 | tf_op jit(solution)/shard_map/all_to_all | solution.py:16
  12.8 0.7 copy-start.3
  13.5 0.7 copy-start.2
  14.9 0.7 copy-start.4
  39.8 6.1 %collective-permute-start = (f32[8,128]{1,0:T(8,128)S(1)}, f32[8,128]{1,0:T(8,128)S(1)}, u32[]{:S(2)}, u32[]{:S(2)}) collective-permute-start(f32[8,128]{1,0:T(8,128)S(1)} %bitcast.306), channel_id=1, source_target_pairs={{0,4},{4,8},{8,12},{12,16},{16,20},{20,24},{24,28},{1,5},{5,9},{9,... | collective-permute-start | bytes 12296 | tf_op jit(solution)/shard_map/ppermute | solution.py:33
  42.6 5.5 %collective-permute-start.1 = (f32[8,128]{1,0:T(8,128)S(1)}, f32[8,128]{1,0:T(8,128)S(1)}, u32[]{:S(2)}, u32[]{:S(2)}) collective-permute-start(f32[8,128]{1,0:T(8,128)S(1)} %bitcast.307), channel_id=1, source_target_pairs={{4,0},{8,4},{12,8},{16,12},{20,16},{24,20},{28,24},{5,1},{9,5},{13... | collective-permute-start | bytes 12296 | tf_op jit(solution)/shard_map/ppermute | solution.py:34
  53.8 10.3 %all-to-all-start.1 = ((f32[32,1,128]{2,1,0:T(1,128)}), f32[32,1,128]{2,1,0:T(1,128)S(1)}, u32[]{:S(2)}, u32[]{:S(2)}) async-start(f32[32,1,128]{2,1,0:T(1,128)} %broadcast_in_dim.48), calls=%async_computation.1 | async-start | bytes 32768 | tf_op jit(solution)/shard_map/all_to_all | solution.py:16
  74.0 3.9 %collective-permute-start.2 = (f32[8,128]{1,0:T(8,128)S(1)}, f32[8,128]{1,0:T(8,128)S(1)}, u32[]{:S(2)}, u32[]{:S(2)}) collective-permute-start(f32[8,128]{1,0:T(8,128)S(1)} %bitcast.309), channel_id=1, source_target_pairs={{0,4},{4,8},{8,12},{12,16},{16,20},{20,24},{24,28},{1,5},{5,9},{9,... | collective-permute-start | bytes 12296 | tf_op jit(solution)/shard_map/ppermute | solution.py:33
  76.4 5.5 %collective-permute-start.3 = (f32[8,128]{1,0:T(8,128)S(1)}, f32[8,128]{1,0:T(8,128)S(1)}, u32[]{:S(2)}, u32[]{:S(2)}) collective-permute-start(f32[8,128]{1,0:T(8,128)S(1)} %bitcast.310), channel_id=1, source_target_pairs={{4,0},{8,4},{12,8},{16,12},{20,16},{24,20},{28,24},{5,1},{9,5},{13... | collective-permute-start | bytes 12296 | tf_op jit(solution)/shard_map/ppermute | solution.py:34
  86.6 10.0 %all-to-all-start.2 = ((f32[32,1,128]{2,1,0:T(1,128)}), f32[32,1,128]{2,1,0:T(1,128)S(1)}, u32[]{:S(2)}, u32[]{:S(2)}) async-start(f32[32,1,128]{2,1,0:T(1,128)} %broadcast_in_dim.49), calls=%async_computation.2 | async-start | bytes 32768 | tf_op jit(solution)/shard_map/all_to_all | solution.py:16
  106.0 6.0 %collective-permute-start.4 = (f32[8,128]{1,0:T(8,128)S(1)}, f32[8,128]{1,0:T(8,128)S(1)}, u32[]{:S(2)}, u32[]{:S(2)}) collective-permute-start(f32[8,128]{1,0:T(8,128)S(1)} %bitcast.303), channel_id=1, source_target_pairs={{0,4},{4,8},{8,12},{12,16},{16,20},{20,24},{24,28},{1,5},{5,9},{9,... | collective-permute-start | bytes 12296 | tf_op jit(solution)/shard_map/ppermute | solution.py:33
  108.4 5.5 %collective-permute-start.5 = (f32[8,128]{1,0:T(8,128)S(1)}, f32[8,128]{1,0:T(8,128)S(1)}, u32[]{:S(2)}, u32[]{:S(2)}) collective-permute-start(f32[8,128]{1,0:T(8,128)S(1)} %bitcast.304), channel_id=1, source_target_pairs={{4,0},{8,4},{12,8},{16,12},{20,16},{24,20},{28,24},{5,1},{9,5},{13... | collective-permute-start | bytes 12296 | tf_op jit(solution)/shard_map/ppermute | solution.py:34
  118.5 10.0 %all-to-all-start.3 = ((f32[32,1,128]{2,1,0:T(1,128)}), f32[32,1,128]{2,1,0:T(1,128)S(1)}, u32[]{:S(2)}, u32[]{:S(2)}) async-start(f32[32,1,128]{2,1,0:T(1,128)} %broadcast_in_dim.50), calls=%async_computation.3 | async-start | bytes 32768 | tf_op jit(solution)/shard_map/all_to_all | solution.py:16

commit v2 on v0

v2 whole, which is shorter than its diff:
```python
import functools

import jax
import jax.numpy as jnp
from jax import lax
from jax.experimental import pallas as pl
from jax.experimental.pallas import tpu as pltpu
from jax.sharding import PartitionSpec as P

STEPS = 3
TAIL = 8
ROW_ALIGN = 8
AXES = ("dom", "sub")
VMEM = pl.BlockSpec(memory_space=pltpu.VMEM)
SMEM = pl.BlockSpec(memory_space=pltpu.SMEM)
F32 = jnp.float32


def call(body, name, outs, specs, scratch=()):
    return pl.pallas_call(
        body,
        name=name,
        out_shape=[jax.ShapeDtypeStruct(shape, F32) for shape in outs],
        in_specs=specs,
        out_specs=[VMEM] * len(outs),
        scratch_shapes=list(scratch),
        compiler_params=pltpu.CompilerParams(vmem_limit_bytes=16 * 1024 * 1024),
    )


def round_up(value, step):
    return -(-value // step) * step


def eye(rows, lanes):
    down = lax.broadcasted_iota(jnp.int32, (rows, lanes), 0)
    across = lax.broadcasted_iota(jnp.int32, (rows, lanes), 1)
    return down == across


def to_row(column, mask):
    return jnp.sum(jnp.where(mask, column, 0.0), axis=0, keepdims=True)


def live(live_ref, slot):
    return jnp.where(slot < live_ref[0], 1.0, 0.0).astype(F32)


def tree_sum(parts):
    while len(parts) > 1:
        pairs = [parts[i] + parts[i + 1] for i in range(0, len(parts) - 1, 2)]
        parts = pairs + parts[len(parts) - len(parts) % 2 :]
    return parts[0]


def pack_body(live_ref, load_ref, images_ref, own_ref):
    count, slots, width = images_ref.shape
    rows = own_ref.shape[1]
    for slot in range(slots):
        mask = live(live_ref, slot)
        own_ref[slot, 0:count, :] = images_ref[:, slot, :] * mask
        own_ref[slot, count : count + 1, :] = load_ref[slot : slot + 1, :] * mask
        own_ref[slot, count + 1 : rows, :] = jnp.zeros((rows - count - 1, width), F32)


def lane_groups(count, rows, width):
    groups = width // (count + 1)
    if rows % groups == 0 and (rows // groups) % ROW_ALIGN == 0:
        return groups
    return 1


def gram_body(count, group_ref, out_ref):
    blocks, rows, width = group_ref.shape
    products = []
    for block in range(blocks):
        part = group_ref[block]
        products.append(
            lax.dot_general(
                part, part, (((1,), (1,)), ((), ())),
                precision=lax.Precision.HIGHEST, preferred_element_type=F32,
            )
        )
    gram = jnp.concatenate([tree_sum(products), jnp.zeros((rows, width - rows), F32)], axis=1)
    groups = lane_groups(count, rows, width)
    each, lanes = rows // groups, width // groups
    packed = gram[0:each]
    for group in range(1, groups):
        packed = packed + pltpu.roll(gram[group * each : (group + 1) * each], group * lanes, 1)
    for copy in range(out_ref.shape[0]):
        out_ref[copy] = packed


def sweep(matrix, count):
    rows, width = matrix.shape
    down = lax.broadcasted_iota(jnp.int32, (rows, width), 0)
    across = lax.broadcasted_iota(jnp.int32, (rows, width), 1)
    for k in range(count):
        pivot_row = matrix[k : k + 1, :]
        column = matrix[:, k : k + 1]
        inverse = 1.0 / pivot_row[:, k : k + 1]
        lane_k = across == k
        scaled = jnp.where(lane_k[0:1], inverse, pivot_row * inverse)
        kept = jnp.where(lane_k, 0.0, matrix)
        matrix = jnp.where(down == k, scaled, kept - column * scaled)
    return matrix


def apply_tiles(tiles_ref, columns_ref, vector_ref, live_ref):
    slots, per_row, size, _ = tiles_ref.shape
    mask = eye(size, size)
    images = []
    for slot in range(slots):
        parts = []
        for t in range(per_row):
            picked = vector_ref[pl.ds(columns_ref[slot, t], 1), :]
            parts.append(tiles_ref[slot, t] * picked)
        column = jnp.sum(tree_sum(parts), axis=1, keepdims=True)
        images.append(to_row(column, mask) * live(live_ref, slot))
    return images


def tail_with(old, entries):
    down = lax.broadcasted_iota(jnp.int32, (TAIL, old.shape[1]), 0)
    for row, value in entries:
        old = jnp.where(down == row, value, old)
    return old


def finish_step(step, tails, own_ref, images, tail_ref, out_ref):
    slots, rows, width = own_ref.shape
    last = STEPS
    total = jnp.zeros((rows + TAIL, width), F32)
    for slot in range(slots):
        tails[slot] = tail_with(tails[slot], [(last, images[slot])])
        total = total + jnp.concatenate([own_ref[slot], tails[slot]], axis=0) * images[slot]
    for block, tail in enumerate(tails):
        tail_ref[block] = tail
    partial = to_row(jnp.sum(total, axis=1, keepdims=True), eye(rows + TAIL, width))
    copies, lines, _ = out_ref.shape
    if lines == 1:
        message = partial
    else:
        pad = [jnp.zeros((lines - slots - 1, width), F32)] if lines > slots + 1 else []
        message = jnp.concatenate([*images, partial, *pad], axis=0)
    out_ref[...] = jnp.broadcast_to(message[None], (copies, lines, width))


def start_body(
    count, live_ref, columns_ref, ghosts_ref, parts_ref, own_ref, before_ref, group_ref, after_ref, tiles_ref,
    out_ref, ghost_ref, tail_ref, inverse_ref, start_ref, vector_ref,
):
    slots, rows, width = own_ref.shape
    blocks = group_ref.shape[0]
    ghosts = ghosts_ref.shape[1]
    groups = lane_groups(count, rows, width)
    lanes = width // groups
    packed = tree_sum([parts_ref[i] for i in range(parts_ref.shape[0])])
    across = lax.broadcasted_iota(jnp.int32, (rows, width), 1)
    down = lax.broadcasted_iota(jnp.int32, (rows, width), 0)
    pieces = [packed]
    for group in range(1, groups):
        pieces.append(pltpu.roll(packed, width - group * lanes, 1))
    gram = jnp.where(across <= count, jnp.concatenate(pieces, axis=0), 0.0)
    swept = sweep(gram, count)
    keep = (down < count) & (across < count)
    inverse_ref[0:rows, :] = jnp.where(keep, swept, 0.0)
    tail_down = lax.broadcasted_iota(jnp.int32, (TAIL, width), 0)
    tail_across = lax.broadcasted_iota(jnp.int32, (TAIL, width), 1)
    inverse_ref[rows : rows + TAIL, :] = jnp.where(
        (tail_down < STEPS) & (tail_across == tail_down + rows), 1.0, 0.0
    )
    squared = swept[count : count + 1, count : count + 1]
    scale = 1.0 / jnp.sqrt(squared)
    start = jnp.where(down < count, -swept[:, count : count + 1], jnp.where(down == count, 1.0, 0.0))
    start_ref[0:rows, :] = start
    start_ref[rows : rows + TAIL, :] = jnp.broadcast_to(jnp.sqrt(squared), (TAIL, width))
    coefficients = start * scale
    tails = []
    for block in range(slots + ghosts):
        if block < slots:
            held = own_ref[block]
        else:
            code = ghosts_ref[0, block - slots]
            offset = code // blocks
            place = code - offset * blocks
            held = jnp.where(
                offset == 0, before_ref[place], jnp.where(offset == 1, group_ref[place], after_ref[place])
            )
            ghost_ref[block - slots] = held
        vector = jnp.sum(held * coefficients, axis=0, keepdims=True)
        vector_ref[block : block + 1, :] = vector
        tails.append(tail_with(jnp.zeros((TAIL, width), F32), [(0, vector)]))
    images = apply_tiles(tiles_ref, columns_ref, vector_ref, live_ref)
    finish_step(0, tails, own_ref, images, tail_ref, out_ref)


def project(total_row, inverse, rows, width):
    full = rows + TAIL
    down = lax.broadcasted_iota(jnp.int32, (full, width), 0)
    projected = jnp.sum(inverse * total_row, axis=1, keepdims=True)
    column = jnp.sum(jnp.where(eye(full, width), total_row, 0.0), axis=1, keepdims=True)
    projected = jnp.broadcast_to(projected, (full, width))
    squared = jnp.sum(
        jnp.where(down == rows + STEPS, column, -(column * projected)), axis=0, keepdims=True
    )
    return projected, jnp.sqrt(squared), down


def step_body(
    step, count, live_ref, columns_ref, ghosts_ref, every_ref, own_ref, ghost_ref, old_ref, inverse_ref, tiles_ref,
    out_ref, tail_ref, history_ref, vector_ref,
):
    slots, rows, width = own_ref.shape
    ghosts = ghosts_ref.shape[1]
    subs = lax.axis_size("sub")
    span = subs * slots
    dom = lax.axis_index("dom")
    total_row = tree_sum([every_ref[i, slots : slots + 1, :] for i in range(every_ref.shape[0])])
    projected, norm, down = project(total_row, inverse_ref[...], rows, width)
    history_ref[...] = jnp.where(down == count, norm, projected)
    inverse_norm = 1.0 / norm
    coefficients = jnp.where(down == rows + STEPS, inverse_norm, -(projected * inverse_norm))
    tails = []
    for block in range(slots + ghosts):
        old = old_ref[block]
        if block < slots:
            held = own_ref[block]
        else:
            held = ghost_ref[block - slots]
            code = ghosts_ref[0, block - slots]
            offset = code // span
            place = code - offset * span
            peer = place // slots
            device = (dom + offset - 1) * subs + peer
            image = every_ref[device, pl.ds(place - peer * slots, 1), :]
            old = tail_with(old, [(STEPS, image)])
        vector = jnp.sum(held * coefficients[0:rows], axis=0, keepdims=True)
        vector = vector + jnp.sum(old * coefficients[rows : rows + TAIL], axis=0, keepdims=True)
        vector_ref[block : block + 1, :] = vector
        tails.append(tail_with(old, [(step, vector), (STEPS, 0.0)]))
    images = apply_tiles(tiles_ref, columns_ref, vector_ref, live_ref)
    finish_step(step, tails, own_ref, images, tail_ref, out_ref)


def small_solve(matrix, target):
    size = len(target)
    low = [[None] * size for _ in range(size)]
    inverses = []
    for j in range(size):
        value = matrix[j][j]
        for k in range(j):
            value = value - low[j][k] * low[j][k]
        inverses.append(1.0 / jnp.sqrt(value))
        for i in range(j + 1, size):
            value = matrix[i][j]
            for k in range(j):
                value = value - low[i][k] * low[j][k]
            low[i][j] = value * inverses[j]
    forward = []
    for i in range(size):
        value = target[i]
        for k in range(i):
            value = value - low[i][k] * forward[k]
        forward.append(value * inverses[i])
    back = [None] * size
    for i in reversed(range(size)):
        value = forward[i]
        for k in range(i + 1, size):
            value = value - low[k][i] * back[k]
        back[i] = value * inverses[i]
    return back


def end_body(count, live_ref, every_ref, own_ref, tail_ref, inverse_ref, start_ref, recycled_ref, *rest):
    histories, (solution_ref, residual_ref) = rest[:-2], rest[-2:]
    slots, rows, width = own_ref.shape
    full = rows + TAIL
    total_row = tree_sum([every_ref[i] for i in range(every_ref.shape[0])])
    projected, norm, down = project(total_row, inverse_ref[...], rows, width)
    columns = [history[...] for history in histories]
    columns.append(jnp.where(down == count, norm, projected))
    entries = []
    for j in range(STEPS):
        column = [columns[j][rows + i : rows + i + 1, :] for i in range(j + 1)]
        column.append(columns[j][count : count + 1, :])
        entries.append(column)
    normal = [[None] * STEPS for _ in range(STEPS)]
    for a in range(STEPS):
        for b in range(a + 1):
            shared = range(min(len(entries[a]), len(entries[b])))
            normal[a][b] = tree_sum([entries[a][r] * entries[b][r] for r in shared])
    initial = start_ref[rows : rows + 1, :]
    least = small_solve(normal, [initial * entries[j][0] for j in range(STEPS)])
    image = []
    for r in range(STEPS + 1):
        image.append(tree_sum([entries[j][r] * least[j] for j in range(STEPS) if r < len(entries[j])]))
    start = start_ref[0:rows, :]
    recycled_coefficients = start[0:count] * -1.0
    for j in range(STEPS):
        recycled_coefficients = recycled_coefficients - columns[j][0:count] * least[j]
    ratio = image[STEPS] / norm
    head = jnp.where(down[0:rows] < count, start + columns[-1][0:rows] * ratio, start)
    tail_down = down[0:TAIL]
    solution_tail = jnp.zeros((TAIL, width), F32)
    residual_tail = jnp.zeros((TAIL, width), F32)
    for j in range(STEPS):
        solution_tail = jnp.where(tail_down == j, least[j], solution_tail)
        residual_tail = jnp.where(tail_down == j, entries[-1][j] * ratio - image[j], residual_tail)
    residual_tail = jnp.where(tail_down == STEPS, -ratio, residual_tail)
    for slot in range(slots):
        tail = tail_ref[slot]
        mask = live(live_ref, slot)
        point = jnp.sum(recycled_ref[:, slot, :] * mask * recycled_coefficients, axis=0, keepdims=True)
        point = point + jnp.sum(tail * solution_tail, axis=0, keepdims=True)
        solution_ref[slot : slot + 1, :] = point
        left = jnp.sum(own_ref[slot] * head, axis=0, keepdims=True)
        left = left + jnp.sum(tail * residual_tail, axis=0, keepdims=True)
        residual_ref[slot : slot + 1, :] = left


def local(load_vector, recycled, images, matrix_tiles, tile_columns, ghost_list, live_counts):
    slots, width = load_vector.shape
    count = recycled.shape[0]
    ghosts = ghost_list.shape[1]
    doms, subs = lax.axis_size("dom"), lax.axis_size("sub")
    devices = doms * subs
    rows = round_up(count + 1, ROW_ALIGN)
    full = rows + TAIL
    blocks = slots + ghosts
    (own,) = call(pack_body, "pack", [(slots, rows, width)], [SMEM, VMEM, VMEM])(live_counts, load_vector, images)
    group = lax.all_gather(own, "sub", axis=0, tiled=True)
    up = [(i, i + 1) for i in range(doms - 1)]
    down = [(j, i) for i, j in up]
    before = lax.ppermute(group, "dom", up)
    after = lax.ppermute(group, "dom", down)
    each = rows // lane_groups(count, rows, width)
    (grams,) = call(functools.partial(gram_body, count), "gram", [(doms, each, width)], [VMEM])(group)
    parts = lax.all_to_all(grams, "dom", 0, 0)
    lines = round_up(slots + 1, 4)
    scratch = [pltpu.VMEM((round_up(blocks, 8), width), F32)]
    message, ghost_images, tails, inverse, start = call(
        functools.partial(start_body, count),
        "start",
        [(devices, lines, width), (ghosts, rows, width), (blocks, TAIL, width), (full, width), (full, width)],
        [SMEM] * 3 + [VMEM] * 6,
        scratch,
    )(live_counts, tile_columns, ghost_list, parts, own, before, group, after, matrix_tiles)
    histories = []
    for step in range(1, STEPS):
        every = lax.all_to_all(message, AXES, 0, 0)
        sent = lines if step < STEPS - 1 else 1
        message, tails, history = call(
            functools.partial(step_body, step, count),
            f"step{step}",
            [(devices, sent, width), (blocks, TAIL, width), (full, width)],
            [SMEM] * 3 + [VMEM] * 6,
            scratch,
        )(live_counts, tile_columns, ghost_list, every, own, ghost_images, tails, inverse, matrix_tiles)
        histories.append(history)
    every = lax.all_to_all(message, AXES, 0, 0)
    return tuple(
        call(
            functools.partial(end_body, count),
            "end",
            [(slots, width), (slots, width)],
            [SMEM] + [VMEM] * (6 + len(histories)),
        )(live_counts, every, own, tails, inverse, start, recycled, *histories)
    )


def solution(mesh):
    return jax.shard_map(
        local,
        mesh=mesh,
        in_specs=(
            P(("dom", "sub"), None),
            P(None, ("dom", "sub"), None),
            P(None, ("dom", "sub"), None),
            P(("dom", "sub"), None, None, None),
            P(("dom", "sub"), None),
            P(("dom", "sub"), None),
            P(("dom", "sub")),
        ),
        out_specs=(P(("dom", "sub"), None), P(("dom", "sub"), None)),
        check_vma=False,
    )
```

time: 254 us -> 64.2 us (0.25)
  blocking collectives: 181 us -> 46.9 us
  other arithmetic: 26.9 us -> 0 us
  starting transfers between devices: 17.8 us -> 5.84 us
  between operations: 9.6 us -> 1.39 us
  local copies, waits for them, and re-layouts: 9.88 us -> 2.03 us
  Pallas kernels: 0 us -> 7.57 us
  matrix products: 7.11 us -> 0 us
    psum x4 -> x0, blocking collectives: 165 us -> none  [the longest x3 122 us: local(): lax.psum((local_images, jnp.dot(stacked, image_now, precision=highest), j...]
    all_to_all x0 -> x4, blocking collectives: none -> 40 us  [the longest x3 27.3 us: local(): every = lax.all_to_all(message, AXES, 0, 0)]
    another operation x17 -> x0, other arithmetic: 16.5 us -> none
    ppermute x6 -> x2, starting transfers between devices: 17.8 us -> 5.84 us  [the longest x1 4.56 us: local(): before = lax.ppermute(group, 'dom', up)]
    all_gather x3 -> x1, blocking collectives: 16.2 us -> 6.89 us  [local(): group = lax.all_gather(own, 'sub', axis=0, tiled=True)]
    pallas_call x0 -> x6, Pallas kernels: none -> 7.57 us  [the longest x1 4.38 us: local(): call(functools.partial(start_body, count), 'start', [(devices, lines, wid...]
    reduce_sum x9 -> x0, other arithmetic: 6.95 us -> none  [the longest x3 3.04 us: local(): jnp.sum(summed_images * summed_images)]
    dot_general x23 -> x0, matrix products: 5.63 us -> none  [the longest x3 2.87 us: multiply(): jnp.einsum('stij,stj->si', matrix_tiles, picked, precision=lax.Precision....]
  transfers between devices with their start and end apart: 6 -> 2, of which waited for: 0 -> 0; matrix products, arithmetic and copies ran while one was open for 3% -> 0% of each run, Pallas kernels for 0% -> 1%
where the time goes in v2:
time: 64.2 us; the launch traced here: 63.8 us
  blocking collectives  46.9 us (73%)
  Pallas kernels  7.57 us (12%)
  starting transfers between devices  5.84 us (9%)
  local copies, waits for them, and re-layouts  2.03 us (3%)
  between operations  1.39 us (2%)
    all_to_all x3, blocking collectives, local(): every = lax.all_to_all(message, AXES, 0, 0)  27.3 us
    all_to_all x1, blocking collectives, local(): parts = lax.all_to_all(grams, 'dom', 0, 0)  12.7 us
    all_gather x1, blocking collectives, local(): group = lax.all_gather(own, 'sub', axis=0, tiled=True)  6.89 us
    ppermute x1, starting transfers between devices, local(): before = lax.ppermute(group, 'dom', up)  4.56 us
    pallas_call x1, Pallas kernels, local(): call(functools.partial(start_body, count), 'start', [(devices, lines, wid...  4.38 us
    unnamed x14, local copies, waits for them, and re-layouts  2.03 us
    pallas_call x2, Pallas kernels, local(): call(functools.partial(step_body, step, count), f'step{step}', [(devices,...  1.93 us
  transfers between devices with their start and end apart: 2, of which 0 were waited for; matrix products, arithmetic and copies ran while one was open for 0% of the time, Pallas kernels for 1%

profile of v2, /device:TPU:0, one launch (start us, length us, event | category | flops | bytes accessed | tf_op | source)
XLA Modules:
  0.0 63.8 jit_solution(11747106340959822098)
XLA Ops:
  0.6 0.0 copy-start.6
  1.3 0.0 copy-done.6
  1.3 0.0 copy-start.2
  1.3 0.8 %copy-done.2 = f32[40,2,128]{2,1,0:T(2,128)S(1)} copy-done((f32[40,2,128]{2,1,0:T(2,128)S(1)}, f32[40,2,128]{2,1,0:T(2,128)}, u32[]{:S(2)}) %copy-start.2) | copy-done | bytes 40984
  2.1 6.9 %all_gather.3.group_ref = f32[8,48,128]{2,1,0:T(8,128)S(1)} all-gather(f32[2,48,128]{2,1,0:T(8,128)S(1)} %pack.1.own_ref), channel_id=1, replica_groups=mesh['dom'=8,'sub'=4] {'sub'}, dimensions={0}, use_global_device_ids=true | all-gather | bytes 245760 | tf_op jit(solution)/shard_map/all_gather | solution.py:332
  9.0 1.3 %collective-permute-start.1 = (f32[8,48,128]{2,1,0:T(8,128)S(1)}, f32[8,48,128]{2,1,0:T(8,128)S(1)}, u32[]{:S(2)}, u32[]{:S(2)}) collective-permute-start(f32[8,48,128]{2,1,0:T(8,128)S(1)} %all_gather.3.group_ref), channel_id=1, source_target_pairs={{4,0},{8,4},{12,8},{16,12},{20,16},{24,20},{28,24},{5,1},{9,5},{13... | collective-permute-start | bytes 589832 | tf_op jit(solution)/shard_map/ppermute | solution.py:336
  10.3 4.6 %collective-permute-start = (f32[8,48,128]{2,1,0:T(8,128)S(1)}, f32[8,48,128]{2,1,0:T(8,128)S(1)}, u32[]{:S(2)}, u32[]{:S(2)}) collective-permute-start(f32[8,48,128]{2,1,0:T(8,128)S(1)} %all_gather.3.group_ref), channel_id=1, source_target_pairs={{0,4},{4,8},{8,12},{12,16},{16,20},{20,24},{24,28},{1,5},{5,9},{9,... | collective-permute-start | bytes 589832 | tf_op jit(solution)/shard_map/ppermute | solution.py:335
  14.9 0.5 gram.1
  15.4 0.0 copy-start.4
  15.4 0.0 copy-start.5
  15.4 12.7 %all_to_all.20.parts_ref = f32[8,16,128]{2,1,0:T(8,128)S(1)} all-to-all(f32[8,16,128]{2,1,0:T(8,128)S(1)} %gram.1), channel_id=1, replica_groups=mesh['dom'=8,'sub'=4] {'dom'}, dimensions={0} | all-to-all | bytes 131072 | tf_op jit(solution)/shard_map/all_to_all | solution.py:339
  28.1 0.0 collective-permute-done.1.after_ref
  28.1 0.0 collective-permute-done.before_ref
  28.1 0.0 copy-done.4
  28.1 0.0 copy-done.5
  28.1 0.0 copy-start
  28.1 1.2 %copy-done = f32[2,8,128,128]{3,2,1,0:T(8,128)S(1)} copy-done((f32[2,8,128,128]{3,2,1,0:T(8,128)S(1)}, f32[2,8,128,128]{3,2,1,0:T(8,128)}, u32[]{:S(2)}) %copy-start) | copy-done | bytes 1048600
  29.3 0.0 copy-start.1
  29.3 4.4 %start.1 = (f32[32,4,128]{2,1,0:T(4,128)S(1)}, f32[4,48,128]{2,1,0:T(8,128)S(1)}, f32[6,8,128]{2,1,0:T(8,128)S(1)}, f32[56,128]{1,0:T(8,128)S(1)}, f32[56,128]{1,0:T(8,128)S(1)}) custom-call(s32[1]{0:T(128)S(6)} %copy.9.live_ref, s32[2,8]{1,0:T(2,128)S(1)} %copy-done.4, s32[1,4]{1,0:T(1,128)S(1)} %copy-done.5, f32[8,16,128]{2,1,0:T(8,128)S(1)} %all_to_all.20.parts_ref, ...), custom_call_target="tpu_custom_call" | custom-call | tf_op jit(solution)/shard_map/start/pallas_call | solution.py:342
  33.7 9.4 %all_to_all.21.every_ref = f32[32,4,128]{2,1,0:T(4,128)S(1)} all-to-all(f32[32,4,128]{2,1,0:T(4,128)S(1)} %get-tuple-element.13), channel_id=1, replica_groups=mesh['dom'=8,'sub'=4] {'dom','sub'}, dimensions={0} | all-to-all | bytes 131072 | tf_op jit(solution)/shard_map/all_to_all | solution.py:351
  43.1 0.0 copy-done.1
  43.1 1.0 %step1.1 = (f32[32,4,128]{2,1,0:T(4,128)S(1)}, f32[6,8,128]{2,1,0:T(8,128)S(1)}, f32[56,128]{1,0:T(8,128)S(1)}) custom-call(s32[1]{0:T(128)S(6)} %copy.9.live_ref, s32[2,8]{1,0:T(2,128)S(1)} %copy-done.4, s32[1,4]{1,0:T(1,128)S(1)} %copy-done.5, f32[32,4,128]{2,1,0:T(4,128)S(1)} %all_to_all.21.every_ref, f32[2,48,128]{2,1,0:T(8,128)S(1)} %pack.1.own_ref, ...), custom_call_target="tpu_custom_call" | custom-call | tf_op jit(solution)/shard_map/step1/pallas_call | solution.py:353
  44.1 9.1 %all_to_all.22.every_ref = f32[32,4,128]{2,1,0:T(4,128)S(1)} all-to-all(f32[32,4,128]{2,1,0:T(4,128)S(1)} %get-tuple-element.17), channel_id=1, replica_groups=mesh['dom'=8,'sub'=4] {'dom','sub'}, dimensions={0} | all-to-all | bytes 131072 | tf_op jit(solution)/shard_map/all_to_all | solution.py:351
  53.2 1.0 %step2.1 = (f32[32,1,128]{2,1,0:T(1,128)S(1)}, f32[6,8,128]{2,1,0:T(8,128)S(1)}, f32[56,128]{1,0:T(8,128)S(1)}) custom-call(s32[1]{0:T(128)S(6)} %copy.9.live_ref, s32[2,8]{1,0:T(2,128)S(1)} %copy-done.4, s32[1,4]{1,0:T(1,128)S(1)} %copy-done.5, f32[32,4,128]{2,1,0:T(4,128)S(1)} %all_to_all.22.every_ref, f32[2,48,128]{2,1,0:T(8,128)S(1)} %pack.1.own_ref, ...), custom_call_target="tpu_custom_call" | custom-call | tf_op jit(solution)/shard_map/step2/pallas_call | solution.py:353
  54.1 0.0 copy-start.3
  54.2 8.9 %all_to_all.23.every_ref = f32[32,1,128]{2,1,0:T(1,128)S(1)} all-to-all(f32[32,1,128]{2,1,0:T(1,128)S(1)} %get-tuple-element.19), channel_id=1, replica_groups=mesh['dom'=8,'sub'=4] {'dom','sub'}, dimensions={0} | all-to-all | bytes 32768 | tf_op jit(solution)/shard_map/all_to_all | solution.py:361
  63.0 0.0 copy-done.3
  63.0 0.7 %end.1 = (f32[2,128]{1,0:T(2,128)}, f32[2,128]{1,0:T(2,128)}) custom-call(s32[1]{0:T(128)S(6)} %copy.9.live_ref, f32[32,1,128]{2,1,0:T(1,128)S(1)} %all_to_all.23.every_ref, f32[2,48,128]{2,1,0:T(8,128)S(1)} %pack.1.own_ref, f32[6,8,128]{2,1,0:T(8,128)S(1)} %get-tuple-element.20.tail_ref, f32[56,128]{1,0:T(8,128)S(1)} %get-tuple-element.16.inverse_ref, ...), custom_call_target="tpu_custom_call" | custom-call | tf_op jit(solution)/shard_map/end/pallas_call | solution.py:363
  (1 shorter events, 0.0 us)
Async XLA Ops:
  0.6 0.7 %copy-start.6 = (f32[2,128]{1,0:T(2,128)S(1)}, f32[2,128]{1,0:T(2,128)}, u32[]{:S(2)}) copy-start(f32[2,128]{1,0:T(2,128)} %load_ref.1) | copy-start | bytes 3076
  1.3 0.8 %copy-start.2 = (f32[40,2,128]{2,1,0:T(2,128)S(1)}, f32[40,2,128]{2,1,0:T(2,128)}, u32[]{:S(2)}) copy-start(f32[40,2,128]{2,1,0:T(2,128)} %images_ref.1) | copy-start | bytes 122884
  9.0 19.1 %collective-permute-start.1 = (f32[8,48,128]{2,1,0:T(8,128)S(1)}, f32[8,48,128]{2,1,0:T(8,128)S(1)}, u32[]{:S(2)}, u32[]{:S(2)}) collective-permute-start(f32[8,48,128]{2,1,0:T(8,128)S(1)} %all_gather.3.group_ref), channel_id=1, source_target_pairs={{4,0},{8,4},{12,8},{16,12},{20,16},{24,20},{28,24},{5,1},{9,5},{13... | collective-permute-start | bytes 589832 | tf_op jit(solution)/shard_map/ppermute | solution.py:336
  10.3 17.8 %collective-permute-start = (f32[8,48,128]{2,1,0:T(8,128)S(1)}, f32[8,48,128]{2,1,0:T(8,128)S(1)}, u32[]{:S(2)}, u32[]{:S(2)}) collective-permute-start(f32[8,48,128]{2,1,0:T(8,128)S(1)} %all_gather.3.group_ref), channel_id=1, source_target_pairs={{0,4},{4,8},{8,12},{12,16},{16,20},{20,24},{24,28},{1,5},{5,9},{9,... | collective-permute-start | bytes 589832 | tf_op jit(solution)/shard_map/ppermute | solution.py:335
  15.4 12.7 %copy-start.4 = (s32[2,8]{1,0:T(2,128)S(1)}, s32[2,8]{1,0:T(2,128)}, u32[]{:S(2)}) copy-start(s32[2,8]{1,0:T(2,128)} %columns_ref.5) | copy-start | bytes 196
  15.4 12.7 %copy-start.5 = (s32[1,4]{1,0:T(1,128)S(1)}, s32[1,4]{1,0:T(1,128)}, u32[]{:S(2)}) copy-start(s32[1,4]{1,0:T(1,128)} %ghosts_ref.5) | copy-start | bytes 52
  28.1 1.2 %copy-start = (f32[2,8,128,128]{3,2,1,0:T(8,128)S(1)}, f32[2,8,128,128]{3,2,1,0:T(8,128)}, u32[]{:S(2)}) copy-start(f32[2,8,128,128]{3,2,1,0:T(8,128)} %tiles_ref.5) | copy-start | bytes 3145732
  29.3 13.8 %copy-start.1 = (f32[2,8,128,128]{3,2,1,0:T(8,128)S(1)}, f32[2,8,128,128]{3,2,1,0:T(8,128)}, u32[]{:S(2)}) copy-start(f32[2,8,128,128]{3,2,1,0:T(8,128)} %tiles_ref.5) | copy-start | bytes 3145732
  54.1 8.9 %copy-start.3 = (f32[40,2,128]{2,1,0:T(2,128)S(1)}, f32[40,2,128]{2,1,0:T(2,128)}, u32[]{:S(2)}) copy-start(f32[40,2,128]{2,1,0:T(2,128)} %recycled_ref.1) | copy-start | bytes 122884

commit v3 on v2

--- a/solution.py
+++ b/solution.py
@@ -13,10 +13,11 @@
 AXES = ("dom", "sub")
 VMEM = pl.BlockSpec(memory_space=pltpu.VMEM)
 SMEM = pl.BlockSpec(memory_space=pltpu.SMEM)
+HBM = pl.BlockSpec(memory_space=pltpu.HBM)
 F32 = jnp.float32
 
 
-def call(body, name, outs, specs, scratch=()):
+def call(body, name, outs, specs, scratch=(), work=10_000_000):
     return pl.pallas_call(
         body,
         name=name,
@@ -24,6 +25,7 @@
         in_specs=specs,
         out_specs=[VMEM] * len(outs),
         scratch_shapes=list(scratch),
+        cost_estimate=pl.CostEstimate(flops=work, bytes_accessed=1 << 20, transcendentals=0),
         compiler_params=pltpu.CompilerParams(vmem_limit_bytes=16 * 1024 * 1024),
     )
 
@@ -40,10 +42,6 @@
 
 def to_row(column, mask):
     return jnp.sum(jnp.where(mask, column, 0.0), axis=0, keepdims=True)
-
-
-def live(live_ref, slot):
-    return jnp.where(slot < live_ref[0], 1.0, 0.0).astype(F32)
 
 
 def tree_sum(parts):
@@ -53,11 +51,13 @@
     return parts[0]
 
 
-def pack_body(live_ref, load_ref, images_ref, own_ref):
+def pack_body(live_ref, load_ref, images_ref, own_ref, mask_ref):
     count, slots, width = images_ref.shape
     rows = own_ref.shape[1]
+    line = lax.broadcasted_iota(jnp.int32, mask_ref.shape, 0)
+    mask_ref[...] = jnp.where(line < live_ref[0], 1.0, 0.0).astype(F32)
     for slot in range(slots):
-        mask = live(live_ref, slot)
+        mask = jnp.where(slot < live_ref[0], 1.0, 0.0).astype(F32)
         own_ref[slot, 0:count, :] = images_ref[:, slot, :] * mask
         own_ref[slot, count : count + 1, :] = load_ref[slot : slot + 1, :] * mask
         own_ref[slot, count + 1 : rows, :] = jnp.zeros((rows - count - 1, width), F32)
@@ -91,32 +91,78 @@
         out_ref[copy] = packed
 
 
+def multiply(left, right):
+    return [[tree_sum([a * right[k][j] for k, a in enumerate(row)]) for j in range(len(right[0]))] for row in left]
+
+
+def small_inverse(matrix):
+    size = len(matrix)
+    if size == 1:
+        return [[1.0 / matrix[0][0]]]
+    half = size // 2
+    corner = [row[half:] for row in matrix[:half]]
+    rest = [row[half:] for row in matrix[half:]]
+    first = small_inverse([row[:half] for row in matrix[:half]])
+    across = multiply(first, corner)
+    taken = multiply([list(row) for row in zip(*corner)], across)
+    second = small_inverse([[rest[i][j] - taken[i][j] for j in range(half)] for i in range(half)])
+    product = multiply(across, second)
+    added = multiply(product, [list(row) for row in zip(*across)])
+    top = [[first[i][j] + added[i][j] for j in range(half)] + [-value for value in product[i]] for i in range(half)]
+    bottom = [[-product[j][i] for j in range(half)] + second[i] for i in range(half)]
+    return top + bottom
+
+
 def sweep(matrix, count):
     rows, width = matrix.shape
-    down = lax.broadcasted_iota(jnp.int32, (rows, width), 0)
-    across = lax.broadcasted_iota(jnp.int32, (rows, width), 1)
-    for k in range(count):
-        pivot_row = matrix[k : k + 1, :]
-        column = matrix[:, k : k + 1]
-        inverse = 1.0 / pivot_row[:, k : k + 1]
-        lane_k = across == k
-        scaled = jnp.where(lane_k[0:1], inverse, pivot_row * inverse)
-        kept = jnp.where(lane_k, 0.0, matrix)
-        matrix = jnp.where(down == k, scaled, kept - column * scaled)
-    return matrix
-
-
-def apply_tiles(tiles_ref, columns_ref, vector_ref, live_ref):
+    size = next(size for size in (8, 4, 2, 1) if count % size == 0)
+    tiles = [matrix[i : i + 8, :] for i in range(0, rows, 8)]
+    across = lax.broadcasted_iota(jnp.int32, (8, width), 1)
+    down = lax.broadcasted_iota(jnp.int32, (8, width), 0)
+
+    def spread(value):
+        return jnp.broadcast_to(value, (8, width))
+
+    for k in range(0, count, size):
+        at, inner = divmod(k, 8)
+        columns = [[tile[:, k + i : k + i + 1] for tile in tiles] for i in range(size)]
+        lines = [spread(tiles[at][inner + i : inner + i + 1, :]) for i in range(size)]
+        full = [spread(columns[i][at]) for i in range(size)]
+        pivots = [
+            [spread(full[max(i, j)][inner + min(i, j) : inner + min(i, j) + 1, :]) for j in range(size)]
+            for i in range(size)
+        ]
+        inverse = small_inverse(pivots)
+        scaled = []
+        for i in range(size):
+            line = tree_sum([lines[j] * inverse[i][j] for j in range(size)])
+            for j in range(size):
+                line = jnp.where(across == k + j, inverse[i][j], line)
+            scaled.append(line)
+        inside = (across >= k) & (across < k + size)
+        updated = []
+        for n, tile in enumerate(tiles):
+            value = jnp.where(inside, 0.0, tile)
+            value = value - tree_sum([columns[i][n] * scaled[i] for i in range(size)])
+            if n == at:
+                for i in range(size):
+                    value = jnp.where(down == inner + i, scaled[i], value)
+            updated.append(value)
+        tiles = updated
+    return jnp.concatenate(tiles, axis=0)
+
+
+def apply_tiles(tiles_ref, pick_ref, vectors, mask_ref):
     slots, per_row, size, _ = tiles_ref.shape
     mask = eye(size, size)
     images = []
     for slot in range(slots):
-        parts = []
-        for t in range(per_row):
-            picked = vector_ref[pl.ds(columns_ref[slot, t], 1), :]
-            parts.append(tiles_ref[slot, t] * picked)
+        picked = tree_sum(
+            [pick_ref[e, slot * per_row : (slot + 1) * per_row, :] * vector for e, vector in enumerate(vectors)]
+        )
+        parts = [tiles_ref[slot, t] * picked[t : t + 1, :] for t in range(per_row)]
         column = jnp.sum(tree_sum(parts), axis=1, keepdims=True)
-        images.append(to_row(column, mask) * live(live_ref, slot))
+        images.append(to_row(column, mask) * mask_ref[slot : slot + 1, :])
     return images
 
 
@@ -127,7 +173,7 @@
     return old
 
 
-def finish_step(step, tails, own_ref, images, tail_ref, out_ref):
+def finish_step(tails, own_ref, images, tail_ref, out_ref):
     slots, rows, width = own_ref.shape
     last = STEPS
     total = jnp.zeros((rows + TAIL, width), F32)
@@ -146,13 +192,19 @@
     out_ref[...] = jnp.broadcast_to(message[None], (copies, lines, width))
 
 
-def start_body(
-    count, live_ref, columns_ref, ghosts_ref, parts_ref, own_ref, before_ref, group_ref, after_ref, tiles_ref,
-    out_ref, ghost_ref, tail_ref, inverse_ref, start_ref, vector_ref,
+def factor_body(
+    count, rows, columns_ref, tiles_ref, parts_ref, inverse_ref, start_ref, pick_ref, here_ref, sem,
 ):
-    slots, rows, width = own_ref.shape
-    blocks = group_ref.shape[0]
-    ghosts = ghosts_ref.shape[1]
+    move = pltpu.make_async_copy(tiles_ref, here_ref, sem)
+    move.start()
+    width = parts_ref.shape[2]
+    slots, per_row = columns_ref.shape
+    for slot in range(slots):
+        names = columns_ref[slot : slot + 1, :].astype(F32)
+        column = jnp.sum(jnp.where(eye(per_row, per_row), names, 0.0), axis=1, keepdims=True)
+        column = jnp.broadcast_to(column, (per_row, width))
+        for block in range(pick_ref.shape[0]):
+            pick_ref[block, slot * per_row : (slot + 1) * per_row, :] = jnp.where(column == float(block), 1.0, 0.0)
     groups = lane_groups(count, rows, width)
     lanes = width // groups
     packed = tree_sum([parts_ref[i] for i in range(parts_ref.shape[0])])
@@ -170,12 +222,23 @@
     inverse_ref[rows : rows + TAIL, :] = jnp.where(
         (tail_down < STEPS) & (tail_across == tail_down + rows), 1.0, 0.0
     )
-    squared = swept[count : count + 1, count : count + 1]
-    scale = 1.0 / jnp.sqrt(squared)
+    norm = jnp.sqrt(swept[count : count + 1, count : count + 1])
     start = jnp.where(down < count, -swept[:, count : count + 1], jnp.where(down == count, 1.0, 0.0))
     start_ref[0:rows, :] = start
-    start_ref[rows : rows + TAIL, :] = jnp.broadcast_to(jnp.sqrt(squared), (TAIL, width))
-    coefficients = start * scale
+    start_ref[rows : rows + TAIL, :] = jnp.broadcast_to(norm, (TAIL, width))
+    move.wait()
+
+
+def start_body(
+    paired, ghosts_ref, start_ref, own_ref, one_ref, group_ref, two_ref, tiles_ref, pick_ref, mask_ref,
+    out_ref, ghost_ref, tail_ref,
+):
+    slots, rows, width = own_ref.shape
+    blocks = group_ref.shape[0]
+    ghosts = ghosts_ref.shape[1]
+    after = lax.axis_index("sub") % 2 * 2 if paired else 2
+    coefficients = start_ref[0:rows, :] * (1.0 / start_ref[rows : rows + 1, :])
+    vectors = []
     tails = []
     for block in range(slots + ghosts):
         if block < slots:
@@ -185,14 +248,14 @@
             offset = code // blocks
             place = code - offset * blocks
             held = jnp.where(
-                offset == 0, before_ref[place], jnp.where(offset == 1, group_ref[place], after_ref[place])
+                offset == 1, group_ref[place], jnp.where(offset == after, two_ref[place], one_ref[place])
             )
             ghost_ref[block - slots] = held
         vector = jnp.sum(held * coefficients, axis=0, keepdims=True)
-        vector_ref[block : block + 1, :] = vector
+        vectors.append(vector)
         tails.append(tail_with(jnp.zeros((TAIL, width), F32), [(0, vector)]))
-    images = apply_tiles(tiles_ref, columns_ref, vector_ref, live_ref)
-    finish_step(0, tails, own_ref, images, tail_ref, out_ref)
+    images = apply_tiles(tiles_ref, pick_ref, vectors, mask_ref)
+    finish_step(tails, own_ref, images, tail_ref, out_ref)
 
 
 def project(total_row, inverse, rows, width):
@@ -208,8 +271,8 @@
 
 
 def step_body(
-    step, count, live_ref, columns_ref, ghosts_ref, every_ref, own_ref, ghost_ref, old_ref, inverse_ref, tiles_ref,
-    out_ref, tail_ref, history_ref, vector_ref,
+    step, count, ghosts_ref, every_ref, own_ref, ghost_ref, old_ref, inverse_ref, tiles_ref, pick_ref, mask_ref,
+    out_ref, tail_ref, history_ref,
 ):
     slots, rows, width = own_ref.shape
     ghosts = ghosts_ref.shape[1]
@@ -221,6 +284,7 @@
     history_ref[...] = jnp.where(down == count, norm, projected)
     inverse_norm = 1.0 / norm
     coefficients = jnp.where(down == rows + STEPS, inverse_norm, -(projected * inverse_norm))
+    vectors = []
     tails = []
     for block in range(slots + ghosts):
         old = old_ref[block]
@@ -237,10 +301,10 @@
             old = tail_with(old, [(STEPS, image)])
         vector = jnp.sum(held * coefficients[0:rows], axis=0, keepdims=True)
         vector = vector + jnp.sum(old * coefficients[rows : rows + TAIL], axis=0, keepdims=True)
-        vector_ref[block : block + 1, :] = vector
+        vectors.append(vector)
         tails.append(tail_with(old, [(step, vector), (STEPS, 0.0)]))
-    images = apply_tiles(tiles_ref, columns_ref, vector_ref, live_ref)
-    finish_step(step, tails, own_ref, images, tail_ref, out_ref)
+    images = apply_tiles(tiles_ref, pick_ref, vectors, mask_ref)
+    finish_step(tails, own_ref, images, tail_ref, out_ref)
 
 
 def small_solve(matrix, target):
@@ -272,7 +336,7 @@
     return back
 
 
-def end_body(count, live_ref, every_ref, own_ref, tail_ref, inverse_ref, start_ref, recycled_ref, *rest):
+def end_body(count, mask_ref, every_ref, own_ref, tail_ref, inverse_ref, start_ref, recycled_ref, *rest):
     histories, (solution_ref, residual_ref) = rest[:-2], rest[-2:]
     slots, rows, width = own_ref.shape
     full = rows + TAIL
@@ -310,7 +374,7 @@
     residual_tail = jnp.where(tail_down == STEPS, -ratio, residual_tail)
     for slot in range(slots):
         tail = tail_ref[slot]
-        mask = live(live_ref, slot)
+        mask = mask_ref[slot : slot + 1, :]
         point = jnp.sum(recycled_ref[:, slot, :] * mask * recycled_coefficients, axis=0, keepdims=True)
         point = point + jnp.sum(tail * solution_tail, axis=0, keepdims=True)
         solution_ref[slot : slot + 1, :] = point
@@ -328,24 +392,46 @@
     rows = round_up(count + 1, ROW_ALIGN)
     full = rows + TAIL
     blocks = slots + ghosts
-    (own,) = call(pack_body, "pack", [(slots, rows, width)], [SMEM, VMEM, VMEM])(live_counts, load_vector, images)
+    per_row = tile_columns.shape[1]
+    own, mask = call(
+        pack_body,
+        "pack",
+        [(slots, rows, width), (round_up(slots, 8), width)],
+        [SMEM, VMEM, VMEM],
+    )(live_counts, load_vector, images)
     group = lax.all_gather(own, "sub", axis=0, tiled=True)
-    up = [(i, i + 1) for i in range(doms - 1)]
-    down = [(j, i) for i, j in up]
-    before = lax.ppermute(group, "dom", up)
-    after = lax.ppermute(group, "dom", down)
     each = rows // lane_groups(count, rows, width)
     (grams,) = call(functools.partial(gram_body, count), "gram", [(doms, each, width)], [VMEM])(group)
     parts = lax.all_to_all(grams, "dom", 0, 0)
+    paired = subs % 2 == 0
+    if paired:
+        pairs = []
+        for d in range(doms):
+            for s in range(subs):
+                to = d + 1 if s % 2 else d - 1
+                if 0 <= to < doms:
+                    pairs.append((d * subs + s, to * subs + s))
+        one = lax.ppermute(group, AXES, pairs)
+        one, parts = lax.optimization_barrier((one, parts))
+        two = lax.ppermute(one, "sub", [(i, i ^ 1) for i in range(subs)])
+    else:
+        up = [(i, i + 1) for i in range(doms - 1)]
+        one = lax.ppermute(group, "dom", up)
+        two = lax.ppermute(group, "dom", [(j, i) for i, j in up])
     lines = round_up(slots + 1, 4)
-    scratch = [pltpu.VMEM((round_up(blocks, 8), width), F32)]
-    message, ghost_images, tails, inverse, start = call(
-        functools.partial(start_body, count),
+    inverse, start, pick, tiles = call(
+        functools.partial(factor_body, count, rows),
+        "factor",
+        [(full, width), (full, width), (blocks, slots * per_row, width), matrix_tiles.shape],
+        [VMEM, HBM, VMEM],
+        [pltpu.SemaphoreType.DMA],
+    )(tile_columns, pltpu.with_memory_space_constraint(matrix_tiles, pltpu.HBM), parts)
+    message, ghost_images, tails = call(
+        functools.partial(start_body, paired),
         "start",
-        [(devices, lines, width), (ghosts, rows, width), (blocks, TAIL, width), (full, width), (full, width)],
-        [SMEM] * 3 + [VMEM] * 6,
-        scratch,
-    )(live_counts, tile_columns, ghost_list, parts, own, before, group, after, matrix_tiles)
+        [(devices, lines, width), (ghosts, rows, width), (blocks, TAIL, width)],
+        [SMEM] + [VMEM] * 8,
+    )(ghost_list, start, own, one, group, two, tiles, pick, mask)
     histories = []
     for step in range(1, STEPS):
         every = lax.all_to_all(message, AXES, 0, 0)
@@ -354,9 +440,8 @@
             functools.partial(step_body, step, count),
             f"step{step}",
             [(devices, sent, width), (blocks, TAIL, width), (full, width)],
-            [SMEM] * 3 + [VMEM] * 6,
-            scratch,
-        )(live_counts, tile_columns, ghost_list, every, own, ghost_images, tails, inverse, matrix_tiles)
+            [SMEM] + [VMEM] * 8,
+        )(ghost_list, every, own, ghost_images, tails, inverse, tiles, pick, mask)
         histories.append(history)
     every = lax.all_to_all(message, AXES, 0, 0)
     return tuple(
@@ -364,8 +449,8 @@
             functools.partial(end_body, count),
             "end",
             [(slots, width), (slots, width)],
-            [SMEM] + [VMEM] * (6 + len(histories)),
-        )(live_counts, every, own, tails, inverse, start, recycled, *histories)
+            [VMEM] * (7 + len(histories)),
+        )(mask, every, own, tails, inverse, start, recycled, *histories)
     )
 
 

time: 64.2 us -> 59.5 us (0.927)
  starting transfers between devices: 5.84 us -> 1.28 us
  blocking collectives: 46.9 us -> 48.3 us
  Pallas kernels: 7.57 us -> 6.72 us
    ppermute x2, starting transfers between devices: 5.84 us -> 1.28 us  [the longest x1 1.28 us: local(): one = lax.ppermute(group, AXES, pairs)]
    all_to_all x1, blocking collectives: 12.7 us -> 14 us  [local(): parts = lax.all_to_all(grams, 'dom', 0, 0)]
    pallas_call x2 -> x3, Pallas kernels: 4.41 us -> 3.6 us  [the longest x1 2.72 us: local(): call(functools.partial(factor_body, count, rows), 'factor', [(full, width...]
    unnamed x14 -> x10, local copies, waits for them, and re-layouts: 2.03 us -> 1.44 us
  transfers between devices with their start and end apart: 2 -> 2, of which waited for: 0 -> 0; matrix products, arithmetic and copies ran while one was open for 0% -> 0% of each run, Pallas kernels for 1% -> 5%
where the time goes in v3:
time: 59.5 us; the launch traced here: 59.1 us
  blocking collectives  48.3 us (81%)
  Pallas kernels  6.72 us (11%)
  local copies, waits for them, and re-layouts  1.44 us (2%)
  between operations  1.37 us (2%)
  starting transfers between devices  1.28 us (2%)
    all_to_all x3, blocking collectives, local(): every = lax.all_to_all(message, AXES, 0, 0)  27.4 us
    all_to_all x1, blocking collectives, local(): parts = lax.all_to_all(grams, 'dom', 0, 0)  14 us
    all_gather x1, blocking collectives, local(): group = lax.all_gather(own, 'sub', axis=0, tiled=True)  6.89 us
    pallas_call x1, Pallas kernels, local(): call(functools.partial(factor_body, count, rows), 'factor', [(full, width...  2.72 us
    pallas_call x2, Pallas kernels, local(): call(functools.partial(step_body, step, count), f'step{step}', [(devices,...  1.89 us
    unnamed x10, local copies, waits for them, and re-layouts  1.44 us
    ppermute x1, starting transfers between devices, local(): one = lax.ppermute(group, AXES, pairs)  1.28 us
  transfers between devices with their start and end apart: 2, of which 0 were waited for; matrix products, arithmetic and copies ran while one was open for 0% of the time, Pallas kernels for 5%

profile of v3, /device:TPU:0, one launch (start us, length us, event | category | flops | bytes accessed | tf_op | source)
XLA Modules:
  0.0 59.1 jit_solution(11706779055814461683)
XLA Ops:
  0.6 0.0 copy-start.4
  1.3 0.0 copy-done.4
  1.3 0.0 copy-start
  1.3 0.8 %copy-done = f32[40,2,128]{2,1,0:T(2,128)S(1)} copy-done((f32[40,2,128]{2,1,0:T(2,128)S(1)}, f32[40,2,128]{2,1,0:T(2,128)}, u32[]{:S(2)}) %copy-start) | copy-done | bytes 40984
  2.1 6.9 %all_gather.3.group_ref = f32[8,48,128]{2,1,0:T(8,128)S(1)} all-gather(f32[2,48,128]{2,1,0:T(8,128)S(1)} %get-tuple-element.20.own_ref), channel_id=1, replica_groups=mesh['dom'=8,'sub'=4] {'sub'}, dimensions={0}, use_global_device_ids=true | all-gather | bytes 245760 | tf_op jit(solution)/shard_map/all_gather | solution.py:402
  9.0 1.3 %collective-permute-start = (f32[8,48,128]{2,1,0:T(8,128)S(1)}, f32[8,48,128]{2,1,0:T(8,128)S(1)}, u32[]{:S(2)}, u32[]{:S(2)}) collective-permute-start(f32[8,48,128]{2,1,0:T(8,128)S(1)} %all_gather.3.group_ref), channel_id=1, source_target_pairs={{1,5},{3,7},{4,0},{5,9},{6,2},{7,11},{8,4},{9,13},{10,6},{11,15},{... | collective-permute-start | bytes 589832 | tf_op jit(solution)/shard_map/ppermute | solution.py:414
  10.3 0.5 gram.1
  10.8 0.0 copy-start.3
  10.8 14.0 %all_to_all.20.parts_ref = f32[8,16,128]{2,1,0:T(8,128)S(1)} all-to-all(f32[8,16,128]{2,1,0:T(8,128)S(1)} %gram.1), channel_id=1, replica_groups=mesh['dom'=8,'sub'=4] {'dom'}, dimensions={0} | all-to-all | bytes 131072 | tf_op jit(solution)/shard_map/all_to_all | solution.py:405
  24.8 0.0 collective-permute-done.one_ref
  24.8 0.0 collective-permute-start.1
  24.8 0.0 copy-done.3
  24.8 2.7 %factor.1 = (f32[56,128]{1,0:T(8,128)S(1)}, f32[56,128]{1,0:T(8,128)S(1)}, f32[6,16,128]{2,1,0:T(8,128)S(1)}, f32[2,8,128,128]{3,2,1,0:T(8,128)S(1)}) custom-call(s32[2,8]{1,0:T(2,128)S(1)} %copy-done.3, f32[2,8,128,128]{3,2,1,0:T(8,128)} %tiles_ref.1, f32[8,16,128]{2,1,0:T(8,128)S(1)} %all_to_all.20.parts_ref), custom_call_target="tpu_custom_call" | custom-call | flops 10000000 | bytes 1048576 | tf_op jit(solution)/shard_map/factor/pallas_call | solution.py:422
  27.5 0.0 collective-permute-done.1.two_ref
  27.5 0.0 copy-start.2
  27.5 0.6 %copy-done.2 = s32[1,4]{1,0:T(1,128)S(1)} copy-done((s32[1,4]{1,0:T(1,128)S(1)}, s32[1,4]{1,0:T(1,128)}, u32[]{:S(2)}) %copy-start.2) | copy-done | bytes 40
  28.2 0.8 %start.1 = (f32[32,4,128]{2,1,0:T(4,128)S(1)}, f32[4,48,128]{2,1,0:T(8,128)S(1)}, f32[6,8,128]{2,1,0:T(8,128)S(1)}) custom-call(s32[1,4]{1,0:T(1,128)S(1)} %copy-done.2, f32[56,128]{1,0:T(8,128)S(1)} %get-tuple-element.22.start_ref, f32[2,48,128]{2,1,0:T(8,128)S(1)} %get-tuple-element.20.own_ref, f32[8,48,128]{2,1,0:T(8,128)S(1)} %collective-permute-done.one_ref, ...), custom_call_target="tpu_custom_call" | custom-call | flops 10000000 | bytes 1048576 | tf_op jit(solution)/shard_map/start/pallas_call | solution.py:429
  29.0 9.5 %all_to_all.21.every_ref = f32[32,4,128]{2,1,0:T(4,128)S(1)} all-to-all(f32[32,4,128]{2,1,0:T(4,128)S(1)} %get-tuple-element.26), channel_id=1, replica_groups=mesh['dom'=8,'sub'=4] {'dom','sub'}, dimensions={0} | all-to-all | bytes 131072 | tf_op jit(solution)/shard_map/all_to_all | solution.py:437
  38.5 0.9 %step1.1 = (f32[32,4,128]{2,1,0:T(4,128)S(1)}, f32[6,8,128]{2,1,0:T(8,128)S(1)}, f32[56,128]{1,0:T(8,128)S(1)}) custom-call(s32[1,4]{1,0:T(1,128)S(1)} %copy-done.2, f32[32,4,128]{2,1,0:T(4,128)S(1)} %all_to_all.21.every_ref, f32[2,48,128]{2,1,0:T(8,128)S(1)} %get-tuple-element.20.own_ref, f32[4,48,128]{2,1,0:T(8,128)S(1)} %get-tuple-element.27.ghost_ref, ...), custom_call_target="tpu_custom_call" | custom-call | flops 10000000 | bytes 1048576 | tf_op jit(solution)/shard_map/step1/pallas_call | solution.py:439
  39.5 9.1 %all_to_all.22.every_ref = f32[32,4,128]{2,1,0:T(4,128)S(1)} all-to-all(f32[32,4,128]{2,1,0:T(4,128)S(1)} %get-tuple-element.30), channel_id=1, replica_groups=mesh['dom'=8,'sub'=4] {'dom','sub'}, dimensions={0} | all-to-all | bytes 131072 | tf_op jit(solution)/shard_map/all_to_all | solution.py:437
  48.6 0.0 copy-start.1
  48.6 0.9 %step2.1 = (f32[32,1,128]{2,1,0:T(1,128)S(1)}, f32[6,8,128]{2,1,0:T(8,128)S(1)}, f32[56,128]{1,0:T(8,128)S(1)}) custom-call(s32[1,4]{1,0:T(1,128)S(1)} %copy-done.2, f32[32,4,128]{2,1,0:T(4,128)S(1)} %all_to_all.22.every_ref, f32[2,48,128]{2,1,0:T(8,128)S(1)} %get-tuple-element.20.own_ref, f32[4,48,128]{2,1,0:T(8,128)S(1)} %get-tuple-element.27.ghost_ref, ...), custom_call_target="tpu_custom_call" | custom-call | flops 10000000 | bytes 1048576 | tf_op jit(solution)/shard_map/step2/pallas_call | solution.py:439
  49.5 8.9 %all_to_all.23.every_ref = f32[32,1,128]{2,1,0:T(1,128)S(1)} all-to-all(f32[32,1,128]{2,1,0:T(1,128)S(1)} %get-tuple-element.32), channel_id=1, replica_groups=mesh['dom'=8,'sub'=4] {'dom','sub'}, dimensions={0} | all-to-all | bytes 32768 | tf_op jit(solution)/shard_map/all_to_all | solution.py:446
  58.4 0.0 copy-done.1
  58.4 0.7 %end.1 = (f32[2,128]{1,0:T(2,128)}, f32[2,128]{1,0:T(2,128)}) custom-call(f32[8,128]{1,0:T(8,128)S(1)} %get-tuple-element.19.mask_ref, f32[32,1,128]{2,1,0:T(1,128)S(1)} %all_to_all.23.every_ref, f32[2,48,128]{2,1,0:T(8,128)S(1)} %get-tuple-element.20.own_ref, f32[6,8,128]{2,1,0:T(8,128)S(1)} %get-tuple-element.33.tail_ref, ...), custom_call_target="tpu_custom_call" | custom-call | flops 10000000 | bytes 1048576 | tf_op jit(solution)/shard_map/end/pallas_call | solution.py:448
  (1 shorter events, 0.0 us)
Async XLA Ops:
  0.6 0.7 %copy-start.4 = (f32[2,128]{1,0:T(2,128)S(1)}, f32[2,128]{1,0:T(2,128)}, u32[]{:S(2)}) copy-start(f32[2,128]{1,0:T(2,128)} %load_ref.1) | copy-start | bytes 3076
  1.3 0.8 %copy-start = (f32[40,2,128]{2,1,0:T(2,128)S(1)}, f32[40,2,128]{2,1,0:T(2,128)}, u32[]{:S(2)}) copy-start(f32[40,2,128]{2,1,0:T(2,128)} %images_ref.1) | copy-start | bytes 122884
  9.0 15.8 %collective-permute-start = (f32[8,48,128]{2,1,0:T(8,128)S(1)}, f32[8,48,128]{2,1,0:T(8,128)S(1)}, u32[]{:S(2)}, u32[]{:S(2)}) collective-permute-start(f32[8,48,128]{2,1,0:T(8,128)S(1)} %all_gather.3.group_ref), channel_id=1, source_target_pairs={{1,5},{3,7},{4,0},{5,9},{6,2},{7,11},{8,4},{9,13},{10,6},{11,15},{... | collective-permute-start | bytes 589832 | tf_op jit(solution)/shard_map/ppermute | solution.py:414
  10.8 14.0 %copy-start.3 = (s32[2,8]{1,0:T(2,128)S(1)}, s32[2,8]{1,0:T(2,128)}, u32[]{:S(2)}) copy-start(s32[2,8]{1,0:T(2,128)} %columns_ref.1) | copy-start | bytes 196
  24.8 2.7 %collective-permute-start.1 = (f32[8,48,128]{2,1,0:T(8,128)S(1)}, f32[8,48,128]{2,1,0:T(8,128)S(1)}, u32[]{:S(2)}, u32[]{:S(2)}) collective-permute-start(f32[8,48,128]{2,1,0:T(8,128)S(1)} %collective-permute-done.one_ref), channel_id=1, source_target_pairs={{0,1},{1,0},{2,3},{3,2},{4,5},{5,4},{6,7},{7,6},{8,9},{9,8},{10,11... | collective-permute-start | bytes 589832 | tf_op jit(solution)/shard_map/ppermute | solution.py:416
  27.5 0.7 %copy-start.2 = (s32[1,4]{1,0:T(1,128)S(1)}, s32[1,4]{1,0:T(1,128)}, u32[]{:S(2)}) copy-start(s32[1,4]{1,0:T(1,128)} %ghosts_ref.5) | copy-start | bytes 52
  48.6 9.8 %copy-start.1 = (f32[40,2,128]{2,1,0:T(2,128)S(1)}, f32[40,2,128]{2,1,0:T(2,128)}, u32[]{:S(2)}) copy-start(f32[40,2,128]{2,1,0:T(2,128)} %recycled_ref.1) | copy-start | bytes 122884

commit v4 on v3

--- a/solution.py
+++ b/solution.py
@@ -166,22 +166,19 @@
     return images
 
 
-def tail_with(old, entries):
+def tail_with(old, row, value):
     down = lax.broadcasted_iota(jnp.int32, (TAIL, old.shape[1]), 0)
-    for row, value in entries:
-        old = jnp.where(down == row, value, old)
-    return old
-
-
-def finish_step(tails, own_ref, images, tail_ref, out_ref):
+    return jnp.where(down == row, value, old)
+
+
+def finish_step(vectors, tails, own_ref, tiles_ref, pick_ref, mask_ref, own_tail_ref, out_ref):
     slots, rows, width = own_ref.shape
-    last = STEPS
+    images = apply_tiles(tiles_ref, pick_ref, vectors, mask_ref)
     total = jnp.zeros((rows + TAIL, width), F32)
     for slot in range(slots):
-        tails[slot] = tail_with(tails[slot], [(last, images[slot])])
-        total = total + jnp.concatenate([own_ref[slot], tails[slot]], axis=0) * images[slot]
-    for block, tail in enumerate(tails):
-        tail_ref[block] = tail
+        tail = tail_with(tails[slot], STEPS, images[slot])
+        own_tail_ref[slot] = tail
+        total = total + jnp.concatenate([own_ref[slot], tail], axis=0) * images[slot]
     partial = to_row(jnp.sum(total, axis=1, keepdims=True), eye(rows + TAIL, width))
     copies, lines, _ = out_ref.shape
     if lines == 1:
@@ -193,18 +190,26 @@
 
 
 def factor_body(
-    count, rows, columns_ref, tiles_ref, parts_ref, inverse_ref, start_ref, pick_ref, here_ref, sem,
+    count, rows, paired, columns_ref, ghosts_ref, tiles_ref, parts_ref, inverse_ref, start_ref, pick_ref, here_ref, sem
 ):
     move = pltpu.make_async_copy(tiles_ref, here_ref, sem)
     move.start()
     width = parts_ref.shape[2]
     slots, per_row = columns_ref.shape
+    blocks = (pick_ref.shape[0] - slots) // 3
+    codes = ghosts_ref[...].astype(F32)
+    if paired:
+        flipped = jnp.where(codes < blocks, codes + 2 * blocks, jnp.where(codes < 2 * blocks, codes, codes - 2 * blocks))
+        codes = jnp.where(lax.axis_index("sub") % 2 == 0, flipped, codes)
     for slot in range(slots):
         names = columns_ref[slot : slot + 1, :].astype(F32)
-        column = jnp.sum(jnp.where(eye(per_row, per_row), names, 0.0), axis=1, keepdims=True)
+        places = names + 3 * blocks
+        for ghost in range(codes.shape[1]):
+            places = jnp.where(names == slots + ghost, codes[:, ghost : ghost + 1], places)
+        column = jnp.sum(jnp.where(eye(per_row, per_row), places, 0.0), axis=1, keepdims=True)
         column = jnp.broadcast_to(column, (per_row, width))
-        for block in range(pick_ref.shape[0]):
-            pick_ref[block, slot * per_row : (slot + 1) * per_row, :] = jnp.where(column == float(block), 1.0, 0.0)
+        for place in range(pick_ref.shape[0]):
+            pick_ref[place, slot * per_row : (slot + 1) * per_row, :] = jnp.where(column == place, 1.0, 0.0)
     groups = lane_groups(count, rows, width)
     lanes = width // groups
     packed = tree_sum([parts_ref[i] for i in range(parts_ref.shape[0])])
@@ -222,40 +227,33 @@
     inverse_ref[rows : rows + TAIL, :] = jnp.where(
         (tail_down < STEPS) & (tail_across == tail_down + rows), 1.0, 0.0
     )
-    norm = jnp.sqrt(swept[count : count + 1, count : count + 1])
+    squared = jnp.broadcast_to(swept[count : count + 1, count : count + 1], (TAIL, width))
+    inverse_norm = lax.rsqrt(squared)
     start = jnp.where(down < count, -swept[:, count : count + 1], jnp.where(down == count, 1.0, 0.0))
     start_ref[0:rows, :] = start
-    start_ref[rows : rows + TAIL, :] = jnp.broadcast_to(norm, (TAIL, width))
+    start_ref[rows : rows + TAIL, :] = jnp.where(tail_down == 0, squared * inverse_norm, inverse_norm)
     move.wait()
 
 
 def start_body(
-    paired, ghosts_ref, start_ref, own_ref, one_ref, group_ref, two_ref, tiles_ref, pick_ref, mask_ref,
-    out_ref, ghost_ref, tail_ref,
+    start_ref, own_ref, one_ref, group_ref, two_ref, tiles_ref, pick_ref, mask_ref, out_ref, tail_ref, own_tail_ref
 ):
     slots, rows, width = own_ref.shape
     blocks = group_ref.shape[0]
-    ghosts = ghosts_ref.shape[1]
-    after = lax.axis_index("sub") % 2 * 2 if paired else 2
-    coefficients = start_ref[0:rows, :] * (1.0 / start_ref[rows : rows + 1, :])
+    coefficients = start_ref[0:rows, :] * start_ref[rows + 1 : rows + 2, :]
+    empty = jnp.zeros((TAIL, width), F32)
     vectors = []
     tails = []
-    for block in range(slots + ghosts):
-        if block < slots:
-            held = own_ref[block]
-        else:
-            code = ghosts_ref[0, block - slots]
-            offset = code // blocks
-            place = code - offset * blocks
-            held = jnp.where(
-                offset == 1, group_ref[place], jnp.where(offset == after, two_ref[place], one_ref[place])
-            )
-            ghost_ref[block - slots] = held
-        vector = jnp.sum(held * coefficients, axis=0, keepdims=True)
-        vectors.append(vector)
-        tails.append(tail_with(jnp.zeros((TAIL, width), F32), [(0, vector)]))
-    images = apply_tiles(tiles_ref, pick_ref, vectors, mask_ref)
-    finish_step(tails, own_ref, images, tail_ref, out_ref)
+    for part in (one_ref, group_ref, two_ref, own_ref):
+        for place in range(part.shape[0]):
+            vector = jnp.sum(part[place] * coefficients, axis=0, keepdims=True)
+            tail = tail_with(empty, 0, vector)
+            if len(vectors) < 3 * blocks:
+                tail_ref[len(vectors)] = tail
+            else:
+                tails.append(tail)
+            vectors.append(vector)
+    finish_step(vectors, tails, own_ref, tiles_ref, pick_ref, mask_ref, own_tail_ref, out_ref)
 
 
 def project(total_row, inverse, rows, width):
@@ -267,44 +265,47 @@
     squared = jnp.sum(
         jnp.where(down == rows + STEPS, column, -(column * projected)), axis=0, keepdims=True
     )
-    return projected, jnp.sqrt(squared), down
+    inverse_norm = lax.rsqrt(squared)
+    return projected, squared * inverse_norm, inverse_norm, down
 
 
 def step_body(
-    step, count, ghosts_ref, every_ref, own_ref, ghost_ref, old_ref, inverse_ref, tiles_ref, pick_ref, mask_ref,
-    out_ref, tail_ref, history_ref,
+    step, count, paired, every_ref, own_ref, one_ref, group_ref, two_ref, old_ref, old_own_ref, inverse_ref,
+    tiles_ref, pick_ref, mask_ref, out_ref, tail_ref, own_tail_ref, history_ref,
 ):
     slots, rows, width = own_ref.shape
-    ghosts = ghosts_ref.shape[1]
     subs = lax.axis_size("sub")
-    span = subs * slots
     dom = lax.axis_index("dom")
+    toward = lax.axis_index("sub") % 2 * 2 - 1 if paired else 1
     total_row = tree_sum([every_ref[i, slots : slots + 1, :] for i in range(every_ref.shape[0])])
-    projected, norm, down = project(total_row, inverse_ref[...], rows, width)
+    projected, norm, inverse_norm, down = project(total_row, inverse_ref[...], rows, width)
     history_ref[...] = jnp.where(down == count, norm, projected)
-    inverse_norm = 1.0 / norm
     coefficients = jnp.where(down == rows + STEPS, inverse_norm, -(projected * inverse_norm))
+    head, foot = coefficients[0:rows], coefficients[rows : rows + TAIL]
     vectors = []
+    for part, shift in ((one_ref, -toward), (group_ref, 0), (two_ref, toward)):
+        first = jnp.clip(dom + shift, 0, lax.axis_size("dom") - 1) * subs
+        for place in range(part.shape[0]):
+            at = len(vectors)
+            old = old_ref[at]
+            image = every_ref[first + place // slots, place % slots : place % slots + 1, :]
+            vector = jnp.sum(part[place] * head, axis=0, keepdims=True)
+            vector = vector + jnp.sum(old * foot, axis=0, keepdims=True) + image * inverse_norm
+            if tail_ref is not None:
+                tail_ref[at] = tail_with(old, step, vector)
+            vectors.append(vector)
     tails = []
-    for block in range(slots + ghosts):
-        old = old_ref[block]
-        if block < slots:
-            held = own_ref[block]
-        else:
-            held = ghost_ref[block - slots]
-            code = ghosts_ref[0, block - slots]
-            offset = code // span
-            place = code - offset * span
-            peer = place // slots
-            device = (dom + offset - 1) * subs + peer
-            image = every_ref[device, pl.ds(place - peer * slots, 1), :]
-            old = tail_with(old, [(STEPS, image)])
-        vector = jnp.sum(held * coefficients[0:rows], axis=0, keepdims=True)
-        vector = vector + jnp.sum(old * coefficients[rows : rows + TAIL], axis=0, keepdims=True)
+    for slot in range(slots):
+        old = old_own_ref[slot]
+        vector = jnp.sum(own_ref[slot] * head, axis=0, keepdims=True)
+        vector = vector + jnp.sum(old * foot, axis=0, keepdims=True)
+        tails.append(tail_with(old, step, vector))
         vectors.append(vector)
-        tails.append(tail_with(old, [(step, vector), (STEPS, 0.0)]))
-    images = apply_tiles(tiles_ref, pick_ref, vectors, mask_ref)
-    finish_step(tails, own_ref, images, tail_ref, out_ref)
+    finish_step(vectors, tails, own_ref, tiles_ref, pick_ref, mask_ref, own_tail_ref, out_ref)
+
+
+def last_step_body(step, count, paired, *refs):
+    step_body(step, count, paired, *refs[:12], None, *refs[12:])
 
 
 def small_solve(matrix, target):
@@ -341,7 +342,7 @@
     slots, rows, width = own_ref.shape
     full = rows + TAIL
     total_row = tree_sum([every_ref[i] for i in range(every_ref.shape[0])])
-    projected, norm, down = project(total_row, inverse_ref[...], rows, width)
+    projected, norm, _, down = project(total_row, inverse_ref[...], rows, width)
     columns = [history[...] for history in histories]
     columns.append(jnp.where(down == count, norm, projected))
     entries = []
@@ -386,12 +387,10 @@
 def local(load_vector, recycled, images, matrix_tiles, tile_columns, ghost_list, live_counts):
     slots, width = load_vector.shape
     count = recycled.shape[0]
-    ghosts = ghost_list.shape[1]
     doms, subs = lax.axis_size("dom"), lax.axis_size("sub")
     devices = doms * subs
     rows = round_up(count + 1, ROW_ALIGN)
     full = rows + TAIL
-    blocks = slots + ghosts
     per_row = tile_columns.shape[1]
     own, mask = call(
         pack_body,
@@ -419,29 +418,35 @@
         one = lax.ppermute(group, "dom", up)
         two = lax.ppermute(group, "dom", [(j, i) for i, j in up])
     lines = round_up(slots + 1, 4)
+    near = 3 * group.shape[0]
     inverse, start, pick, tiles = call(
-        functools.partial(factor_body, count, rows),
+        functools.partial(factor_body, count, rows, paired),
         "factor",
-        [(full, width), (full, width), (blocks, slots * per_row, width), matrix_tiles.shape],
-        [VMEM, HBM, VMEM],
+        [(full, width), (full, width), (near + slots, slots * per_row, width), matrix_tiles.shape],
+        [VMEM, VMEM, HBM, VMEM],
         [pltpu.SemaphoreType.DMA],
-    )(tile_columns, pltpu.with_memory_space_constraint(matrix_tiles, pltpu.HBM), parts)
-    message, ghost_images, tails = call(
-        functools.partial(start_body, paired),
+    )(tile_columns, ghost_list, pltpu.with_memory_space_constraint(matrix_tiles, pltpu.HBM), parts)
+    message, tails, own_tails = call(
+        start_body,
         "start",
-        [(devices, lines, width), (ghosts, rows, width), (blocks, TAIL, width)],
-        [SMEM] + [VMEM] * 8,
-    )(ghost_list, start, own, one, group, two, tiles, pick, mask)
+        [(devices, lines, width), (near, TAIL, width), (slots, TAIL, width)],
+        [VMEM] * 8,
+    )(start, own, one, group, two, tiles, pick, mask)
     histories = []
     for step in range(1, STEPS):
         every = lax.all_to_all(message, AXES, 0, 0)
-        sent = lines if step < STEPS - 1 else 1
-        message, tails, history = call(
-            functools.partial(step_body, step, count),
+        last = step == STEPS - 1
+        sent = 1 if last else lines
+        results = call(
+            functools.partial(last_step_body if last else step_body, step, count, paired),
             f"step{step}",
-            [(devices, sent, width), (blocks, TAIL, width), (full, width)],
-            [SMEM] + [VMEM] * 8,
-        )(ghost_list, every, own, ghost_images, tails, inverse, tiles, pick, mask)
+            [(devices, sent, width)]
+            + ([] if last else [(near, TAIL, width)])
+            + [(slots, TAIL, width), (full, width)],
+            [VMEM] * 11,
+        )(every, own, one, group, two, tails, own_tails, inverse, tiles, pick, mask)
+        message, own_tails, history = results[0], results[-2], results[-1]
+        tails = tails if last else results[1]
         histories.append(history)
     every = lax.all_to_all(message, AXES, 0, 0)
     return tuple(
@@ -450,7 +455,7 @@
             "end",
             [(slots, width), (slots, width)],
             [VMEM] * (7 + len(histories)),
-        )(mask, every, own, tails, inverse, start, recycled, *histories)
+        )(mask, every, own, own_tails, inverse, start, recycled, *histories)
     )
 
 

time: 59.5 us -> 57.5 us (0.966)
  Pallas kernels: 6.72 us -> 5.32 us
  local copies, waits for them, and re-layouts: 1.44 us -> 0.8 us
    pallas_call x4, Pallas kernels: 5.46 us -> 4.06 us  [the longest x1 2.76 us: local(): call(functools.partial(factor_body, count, rows, paired), 'factor', [(ful...]
    unnamed x10, local copies, waits for them, and re-layouts: 1.44 us -> 0.8 us
  transfers between devices with their start and end apart: 2 -> 2, of which waited for: 0 -> 0; matrix products, arithmetic and copies ran while one was open for 0% -> 0% of each run, Pallas kernels for 5% -> 6%
where the time goes in v4:
time: 57.5 us; the launch traced here: 57.1 us
  blocking collectives  48.3 us (84%)
  Pallas kernels  5.32 us (9%)
  between operations  1.38 us (2%)
  starting transfers between devices  1.28 us (2%)
  local copies, waits for them, and re-layouts  0.8 us (1%)
    all_to_all x3, blocking collectives, local(): every = lax.all_to_all(message, AXES, 0, 0)  27.4 us
    all_to_all x1, blocking collectives, local(): parts = lax.all_to_all(grams, 'dom', 0, 0)  14 us
    all_gather x1, blocking collectives, local(): group = lax.all_gather(own, 'sub', axis=0, tiled=True)  6.89 us
    pallas_call x1, Pallas kernels, local(): call(functools.partial(factor_body, count, rows, paired), 'factor', [(ful...  2.76 us
    ppermute x1, starting transfers between devices, local(): one = lax.ppermute(group, AXES, pairs)  1.28 us
  transfers between devices with their start and end apart: 2, of which 0 were waited for; matrix products, arithmetic and copies ran while one was open for 0% of the time, Pallas kernels for 6%

profile of v4, /device:TPU:0, one launch (start us, length us, event | category | flops | bytes accessed | tf_op | source)
XLA Modules:
  0.0 57.1 jit_solution(1900705075992069960)
XLA Ops:
  0.6 0.0 copy-start.3
  1.3 0.0 copy-done.3
  1.3 0.0 copy-start.1
  1.3 0.8 %copy-done.1 = f32[40,2,128]{2,1,0:T(2,128)S(1)} copy-done((f32[40,2,128]{2,1,0:T(2,128)S(1)}, f32[40,2,128]{2,1,0:T(2,128)}, u32[]{:S(2)}) %copy-start.1) | copy-done | bytes 40984
  2.1 6.9 %all_gather.3.group_ref.refs_3_ = f32[8,48,128]{2,1,0:T(8,128)S(1)} all-gather(f32[2,48,128]{2,1,0:T(8,128)S(1)} %get-tuple-element.21.own_ref.refs_1_), channel_id=1, replica_groups=mesh['dom'=8,'sub'=4] {'sub'}, dimensions={0}, use_global_device_ids=true | all-gather | bytes 245760 | tf_op jit(solution)/shard_map/all_gather | solution.py:401
  9.0 1.3 %collective-permute-start = (f32[8,48,128]{2,1,0:T(8,128)S(1)}, f32[8,48,128]{2,1,0:T(8,128)S(1)}, u32[]{:S(2)}, u32[]{:S(2)}) collective-permute-start(f32[8,48,128]{2,1,0:T(8,128)S(1)} %all_gather.3.group_ref.refs_3_), channel_id=1, source_target_pairs={{1,5},{3,7},{4,0},{5,9},{6,2},{7,11},{8,4},{9,13},{10,6},{11,15},{... | collective-permute-start | bytes 589832 | tf_op jit(solution)/shard_map/ppermute | solution.py:413
  10.3 0.5 gram.1
  10.8 0.0 copy-start.2
  10.8 0.0 copy-start.4
  10.8 14.0 %all_to_all.20.parts_ref = f32[8,16,128]{2,1,0:T(8,128)S(1)} all-to-all(f32[8,16,128]{2,1,0:T(8,128)S(1)} %gram.1), channel_id=1, replica_groups=mesh['dom'=8,'sub'=4] {'dom'}, dimensions={0} | all-to-all | bytes 131072 | tf_op jit(solution)/shard_map/all_to_all | solution.py:404
  24.8 0.0 collective-permute-done.one_ref.refs_2_
  24.8 0.0 collective-permute-start.1
  24.8 0.0 copy-done.2
  24.8 0.0 copy-done.4
  24.8 2.8 %factor.1 = (f32[56,128]{1,0:T(8,128)S(1)}, f32[56,128]{1,0:T(8,128)S(1)}, f32[26,16,128]{2,1,0:T(8,128)S(1)}, f32[2,8,128,128]{3,2,1,0:T(8,128)S(1)}) custom-call(s32[2,8]{1,0:T(2,128)S(1)} %copy-done.2, s32[1,4]{1,0:T(1,128)S(1)} %copy-done.4, f32[2,8,128,128]{3,2,1,0:T(8,128)} %tiles_ref.1, f32[8,16,128]{2,1,0:T(8,128)S(1)} %all_to_all.20.parts_ref), custom_call_target="tpu_custom_call" | custom-call | flops 10000000 | bytes 1048576 | tf_op jit(solution)/shard_map/factor/pallas_call | solution.py:422
  27.6 0.0 collective-permute-done.1.two_ref.refs_4_
  27.6 0.3 start.1
  27.9 9.5 %all_to_all.21.every_ref = f32[32,4,128]{2,1,0:T(4,128)S(1)} all-to-all(f32[32,4,128]{2,1,0:T(4,128)S(1)} %get-tuple-element.27), channel_id=1, replica_groups=mesh['dom'=8,'sub'=4] {'dom','sub'}, dimensions={0} | all-to-all | bytes 131072 | tf_op jit(solution)/shard_map/all_to_all | solution.py:437
  37.4 0.5 step1.1
  37.9 9.1 %all_to_all.22.refs_0_ = f32[32,4,128]{2,1,0:T(4,128)S(1)} all-to-all(f32[32,4,128]{2,1,0:T(4,128)S(1)} %get-tuple-element.31), channel_id=1, replica_groups=mesh['dom'=8,'sub'=4] {'dom','sub'}, dimensions={0} | all-to-all | bytes 131072 | tf_op jit(solution)/shard_map/all_to_all | solution.py:437
  47.0 0.0 copy-start
  47.0 0.5 step2.1
  47.5 8.9 %all_to_all.23.every_ref = f32[32,1,128]{2,1,0:T(1,128)S(1)} all-to-all(f32[32,1,128]{2,1,0:T(1,128)S(1)} %get-tuple-element.34), channel_id=1, replica_groups=mesh['dom'=8,'sub'=4] {'dom','sub'}, dimensions={0} | all-to-all | bytes 32768 | tf_op jit(solution)/shard_map/all_to_all | solution.py:451
  56.4 0.0 copy-done
  56.4 0.7 %end.1 = (f32[2,128]{1,0:T(2,128)}, f32[2,128]{1,0:T(2,128)}) custom-call(f32[8,128]{1,0:T(8,128)S(1)} %get-tuple-element.20.mask_ref.refs_10_, f32[32,1,128]{2,1,0:T(1,128)S(1)} %all_to_all.23.every_ref, f32[2,48,128]{2,1,0:T(8,128)S(1)} %get-tuple-element.21.own_ref.refs_1_, f32[2,8,128]{2,1,0:T(8,128)S(1)} %get-tuple-element.35.tail_ref, ...), custom_call_target="tpu_custom_call" | custom-call | flops 10000000 | bytes 1048576 | tf_op jit(solution)/shard_map/end/pallas_call | solution.py:453
  (1 shorter events, 0.0 us)
Async XLA Ops:
  0.6 0.7 %copy-start.3 = (f32[2,128]{1,0:T(2,128)S(1)}, f32[2,128]{1,0:T(2,128)}, u32[]{:S(2)}) copy-start(f32[2,128]{1,0:T(2,128)} %load_ref.1) | copy-start | bytes 3076
  1.3 0.8 %copy-start.1 = (f32[40,2,128]{2,1,0:T(2,128)S(1)}, f32[40,2,128]{2,1,0:T(2,128)}, u32[]{:S(2)}) copy-start(f32[40,2,128]{2,1,0:T(2,128)} %images_ref.1) | copy-start | bytes 122884
  9.0 15.8 %collective-permute-start = (f32[8,48,128]{2,1,0:T(8,128)S(1)}, f32[8,48,128]{2,1,0:T(8,128)S(1)}, u32[]{:S(2)}, u32[]{:S(2)}) collective-permute-start(f32[8,48,128]{2,1,0:T(8,128)S(1)} %all_gather.3.group_ref.refs_3_), channel_id=1, source_target_pairs={{1,5},{3,7},{4,0},{5,9},{6,2},{7,11},{8,4},{9,13},{10,6},{11,15},{... | collective-permute-start | bytes 589832 | tf_op jit(solution)/shard_map/ppermute | solution.py:413
  10.8 14.0 %copy-start.2 = (s32[2,8]{1,0:T(2,128)S(1)}, s32[2,8]{1,0:T(2,128)}, u32[]{:S(2)}) copy-start(s32[2,8]{1,0:T(2,128)} %columns_ref.1) | copy-start | bytes 196
  10.8 14.0 %copy-start.4 = (s32[1,4]{1,0:T(1,128)S(1)}, s32[1,4]{1,0:T(1,128)}, u32[]{:S(2)}) copy-start(s32[1,4]{1,0:T(1,128)} %ghosts_ref.1) | copy-start | bytes 52
  24.8 2.8 %collective-permute-start.1 = (f32[8,48,128]{2,1,0:T(8,128)S(1)}, f32[8,48,128]{2,1,0:T(8,128)S(1)}, u32[]{:S(2)}, u32[]{:S(2)}) collective-permute-start(f32[8,48,128]{2,1,0:T(8,128)S(1)} %collective-permute-done.one_ref.refs_2_), channel_id=1, source_target_pairs={{0,1},{1,0},{2,3},{3,2},{4,5},{5,4},{6,7},{7,6},{8,9},{9,8},{10,11... | collective-permute-start | bytes 589832 | tf_op jit(solution)/shard_map/ppermute | solution.py:415
  47.0 9.4 %copy-start = (f32[40,2,128]{2,1,0:T(2,128)S(1)}, f32[40,2,128]{2,1,0:T(2,128)}, u32[]{:S(2)}) copy-start(f32[40,2,128]{2,1,0:T(2,128)} %recycled_ref.1) | copy-start | bytes 122884

commit v5 on v4

--- a/solution.py
+++ b/solution.py
@@ -195,24 +195,9 @@
     move = pltpu.make_async_copy(tiles_ref, here_ref, sem)
     move.start()
     width = parts_ref.shape[2]
-    slots, per_row = columns_ref.shape
-    blocks = (pick_ref.shape[0] - slots) // 3
-    codes = ghosts_ref[...].astype(F32)
-    if paired:
-        flipped = jnp.where(codes < blocks, codes + 2 * blocks, jnp.where(codes < 2 * blocks, codes, codes - 2 * blocks))
-        codes = jnp.where(lax.axis_index("sub") % 2 == 0, flipped, codes)
-    for slot in range(slots):
-        names = columns_ref[slot : slot + 1, :].astype(F32)
-        places = names + 3 * blocks
-        for ghost in range(codes.shape[1]):
-            places = jnp.where(names == slots + ghost, codes[:, ghost : ghost + 1], places)
-        column = jnp.sum(jnp.where(eye(per_row, per_row), places, 0.0), axis=1, keepdims=True)
-        column = jnp.broadcast_to(column, (per_row, width))
-        for place in range(pick_ref.shape[0]):
-            pick_ref[place, slot * per_row : (slot + 1) * per_row, :] = jnp.where(column == place, 1.0, 0.0)
     groups = lane_groups(count, rows, width)
     lanes = width // groups
-    packed = tree_sum([parts_ref[i] for i in range(parts_ref.shape[0])])
+    packed = lax.fori_loop(1, parts_ref.shape[0], lambda i, held: held + parts_ref[i], parts_ref[0])
     across = lax.broadcasted_iota(jnp.int32, (rows, width), 1)
     down = lax.broadcasted_iota(jnp.int32, (rows, width), 0)
     pieces = [packed]
@@ -232,6 +217,21 @@
     start = jnp.where(down < count, -swept[:, count : count + 1], jnp.where(down == count, 1.0, 0.0))
     start_ref[0:rows, :] = start
     start_ref[rows : rows + TAIL, :] = jnp.where(tail_down == 0, squared * inverse_norm, inverse_norm)
+    slots, per_row = columns_ref.shape
+    blocks = (pick_ref.shape[0] - slots) // 3
+    codes = ghosts_ref[...].astype(F32)
+    if paired:
+        flipped = jnp.where(codes < blocks, codes + 2 * blocks, jnp.where(codes < 2 * blocks, codes, codes - 2 * blocks))
+        codes = jnp.where(lax.axis_index("sub") % 2 == 0, flipped, codes)
+    for slot in range(slots):
+        names = columns_ref[slot : slot + 1, :].astype(F32)
+        places = names + 3 * blocks
+        for ghost in range(codes.shape[1]):
+            places = jnp.where(names == slots + ghost, codes[:, ghost : ghost + 1], places)
+        column = jnp.sum(jnp.where(eye(per_row, per_row), places, 0.0), axis=1, keepdims=True)
+        column = jnp.broadcast_to(column, (per_row, width))
+        for place in range(pick_ref.shape[0]):
+            pick_ref[place, slot * per_row : (slot + 1) * per_row, :] = jnp.where(column == place, 1.0, 0.0)
     move.wait()
 
 

time: 57.5 us -> 56.4 us (0.981)
  Pallas kernels: 5.32 us -> 4.29 us
    pallas_call x1, Pallas kernels: 2.76 us -> 1.73 us  [local(): call(functools.partial(factor_body, count, rows, paired), 'factor', [(ful...]
  transfers between devices with their start and end apart: 2 -> 2, of which waited for: 0 -> 0; matrix products, arithmetic and copies ran while one was open for 0% -> 0% of each run, Pallas kernels for 6% -> 4%
where the time goes in v5:
time: 56.4 us; the launch traced here: 56.1 us
  blocking collectives  48.3 us (86%)
  Pallas kernels  4.29 us (8%)
  between operations  1.38 us (2%)
  starting transfers between devices  1.28 us (2%)
  local copies, waits for them, and re-layouts  0.8 us (1%)
    all_to_all x3, blocking collectives, local(): every = lax.all_to_all(message, AXES, 0, 0)  27.4 us
    all_to_all x1, blocking collectives, local(): parts = lax.all_to_all(grams, 'dom', 0, 0)  14 us
    all_gather x1, blocking collectives, local(): group = lax.all_gather(own, 'sub', axis=0, tiled=True)  6.89 us
    pallas_call x1, Pallas kernels, local(): call(functools.partial(factor_body, count, rows, paired), 'factor', [(ful...  1.73 us
    ppermute x1, starting transfers between devices, local(): one = lax.ppermute(group, AXES, pairs)  1.28 us
  transfers between devices with their start and end apart: 2, of which 0 were waited for; matrix products, arithmetic and copies ran while one was open for 0% of the time, Pallas kernels for 4%

profile of v5, /device:TPU:0, one launch (start us, length us, event | category | flops | bytes accessed | tf_op | source)
XLA Modules:
  0.0 56.1 jit_solution(14298174981096899432)
XLA Ops:
  0.6 0.0 copy-start.3
  1.3 0.0 copy-done.3
  1.3 0.0 copy-start.1
  1.3 0.8 %copy-done.1 = f32[40,2,128]{2,1,0:T(2,128)S(1)} copy-done((f32[40,2,128]{2,1,0:T(2,128)S(1)}, f32[40,2,128]{2,1,0:T(2,128)}, u32[]{:S(2)}) %copy-start.1) | copy-done | bytes 40984
  2.1 6.9 %all_gather.3.group_ref.refs_3_ = f32[8,48,128]{2,1,0:T(8,128)S(1)} all-gather(f32[2,48,128]{2,1,0:T(8,128)S(1)} %get-tuple-element.21.own_ref.refs_1_), channel_id=1, replica_groups=mesh['dom'=8,'sub'=4] {'sub'}, dimensions={0}, use_global_device_ids=true | all-gather | bytes 245760 | tf_op jit(solution)/shard_map/all_gather | solution.py:401
  9.0 1.3 %collective-permute-start = (f32[8,48,128]{2,1,0:T(8,128)S(1)}, f32[8,48,128]{2,1,0:T(8,128)S(1)}, u32[]{:S(2)}, u32[]{:S(2)}) collective-permute-start(f32[8,48,128]{2,1,0:T(8,128)S(1)} %all_gather.3.group_ref.refs_3_), channel_id=1, source_target_pairs={{1,5},{3,7},{4,0},{5,9},{6,2},{7,11},{8,4},{9,13},{10,6},{11,15},{... | collective-permute-start | bytes 589832 | tf_op jit(solution)/shard_map/ppermute | solution.py:413
  10.3 0.5 gram.1
  10.8 0.0 copy-start.2
  10.8 0.0 copy-start.4
  10.8 14.0 %all_to_all.20.parts_ref = f32[8,16,128]{2,1,0:T(8,128)S(1)} all-to-all(f32[8,16,128]{2,1,0:T(8,128)S(1)} %gram.1), channel_id=1, replica_groups=mesh['dom'=8,'sub'=4] {'dom'}, dimensions={0} | all-to-all | bytes 131072 | tf_op jit(solution)/shard_map/all_to_all | solution.py:404
  24.8 0.0 collective-permute-done.one_ref.refs_2_
  24.8 0.0 collective-permute-start.1
  24.8 0.0 copy-done.2
  24.8 0.0 copy-done.4
  24.8 1.7 %factor.1 = (f32[56,128]{1,0:T(8,128)S(1)}, f32[56,128]{1,0:T(8,128)S(1)}, f32[26,16,128]{2,1,0:T(8,128)S(1)}, f32[2,8,128,128]{3,2,1,0:T(8,128)S(1)}) custom-call(s32[2,8]{1,0:T(2,128)S(1)} %copy-done.2, s32[1,4]{1,0:T(1,128)S(1)} %copy-done.4, f32[2,8,128,128]{3,2,1,0:T(8,128)} %tiles_ref.1, f32[8,16,128]{2,1,0:T(8,128)S(1)} %all_to_all.20.parts_ref), custom_call_target="tpu_custom_call" | custom-call | flops 10000000 | bytes 1048576 | tf_op jit(solution)/shard_map/factor/pallas_call | solution.py:422
  26.6 0.0 collective-permute-done.1.two_ref.refs_4_
  26.6 0.3 start.1
  26.9 9.5 %all_to_all.21.every_ref = f32[32,4,128]{2,1,0:T(4,128)S(1)} all-to-all(f32[32,4,128]{2,1,0:T(4,128)S(1)} %get-tuple-element.27), channel_id=1, replica_groups=mesh['dom'=8,'sub'=4] {'dom','sub'}, dimensions={0} | all-to-all | bytes 131072 | tf_op jit(solution)/shard_map/all_to_all | solution.py:437
  36.4 0.5 step1.1
  36.9 9.1 %all_to_all.22.refs_0_ = f32[32,4,128]{2,1,0:T(4,128)S(1)} all-to-all(f32[32,4,128]{2,1,0:T(4,128)S(1)} %get-tuple-element.31), channel_id=1, replica_groups=mesh['dom'=8,'sub'=4] {'dom','sub'}, dimensions={0} | all-to-all | bytes 131072 | tf_op jit(solution)/shard_map/all_to_all | solution.py:437
  46.0 0.0 copy-start
  46.0 0.5 step2.1
  46.4 8.9 %all_to_all.23.every_ref = f32[32,1,128]{2,1,0:T(1,128)S(1)} all-to-all(f32[32,1,128]{2,1,0:T(1,128)S(1)} %get-tuple-element.34), channel_id=1, replica_groups=mesh['dom'=8,'sub'=4] {'dom','sub'}, dimensions={0} | all-to-all | bytes 32768 | tf_op jit(solution)/shard_map/all_to_all | solution.py:451
  55.3 0.0 copy-done
  55.3 0.7 %end.1 = (f32[2,128]{1,0:T(2,128)}, f32[2,128]{1,0:T(2,128)}) custom-call(f32[8,128]{1,0:T(8,128)S(1)} %get-tuple-element.20.mask_ref.refs_10_, f32[32,1,128]{2,1,0:T(1,128)S(1)} %all_to_all.23.every_ref, f32[2,48,128]{2,1,0:T(8,128)S(1)} %get-tuple-element.21.own_ref.refs_1_, f32[2,8,128]{2,1,0:T(8,128)S(1)} %get-tuple-element.35.tail_ref, ...), custom_call_target="tpu_custom_call" | custom-call | flops 10000000 | bytes 1048576 | tf_op jit(solution)/shard_map/end/pallas_call | solution.py:453
  (1 shorter events, 0.0 us)
Async XLA Ops:
  0.6 0.7 %copy-start.3 = (f32[2,128]{1,0:T(2,128)S(1)}, f32[2,128]{1,0:T(2,128)}, u32[]{:S(2)}) copy-start(f32[2,128]{1,0:T(2,128)} %load_ref.1) | copy-start | bytes 3076
  1.3 0.8 %copy-start.1 = (f32[40,2,128]{2,1,0:T(2,128)S(1)}, f32[40,2,128]{2,1,0:T(2,128)}, u32[]{:S(2)}) copy-start(f32[40,2,128]{2,1,0:T(2,128)} %images_ref.1) | copy-start | bytes 122884
  9.0 15.8 %collective-permute-start = (f32[8,48,128]{2,1,0:T(8,128)S(1)}, f32[8,48,128]{2,1,0:T(8,128)S(1)}, u32[]{:S(2)}, u32[]{:S(2)}) collective-permute-start(f32[8,48,128]{2,1,0:T(8,128)S(1)} %all_gather.3.group_ref.refs_3_), channel_id=1, source_target_pairs={{1,5},{3,7},{4,0},{5,9},{6,2},{7,11},{8,4},{9,13},{10,6},{11,15},{... | collective-permute-start | bytes 589832 | tf_op jit(solution)/shard_map/ppermute | solution.py:413
  10.8 14.0 %copy-start.2 = (s32[2,8]{1,0:T(2,128)S(1)}, s32[2,8]{1,0:T(2,128)}, u32[]{:S(2)}) copy-start(s32[2,8]{1,0:T(2,128)} %columns_ref.1) | copy-start | bytes 196
  10.8 14.0 %copy-start.4 = (s32[1,4]{1,0:T(1,128)S(1)}, s32[1,4]{1,0:T(1,128)}, u32[]{:S(2)}) copy-start(s32[1,4]{1,0:T(1,128)} %ghosts_ref.1) | copy-start | bytes 52
  24.8 1.8 %collective-permute-start.1 = (f32[8,48,128]{2,1,0:T(8,128)S(1)}, f32[8,48,128]{2,1,0:T(8,128)S(1)}, u32[]{:S(2)}, u32[]{:S(2)}) collective-permute-start(f32[8,48,128]{2,1,0:T(8,128)S(1)} %collective-permute-done.one_ref.refs_2_), channel_id=1, source_target_pairs={{0,1},{1,0},{2,3},{3,2},{4,5},{5,4},{6,7},{7,6},{8,9},{9,8},{10,11... | collective-permute-start | bytes 589832 | tf_op jit(solution)/shard_map/ppermute | solution.py:415
  46.0 9.4 %copy-start = (f32[40,2,128]{2,1,0:T(2,128)S(1)}, f32[40,2,128]{2,1,0:T(2,128)}, u32[]{:S(2)}) copy-start(f32[40,2,128]{2,1,0:T(2,128)} %recycled_ref.1) | copy-start | bytes 122884

commit v6 on v5

--- a/solution.py
+++ b/solution.py
@@ -6,6 +6,7 @@
 from jax.experimental import pallas as pl
 from jax.experimental.pallas import tpu as pltpu
 from jax.sharding import PartitionSpec as P
+
 
 STEPS = 3
 TAIL = 8
@@ -17,10 +18,9 @@
 F32 = jnp.float32
 
 
-def call(body, name, outs, specs, scratch=(), work=10_000_000):
+def call(body, outs, specs, scratch=(), work=10_000_000):
     return pl.pallas_call(
         body,
-        name=name,
         out_shape=[jax.ShapeDtypeStruct(shape, F32) for shape in outs],
         in_specs=specs,
         out_specs=[VMEM] * len(outs),
@@ -61,6 +61,14 @@
         own_ref[slot, 0:count, :] = images_ref[:, slot, :] * mask
         own_ref[slot, count : count + 1, :] = load_ref[slot : slot + 1, :] * mask
         own_ref[slot, count + 1 : rows, :] = jnp.zeros((rows - count - 1, width), F32)
+
+
+def join_body(*refs):
+    place = 0
+    for part in refs[:-1]:
+        for block in range(part.shape[0]):
+            refs[-1][place] = part[block]
+            place += 1
 
 
 def lane_groups(count, rows, width):
@@ -189,8 +197,17 @@
     out_ref[...] = jnp.broadcast_to(message[None], (copies, lines, width))
 
 
+def near_peers(subs, paired, doubling):
+    me = lax.axis_index("sub")
+    first = (1 - me % 2) * 2 if paired else 0
+    result = []
+    for part, swapped in ((first, 0), (1, 0), (2 - first, 1 if paired else 0)):
+        result.append((part, [(peer ^ swapped) ^ me if doubling else peer for peer in range(subs)]))
+    return result
+
+
 def factor_body(
-    count, rows, paired, columns_ref, ghosts_ref, tiles_ref, parts_ref, inverse_ref, start_ref, pick_ref, here_ref, sem
+    count, rows, paired, doubling, columns_ref, ghosts_ref, tiles_ref, parts_ref, inverse_ref, start_ref, pick_ref, here_ref, sem
 ):
     move = pltpu.make_async_copy(tiles_ref, here_ref, sem)
     move.start()
@@ -219,26 +236,30 @@
     start_ref[rows : rows + TAIL, :] = jnp.where(tail_down == 0, squared * inverse_norm, inverse_norm)
     slots, per_row = columns_ref.shape
     blocks = (pick_ref.shape[0] - slots) // 3
-    codes = ghosts_ref[...].astype(F32)
-    if paired:
-        flipped = jnp.where(codes < blocks, codes + 2 * blocks, jnp.where(codes < 2 * blocks, codes, codes - 2 * blocks))
-        codes = jnp.where(lax.axis_index("sub") % 2 == 0, flipped, codes)
-    for slot in range(slots):
-        names = columns_ref[slot : slot + 1, :].astype(F32)
-        places = names + 3 * blocks
-        for ghost in range(codes.shape[1]):
-            places = jnp.where(names == slots + ghost, codes[:, ghost : ghost + 1], places)
-        column = jnp.sum(jnp.where(eye(per_row, per_row), places, 0.0), axis=1, keepdims=True)
-        column = jnp.broadcast_to(column, (per_row, width))
-        for place in range(pick_ref.shape[0]):
-            pick_ref[place, slot * per_row : (slot + 1) * per_row, :] = jnp.where(column == place, 1.0, 0.0)
+    places = [
+        part * blocks + peer * slots + slot
+        for part, peers in near_peers(blocks // slots, paired, doubling)
+        for peer in peers
+        for slot in range(slots)
+    ]
+    places += [3 * blocks + slot for slot in range(slots)]
+    for slot in range(slots):
+        names = columns_ref[slot : slot + 1, :]
+        wanted = names + 3 * blocks
+        for ghost in range(ghosts_ref.shape[1]):
+            wanted = jnp.where(names == slots + ghost, ghosts_ref[:, ghost : ghost + 1], wanted)
+        wanted = wanted.astype(F32)
+        column = jnp.sum(jnp.where(eye(per_row, per_row), wanted, 0.0), axis=1, keepdims=True)
+        column = jnp.broadcast_to(column, (per_row, width)).astype(jnp.int32)
+        for at, place in enumerate(places):
+            pick_ref[at, slot * per_row : (slot + 1) * per_row, :] = jnp.where(column == place, 1.0, 0.0)
     move.wait()
 
 
 def start_body(
     start_ref, own_ref, one_ref, group_ref, two_ref, tiles_ref, pick_ref, mask_ref, out_ref, tail_ref, own_tail_ref
 ):
-    slots, rows, width = own_ref.shape
+    _, rows, width = own_ref.shape
     blocks = group_ref.shape[0]
     coefficients = start_ref[0:rows, :] * start_ref[rows + 1 : rows + 2, :]
     empty = jnp.zeros((TAIL, width), F32)
@@ -270,25 +291,24 @@
 
 
 def step_body(
-    step, count, paired, every_ref, own_ref, one_ref, group_ref, two_ref, old_ref, old_own_ref, inverse_ref,
+    step, count, paired, doubling, every_ref, own_ref, one_ref, group_ref, two_ref, old_ref, old_own_ref, inverse_ref,
     tiles_ref, pick_ref, mask_ref, out_ref, tail_ref, own_tail_ref, history_ref,
 ):
     slots, rows, width = own_ref.shape
     subs = lax.axis_size("sub")
-    dom = lax.axis_index("dom")
-    toward = lax.axis_index("sub") % 2 * 2 - 1 if paired else 1
+    last_dom = lax.axis_size("dom") - 1
     total_row = tree_sum([every_ref[i, slots : slots + 1, :] for i in range(every_ref.shape[0])])
     projected, norm, inverse_norm, down = project(total_row, inverse_ref[...], rows, width)
     history_ref[...] = jnp.where(down == count, norm, projected)
     coefficients = jnp.where(down == rows + STEPS, inverse_norm, -(projected * inverse_norm))
     head, foot = coefficients[0:rows], coefficients[rows : rows + TAIL]
     vectors = []
-    for part, shift in ((one_ref, -toward), (group_ref, 0), (two_ref, toward)):
-        first = jnp.clip(dom + shift, 0, lax.axis_size("dom") - 1) * subs
+    for part, (offset, peers) in zip((one_ref, group_ref, two_ref), near_peers(subs, paired, doubling)):
+        first = jnp.clip(lax.axis_index("dom") + offset - 1, 0, last_dom) * subs
         for place in range(part.shape[0]):
             at = len(vectors)
             old = old_ref[at]
-            image = every_ref[first + place // slots, place % slots : place % slots + 1, :]
+            image = every_ref[first + peers[place // slots], place % slots : place % slots + 1, :]
             vector = jnp.sum(part[place] * head, axis=0, keepdims=True)
             vector = vector + jnp.sum(old * foot, axis=0, keepdims=True) + image * inverse_norm
             if tail_ref is not None:
@@ -304,8 +324,8 @@
     finish_step(vectors, tails, own_ref, tiles_ref, pick_ref, mask_ref, own_tail_ref, out_ref)
 
 
-def last_step_body(step, count, paired, *refs):
-    step_body(step, count, paired, *refs[:12], None, *refs[12:])
+def last_step_body(step, count, paired, doubling, *refs):
+    step_body(step, count, paired, doubling, *refs[:12], None, *refs[12:])
 
 
 def small_solve(matrix, target):
@@ -340,7 +360,6 @@
 def end_body(count, mask_ref, every_ref, own_ref, tail_ref, inverse_ref, start_ref, recycled_ref, *rest):
     histories, (solution_ref, residual_ref) = rest[:-2], rest[-2:]
     slots, rows, width = own_ref.shape
-    full = rows + TAIL
     total_row = tree_sum([every_ref[i] for i in range(every_ref.shape[0])])
     projected, norm, _, down = project(total_row, inverse_ref[...], rows, width)
     columns = [history[...] for history in histories]
@@ -393,16 +412,25 @@
     full = rows + TAIL
     per_row = tile_columns.shape[1]
     own, mask = call(
-        pack_body,
-        "pack",
-        [(slots, rows, width), (round_up(slots, 8), width)],
-        [SMEM, VMEM, VMEM],
+        pack_body, [(slots, rows, width), (round_up(slots, 8), width)], [SMEM, VMEM, VMEM]
     )(live_counts, load_vector, images)
-    group = lax.all_gather(own, "sub", axis=0, tiled=True)
     each = rows // lane_groups(count, rows, width)
-    (grams,) = call(functools.partial(gram_body, count), "gram", [(doms, each, width)], [VMEM])(group)
-    parts = lax.all_to_all(grams, "dom", 0, 0)
     paired = subs % 2 == 0
+    doubling = subs == 4
+    (grams,) = call(functools.partial(gram_body, count), [(devices, each, width)], [VMEM])(own)
+
+    def turn(value, bit):
+        return lax.ppermute(value, "sub", [(i, i ^ bit) for i in range(subs)])
+
+    if doubling:
+        inner = turn(own, 1)
+        outer = turn(own, 2)
+    parts = lax.all_to_all(grams, AXES, 0, 0)
+    if doubling:
+        corner = turn(outer, 1)
+        (group,) = call(join_body, [(subs * slots, rows, width)], [VMEM] * 4)(own, inner, outer, corner)
+    else:
+        group = lax.all_gather(own, "sub", axis=0, tiled=True)
     if paired:
         pairs = []
         for d in range(doms):
@@ -411,8 +439,6 @@
                 if 0 <= to < doms:
                     pairs.append((d * subs + s, to * subs + s))
         one = lax.ppermute(group, AXES, pairs)
-        one, parts = lax.optimization_barrier((one, parts))
-        two = lax.ppermute(one, "sub", [(i, i ^ 1) for i in range(subs)])
     else:
         up = [(i, i + 1) for i in range(doms - 1)]
         one = lax.ppermute(group, "dom", up)
@@ -420,17 +446,16 @@
     lines = round_up(slots + 1, 4)
     near = 3 * group.shape[0]
     inverse, start, pick, tiles = call(
-        functools.partial(factor_body, count, rows, paired),
-        "factor",
+        functools.partial(factor_body, count, rows, paired, doubling),
         [(full, width), (full, width), (near + slots, slots * per_row, width), matrix_tiles.shape],
         [VMEM, VMEM, HBM, VMEM],
         [pltpu.SemaphoreType.DMA],
     )(tile_columns, ghost_list, pltpu.with_memory_space_constraint(matrix_tiles, pltpu.HBM), parts)
+    if paired:
+        one, start = lax.optimization_barrier((one, start))
+        two = turn(one, 1)
     message, tails, own_tails = call(
-        start_body,
-        "start",
-        [(devices, lines, width), (near, TAIL, width), (slots, TAIL, width)],
-        [VMEM] * 8,
+        start_body, [(devices, lines, width), (near, TAIL, width), (slots, TAIL, width)], [VMEM] * 8
     )(start, own, one, group, two, tiles, pick, mask)
     histories = []
     for step in range(1, STEPS):
@@ -438,8 +463,7 @@
         last = step == STEPS - 1
         sent = 1 if last else lines
         results = call(
-            functools.partial(last_step_body if last else step_body, step, count, paired),
-            f"step{step}",
+            functools.partial(last_step_body if last else step_body, step, count, paired, doubling),
             [(devices, sent, width)]
             + ([] if last else [(near, TAIL, width)])
             + [(slots, TAIL, width), (full, width)],
@@ -451,10 +475,7 @@
     every = lax.all_to_all(message, AXES, 0, 0)
     return tuple(
         call(
-            functools.partial(end_body, count),
-            "end",
-            [(slots, width), (slots, width)],
-            [VMEM] * (7 + len(histories)),
+            functools.partial(end_body, count), [(slots, width), (slots, width)], [VMEM] * (7 + len(histories))
         )(mask, every, own, own_tails, inverse, start, recycled, *histories)
     )
 

time: 56.4 us -> 60.7 us (1.076)
  blocking collectives: 48.3 us -> 32.1 us
  starting transfers between devices: 1.28 us -> 11.4 us
  waiting for transfers between devices: 0.01 us -> 9.79 us
    all_to_all x1 -> x0, blocking collectives: 14 us -> none  [local(): parts = lax.all_to_all(grams, 'dom', 0, 0)]
    all_to_all x0 -> x1, starting transfers between devices: none -> 7.32 us  [local(): parts = lax.all_to_all(grams, AXES, 0, 0)]
    all_gather x1 -> x0, blocking collectives: 6.89 us -> none  [local(): group = lax.all_gather(own, 'sub', axis=0, tiled=True)]
    ppermute x1 -> x4, waiting for transfers between devices: 0.01 us -> 5.28 us  [turn(): return lax.ppermute(value, 'sub', [(i, i ^ bit) for i in range(subs)])]
    all_to_all x3, blocking collectives: 27.4 us -> 32.1 us  [local(): every = lax.all_to_all(message, AXES, 0, 0)]
    all_to_all x0 -> x1, waiting for transfers between devices: none -> 3.18 us  [local(): parts = lax.all_to_all(grams, AXES, 0, 0)]
    ppermute x1 -> x4, starting transfers between devices: 0.01 us -> 2.78 us  [turn(): return lax.ppermute(value, 'sub', [(i, i ^ bit) for i in range(subs)])]
    ppermute x1, waiting for transfers between devices: 0.01 us -> 1.33 us  [local(): one = lax.ppermute(group, AXES, pairs)]
  transfers between devices with their start and end apart: 2 -> 6, of which waited for: 0 -> 5; matrix products, arithmetic and copies ran while one was open for 0% -> 0% of each run, Pallas kernels for 4% -> 3%
where the time goes in v6:
time: 60.7 us; the launch traced here: 60.3 us
  blocking collectives  32.1 us (53%)
  starting transfers between devices  11.4 us (19%)
  waiting for transfers between devices  9.79 us (16%)
  Pallas kernels  4.85 us (8%)
  between operations  1.38 us (2%)
  local copies, waits for them, and re-layouts  0.8 us (1%)
    all_to_all x3, blocking collectives, local(): every = lax.all_to_all(message, AXES, 0, 0)  32.1 us
    all_to_all x1, starting transfers between devices, local(): parts = lax.all_to_all(grams, AXES, 0, 0)  7.32 us
    ppermute x4, waiting for transfers between devices, turn(): return lax.ppermute(value, 'sub', [(i, i ^ bit) for i in range(subs)])  5.28 us
    all_to_all x1, waiting for transfers between devices, local(): parts = lax.all_to_all(grams, AXES, 0, 0)  3.18 us
    ppermute x4, starting transfers between devices, turn(): return lax.ppermute(value, 'sub', [(i, i ^ bit) for i in range(subs)])  2.78 us
    pallas_call x1, Pallas kernels, local(): call(functools.partial(factor_body, count, rows, paired, doubling), [(ful...  1.79 us
    ppermute x1, waiting for transfers between devices, local(): one = lax.ppermute(group, AXES, pairs)  1.33 us
    ppermute x1, starting transfers between devices, local(): one = lax.ppermute(group, AXES, pairs)  1.29 us
  transfers between devices with their start and end apart: 6, of which 5 were waited for; matrix products, arithmetic and copies ran while one was open for 0% of the time, Pallas kernels for 3%

profile of v6, /device:TPU:0, one launch (start us, length us, event | category | flops | bytes accessed | tf_op | source)
XLA Modules:
  0.0 60.3 jit_solution(16913128228763292039)
XLA Ops:
  0.6 0.0 copy-start.2
  1.3 0.0 copy-done.2
  1.3 0.0 copy-start.1
  1.3 0.8 %copy-done.1 = f32[40,2,128]{2,1,0:T(2,128)S(1)} copy-done((f32[40,2,128]{2,1,0:T(2,128)S(1)}, f32[40,2,128]{2,1,0:T(2,128)}, u32[]{:S(2)}) %copy-start.1) | copy-done | bytes 40984
  2.1 1.0 %shard_map.88 = f32[32,16,128]{2,1,0:T(8,128)} custom-call(f32[2,48,128]{2,1,0:T(8,128)S(1)} %get-tuple-element.21.refs_0_.group_ref.own_ref.refs_1_), custom_call_target="tpu_custom_call" | custom-call | flops 10000000 | bytes 1048576 | tf_op jit(solution)/shard_map/pallas_call | solution.py:420
  3.1 7.3 %all-to-all-start = ((f32[32,16,128]{2,1,0:T(8,128)}), f32[32,16,128]{2,1,0:T(8,128)S(1)}, u32[]{:S(2)}, u32[]{:S(2)}) async-start(f32[32,16,128]{2,1,0:T(8,128)} %shard_map.88), calls=%async_computation | async-start | bytes 524288 | tf_op jit(solution)/shard_map/all_to_all | solution.py:428
  10.4 0.0 copy-start.3
  10.5 0.0 copy-start.4
  10.5 1.8 %collective-permute-start.1 = (f32[2,48,128]{2,1,0:T(8,128)S(1)}, f32[2,48,128]{2,1,0:T(8,128)S(1)}, u32[]{:S(2)}, u32[]{:S(2)}) collective-permute-start(f32[2,48,128]{2,1,0:T(8,128)S(1)} %get-tuple-element.21.refs_0_.group_ref.own_ref.refs_1_), channel_id=1, source_target_pairs={{0,2},{1,3},{2,0},{3,1},{4,6},{5,7},{6,4},{7,5},{8,10},{9,11},{10,... | collective-permute-start | bytes 147464 | tf_op jit(solution)/shard_map/ppermute | solution.py:423
  12.3 0.0 collective-permute-start
  12.3 3.0 %collective-permute-done.1.refs_2_ = f32[2,48,128]{2,1,0:T(8,128)S(1)} collective-permute-done((f32[2,48,128]{2,1,0:T(8,128)S(1)}, f32[2,48,128]{2,1,0:T(8,128)S(1)}, u32[]{:S(2)}, u32[]{:S(2)}) %collective-permute-start.1) | collective-permute-done | bytes 49184 | tf_op jit(solution)/shard_map/ppermute | solution.py:423
  15.3 0.0 collective-permute-start.2
  15.3 0.0 collective-permute-done.refs_1_
  15.3 1.2 %collective-permute-done.2.refs_3_ = f32[2,48,128]{2,1,0:T(8,128)S(1)} collective-permute-done((f32[2,48,128]{2,1,0:T(8,128)S(1)}, f32[2,48,128]{2,1,0:T(8,128)S(1)}, u32[]{:S(2)}, u32[]{:S(2)}) %collective-permute-start.2) | collective-permute-done | bytes 49184 | tf_op jit(solution)/shard_map/ppermute | solution.py:423
  16.5 1.3 %collective-permute-start.3 = (f32[8,48,128]{2,1,0:T(8,128)S(1)}, f32[8,48,128]{2,1,0:T(8,128)S(1)}, u32[]{:S(2)}, u32[]{:S(2)}) collective-permute-start(f32[8,48,128]{2,1,0:T(8,128)S(1)} %shard_map.87.group_ref.refs_3_), channel_id=1, source_target_pairs={{1,5},{3,7},{4,0},{5,9},{6,2},{7,11},{8,4},{9,13},{10,6},{11,15},{... | collective-permute-start | bytes 589832 | tf_op jit(solution)/shard_map/ppermute | solution.py:441
  17.8 3.2 %all-to-all-done.parts_ref = f32[32,16,128]{2,1,0:T(8,128)S(1)} async-done(((f32[32,16,128]{2,1,0:T(8,128)}), f32[32,16,128]{2,1,0:T(8,128)S(1)}, u32[]{:S(2)}, u32[]{:S(2)}) %all-to-all-start) | async-done | bytes 262176 | tf_op jit(solution)/shard_map/all_to_all | solution.py:428
  21.0 0.0 copy-done.3
  21.0 0.0 copy-done.4
  21.0 1.8 %shard_map.89 = (f32[56,128]{1,0:T(8,128)S(1)}, f32[56,128]{1,0:T(8,128)S(1)}, f32[26,16,128]{2,1,0:T(8,128)S(1)}, f32[2,8,128,128]{3,2,1,0:T(8,128)S(1)}) custom-call(s32[2,8]{1,0:T(2,128)S(1)} %copy-done.3, s32[1,4]{1,0:T(1,128)S(1)} %copy-done.4, f32[2,8,128,128]{3,2,1,0:T(8,128)} %tiles_ref.1, f32[32,16,128]{2,1,0:T(8,128)S(1)} %all-to-all-done.parts_ref), custom_call_target="tpu_custom_call" | custom-call | flops 10000000 | bytes 1048576 | tf_op jit(solution)/shard_map/pallas_call | solution.py:448
  22.8 1.3 %collective-permute-done.3.one_ref.refs_2_ = f32[8,48,128]{2,1,0:T(8,128)S(1)} collective-permute-done((f32[8,48,128]{2,1,0:T(8,128)S(1)}, f32[8,48,128]{2,1,0:T(8,128)S(1)}, u32[]{:S(2)}, u32[]{:S(2)}) %collective-permute-start.3) | collective-permute-done | bytes 196640 | tf_op jit(solution)/shard_map/ppermute | solution.py:441
  24.1 0.9 %collective-permute-start.4 = (f32[8,48,128]{2,1,0:T(8,128)S(1)}, f32[8,48,128]{2,1,0:T(8,128)S(1)}, u32[]{:S(2)}, u32[]{:S(2)}) collective-permute-start(f32[8,48,128]{2,1,0:T(8,128)S(1)} %collective-permute-done.3.one_ref.refs_2_), channel_id=1, source_target_pairs={{0,1},{1,0},{2,3},{3,2},{4,5},{5,4},{6,7},{7,6},{8,9},{9,8},{10,11... | collective-permute-start | bytes 589832 | tf_op jit(solution)/shard_map/ppermute | solution.py:423
  25.1 1.1 %collective-permute-done.4.two_ref.refs_4_ = f32[8,48,128]{2,1,0:T(8,128)S(1)} collective-permute-done((f32[8,48,128]{2,1,0:T(8,128)S(1)}, f32[8,48,128]{2,1,0:T(8,128)S(1)}, u32[]{:S(2)}, u32[]{:S(2)}) %collective-permute-start.4) | collective-permute-done | bytes 196640 | tf_op jit(solution)/shard_map/ppermute | solution.py:423
  26.2 0.3 shard_map.90
  26.5 14.1 %all_to_all.20.every_ref = f32[32,4,128]{2,1,0:T(4,128)S(1)} all-to-all(f32[32,4,128]{2,1,0:T(4,128)S(1)} %get-tuple-element.27), channel_id=1, replica_groups=mesh['dom'=8,'sub'=4] {'dom','sub'}, dimensions={0} | all-to-all | bytes 131072 | tf_op jit(solution)/shard_map/all_to_all | solution.py:462
  40.6 0.5 shard_map.91
  41.1 9.1 %all_to_all.21.refs_0_ = f32[32,4,128]{2,1,0:T(4,128)S(1)} all-to-all(f32[32,4,128]{2,1,0:T(4,128)S(1)} %get-tuple-element.31), channel_id=1, replica_groups=mesh['dom'=8,'sub'=4] {'dom','sub'}, dimensions={0} | all-to-all | bytes 131072 | tf_op jit(solution)/shard_map/all_to_all | solution.py:462
  50.2 0.0 copy-start
  50.2 0.5 shard_map.92
  50.7 8.9 %all_to_all.22.every_ref = f32[32,1,128]{2,1,0:T(1,128)S(1)} all-to-all(f32[32,1,128]{2,1,0:T(1,128)S(1)} %get-tuple-element.34), channel_id=1, replica_groups=mesh['dom'=8,'sub'=4] {'dom','sub'}, dimensions={0} | all-to-all | bytes 32768 | tf_op jit(solution)/shard_map/all_to_all | solution.py:475
  59.6 0.0 copy-done
  59.6 0.7 %shard_map.93 = (f32[2,128]{1,0:T(2,128)}, f32[2,128]{1,0:T(2,128)}) custom-call(f32[8,128]{1,0:T(8,128)S(1)} %get-tuple-element.20.mask_ref.refs_10_, f32[32,1,128]{2,1,0:T(1,128)S(1)} %all_to_all.22.every_ref, f32[2,48,128]{2,1,0:T(8,128)S(1)} %get-tuple-element.21.refs_0_.group_ref.own_ref.refs_1_, f32[2,8,128]{2,1,0:T(8,128)S(1)} %get-tuple-element.35.tail_ref, ...), custom_call_target="tpu_custom_call" | custom-call | flops 10000000 | bytes 1048576 | tf_op jit(solution)/shard_map/pallas_call | solution.py:477
  (2 shorter events, 0.0 us)
Async XLA Ops:
  0.6 0.7 %copy-start.2 = (f32[2,128]{1,0:T(2,128)S(1)}, f32[2,128]{1,0:T(2,128)}, u32[]{:S(2)}) copy-start(f32[2,128]{1,0:T(2,128)} %load_ref.1) | copy-start | bytes 3076
  1.3 0.8 %copy-start.1 = (f32[40,2,128]{2,1,0:T(2,128)S(1)}, f32[40,2,128]{2,1,0:T(2,128)}, u32[]{:S(2)}) copy-start(f32[40,2,128]{2,1,0:T(2,128)} %images_ref.1) | copy-start | bytes 122884
  3.1 17.9 %all-to-all-start = ((f32[32,16,128]{2,1,0:T(8,128)}), f32[32,16,128]{2,1,0:T(8,128)S(1)}, u32[]{:S(2)}, u32[]{:S(2)}) async-start(f32[32,16,128]{2,1,0:T(8,128)} %shard_map.88), calls=%async_computation | async-start | bytes 524288 | tf_op jit(solution)/shard_map/all_to_all | solution.py:428
  10.4 10.6 %copy-start.3 = (s32[2,8]{1,0:T(2,128)S(1)}, s32[2,8]{1,0:T(2,128)}, u32[]{:S(2)}) copy-start(s32[2,8]{1,0:T(2,128)} %columns_ref.1) | copy-start | bytes 196
  10.5 10.6 %copy-start.4 = (s32[1,4]{1,0:T(1,128)S(1)}, s32[1,4]{1,0:T(1,128)}, u32[]{:S(2)}) copy-start(s32[1,4]{1,0:T(1,128)} %ghosts_ref.1) | copy-start | bytes 52
  10.5 4.8 %collective-permute-start.1 = (f32[2,48,128]{2,1,0:T(8,128)S(1)}, f32[2,48,128]{2,1,0:T(8,128)S(1)}, u32[]{:S(2)}, u32[]{:S(2)}) collective-permute-start(f32[2,48,128]{2,1,0:T(8,128)S(1)} %get-tuple-element.21.refs_0_.group_ref.own_ref.refs_1_), channel_id=1, source_target_pairs={{0,2},{1,3},{2,0},{3,1},{4,6},{5,7},{6,4},{7,5},{8,10},{9,11},{10,... | collective-permute-start | bytes 147464 | tf_op jit(solution)/shard_map/ppermute | solution.py:423
  12.3 3.0 %collective-permute-start = (f32[2,48,128]{2,1,0:T(8,128)S(1)}, f32[2,48,128]{2,1,0:T(8,128)S(1)}, u32[]{:S(2)}, u32[]{:S(2)}) collective-permute-start(f32[2,48,128]{2,1,0:T(8,128)S(1)} %get-tuple-element.21.refs_0_.group_ref.own_ref.refs_1_), channel_id=1, source_target_pairs={{0,1},{1,0},{2,3},{3,2},{4,5},{5,4},{6,7},{7,6},{8,9},{9,8},{10,11... | collective-permute-start | bytes 147464 | tf_op jit(solution)/shard_map/ppermute | solution.py:423
  15.3 1.2 %collective-permute-start.2 = (f32[2,48,128]{2,1,0:T(8,128)S(1)}, f32[2,48,128]{2,1,0:T(8,128)S(1)}, u32[]{:S(2)}, u32[]{:S(2)}) collective-permute-start(f32[2,48,128]{2,1,0:T(8,128)S(1)} %collective-permute-done.1.refs_2_), channel_id=1, source_target_pairs={{0,1},{1,0},{2,3},{3,2},{4,5},{5,4},{6,7},{7,6},{8,9},{9,8},{10,11... | collective-permute-start | bytes 147464 | tf_op jit(solution)/shard_map/ppermute | solution.py:423
  16.5 7.6 %collective-permute-start.3 = (f32[8,48,128]{2,1,0:T(8,128)S(1)}, f32[8,48,128]{2,1,0:T(8,128)S(1)}, u32[]{:S(2)}, u32[]{:S(2)}) collective-permute-start(f32[8,48,128]{2,1,0:T(8,128)S(1)} %shard_map.87.group_ref.refs_3_), channel_id=1, source_target_pairs={{1,5},{3,7},{4,0},{5,9},{6,2},{7,11},{8,4},{9,13},{10,6},{11,15},{... | collective-permute-start | bytes 589832 | tf_op jit(solution)/shard_map/ppermute | solution.py:441
  24.1 2.0 %collective-permute-start.4 = (f32[8,48,128]{2,1,0:T(8,128)S(1)}, f32[8,48,128]{2,1,0:T(8,128)S(1)}, u32[]{:S(2)}, u32[]{:S(2)}) collective-permute-start(f32[8,48,128]{2,1,0:T(8,128)S(1)} %collective-permute-done.3.one_ref.refs_2_), channel_id=1, source_target_pairs={{0,1},{1,0},{2,3},{3,2},{4,5},{5,4},{6,7},{7,6},{8,9},{9,8},{10,11... | collective-permute-start | bytes 589832 | tf_op jit(solution)/shard_map/ppermute | solution.py:423
  50.2 9.4 %copy-start = (f32[40,2,128]{2,1,0:T(2,128)S(1)}, f32[40,2,128]{2,1,0:T(2,128)}, u32[]{:S(2)}) copy-start(f32[40,2,128]{2,1,0:T(2,128)} %recycled_ref.1) | copy-start | bytes 122884

commit v7 on v6

--- a/solution.py
+++ b/solution.py
@@ -6,7 +6,6 @@
 from jax.experimental import pallas as pl
 from jax.experimental.pallas import tpu as pltpu
 from jax.sharding import PartitionSpec as P
-
 
 STEPS = 3
 TAIL = 8
@@ -18,9 +17,10 @@
 F32 = jnp.float32
 
 
-def call(body, outs, specs, scratch=(), work=10_000_000):
+def call(body, name, outs, specs, scratch=(), work=10_000_000):
     return pl.pallas_call(
         body,
+        name=name,
         out_shape=[jax.ShapeDtypeStruct(shape, F32) for shape in outs],
         in_specs=specs,
         out_specs=[VMEM] * len(outs),
@@ -78,18 +78,30 @@
     return 1
 
 
-def gram_body(count, group_ref, out_ref):
-    blocks, rows, width = group_ref.shape
+def gram_of(*refs):
     products = []
-    for block in range(blocks):
-        part = group_ref[block]
-        products.append(
-            lax.dot_general(
-                part, part, (((1,), (1,)), ((), ())),
-                precision=lax.Precision.HIGHEST, preferred_element_type=F32,
+    for ref in refs:
+        for block in range(ref.shape[0]):
+            part = ref[block]
+            products.append(
+                lax.dot_general(
+                    part, part, (((1,), (1,)), ((), ())),
+                    precision=lax.Precision.HIGHEST, preferred_element_type=F32,
+                )
             )
-        )
-    gram = jnp.concatenate([tree_sum(products), jnp.zeros((rows, width - rows), F32)], axis=1)
+    rows, width = refs[0].shape[1:]
+    return jnp.concatenate([tree_sum(products), jnp.zeros((rows, width - rows), F32)], axis=1)
+
+
+def first_gram_body(*refs):
+    refs[-1][...] = gram_of(*refs[:-1])
+
+
+def gram_body(count, held_ref, group_ref, out_ref):
+    rows, width = group_ref.shape[1:]
+    gram = gram_of(group_ref)
+    if held_ref is not None:
+        gram = gram + held_ref[...]
     groups = lane_groups(count, rows, width)
     each, lanes = rows // groups, width // groups
     packed = gram[0:each]
@@ -99,8 +111,18 @@
         out_ref[copy] = packed
 
 
+def whole_gram_body(count, group_ref, out_ref):
+    gram_body(count, None, group_ref, out_ref)
+
+
 def multiply(left, right):
     return [[tree_sum([a * right[k][j] for k, a in enumerate(row)]) for j in range(len(right[0]))] for row in left]
+
+
+def symmetric(left, right):
+    size = len(left)
+    half = [[tree_sum([a * right[k][j] for k, a in enumerate(left[i])]) for j in range(i + 1)] for i in range(size)]
+    return [[half[max(i, j)][min(i, j)] for j in range(size)] for i in range(size)]
 
 
 def small_inverse(matrix):
@@ -112,11 +134,13 @@
     rest = [row[half:] for row in matrix[half:]]
     first = small_inverse([row[:half] for row in matrix[:half]])
     across = multiply(first, corner)
-    taken = multiply([list(row) for row in zip(*corner)], across)
-    second = small_inverse([[rest[i][j] - taken[i][j] for j in range(half)] for i in range(half)])
+    taken = symmetric([list(row) for row in zip(*corner)], across)
+    left = [[rest[i][j] - taken[i][j] for j in range(i + 1)] for i in range(half)]
+    second = small_inverse([[left[max(i, j)][min(i, j)] for j in range(half)] for i in range(half)])
     product = multiply(across, second)
-    added = multiply(product, [list(row) for row in zip(*across)])
-    top = [[first[i][j] + added[i][j] for j in range(half)] + [-value for value in product[i]] for i in range(half)]
+    added = symmetric(product, [list(row) for row in zip(*across)])
+    total = [[first[i][j] + added[i][j] for j in range(i + 1)] for i in range(half)]
+    top = [[total[max(i, j)][min(i, j)] for j in range(half)] + [-value for value in product[i]] for i in range(half)]
     bottom = [[-product[j][i] for j in range(half)] + second[i] for i in range(half)]
     return top + bottom
 
@@ -141,17 +165,16 @@
             for i in range(size)
         ]
         inverse = small_inverse(pivots)
-        scaled = []
-        for i in range(size):
-            line = tree_sum([lines[j] * inverse[i][j] for j in range(size)])
-            for j in range(size):
-                line = jnp.where(across == k + j, inverse[i][j], line)
-            scaled.append(line)
         inside = (across >= k) & (across < k + size)
+        lines = [jnp.where(inside, jnp.where(across == k + i, 1.0, 0.0), line) for i, line in enumerate(lines)]
+        scaled = [tree_sum([lines[j] * inverse[i][j] for j in range(size)]) for i in range(size)]
         updated = []
         for n, tile in enumerate(tiles):
-            value = jnp.where(inside, 0.0, tile)
-            value = value - tree_sum([columns[i][n] * scaled[i] for i in range(size)])
+            if n == at and size == 8:
+                value = scaled[0]
+            else:
+                value = jnp.where(inside, 0.0, tile)
+                value = value - tree_sum([columns[i][n] * scaled[i] for i in range(size)])
             if n == at:
                 for i in range(size):
                     value = jnp.where(down == inner + i, scaled[i], value)
@@ -259,7 +282,7 @@
 def start_body(
     start_ref, own_ref, one_ref, group_ref, two_ref, tiles_ref, pick_ref, mask_ref, out_ref, tail_ref, own_tail_ref
 ):
-    _, rows, width = own_ref.shape
+    slots, rows, width = own_ref.shape
     blocks = group_ref.shape[0]
     coefficients = start_ref[0:rows, :] * start_ref[rows + 1 : rows + 2, :]
     empty = jnp.zeros((TAIL, width), F32)
@@ -360,6 +383,7 @@
 def end_body(count, mask_ref, every_ref, own_ref, tail_ref, inverse_ref, start_ref, recycled_ref, *rest):
     histories, (solution_ref, residual_ref) = rest[:-2], rest[-2:]
     slots, rows, width = own_ref.shape
+    full = rows + TAIL
     total_row = tree_sum([every_ref[i] for i in range(every_ref.shape[0])])
     projected, norm, _, down = project(total_row, inverse_ref[...], rows, width)
     columns = [history[...] for history in histories]
@@ -412,25 +436,34 @@
     full = rows + TAIL
     per_row = tile_columns.shape[1]
     own, mask = call(
-        pack_body, [(slots, rows, width), (round_up(slots, 8), width)], [SMEM, VMEM, VMEM]
+        pack_body,
+        "pack",
+        [(slots, rows, width), (round_up(slots, 8), width)],
+        [SMEM, VMEM, VMEM],
     )(live_counts, load_vector, images)
     each = rows // lane_groups(count, rows, width)
     paired = subs % 2 == 0
     doubling = subs == 4
-    (grams,) = call(functools.partial(gram_body, count), [(devices, each, width)], [VMEM])(own)
 
     def turn(value, bit):
         return lax.ppermute(value, "sub", [(i, i ^ bit) for i in range(subs)])
 
     if doubling:
-        inner = turn(own, 1)
-        outer = turn(own, 2)
-    parts = lax.all_to_all(grams, AXES, 0, 0)
-    if doubling:
-        corner = turn(outer, 1)
-        (group,) = call(join_body, [(subs * slots, rows, width)], [VMEM] * 4)(own, inner, outer, corner)
+        with jax.named_scope("inner"):
+            inner = turn(own, 1)
+        with jax.named_scope("outer"):
+            outer = turn(own, 2)
+        with jax.named_scope("corner"):
+            corner = turn(outer, 1)
+        (held,) = call(first_gram_body, "first_gram", [(rows, width)], [VMEM] * 3)(own, inner, outer)
+        corner, held = lax.optimization_barrier((corner, held))
+        (group,) = call(join_body, "join", [(subs * slots, rows, width)], [VMEM] * 4)(own, inner, outer, corner)
+        (grams,) = call(functools.partial(gram_body, count), "gram", [(doms, each, width)], [VMEM] * 2)(held, corner)
     else:
         group = lax.all_gather(own, "sub", axis=0, tiled=True)
+        (grams,) = call(functools.partial(whole_gram_body, count), "gram", [(doms, each, width)], [VMEM])(group)
+    with jax.named_scope("collect"):
+        parts = lax.all_to_all(grams, "dom", 0, 0)
     if paired:
         pairs = []
         for d in range(doms):
@@ -438,7 +471,11 @@
                 to = d + 1 if s % 2 else d - 1
                 if 0 <= to < doms:
                     pairs.append((d * subs + s, to * subs + s))
-        one = lax.ppermute(group, AXES, pairs)
+        with jax.named_scope("pair"):
+            one = lax.ppermute(group, AXES, pairs)
+        one, parts = lax.optimization_barrier((one, parts))
+        with jax.named_scope("swap"):
+            two = turn(one, 1)
     else:
         up = [(i, i + 1) for i in range(doms - 1)]
         one = lax.ppermute(group, "dom", up)
@@ -447,15 +484,16 @@
     near = 3 * group.shape[0]
     inverse, start, pick, tiles = call(
         functools.partial(factor_body, count, rows, paired, doubling),
+        "factor",
         [(full, width), (full, width), (near + slots, slots * per_row, width), matrix_tiles.shape],
         [VMEM, VMEM, HBM, VMEM],
         [pltpu.SemaphoreType.DMA],
     )(tile_columns, ghost_list, pltpu.with_memory_space_constraint(matrix_tiles, pltpu.HBM), parts)
-    if paired:
-        one, start = lax.optimization_barrier((one, start))
-        two = turn(one, 1)
     message, tails, own_tails = call(
-        start_body, [(devices, lines, width), (near, TAIL, width), (slots, TAIL, width)], [VMEM] * 8
+        start_body,
+        "start",
+        [(devices, lines, width), (near, TAIL, width), (slots, TAIL, width)],
+        [VMEM] * 8,
     )(start, own, one, group, two, tiles, pick, mask)
     histories = []
     for step in range(1, STEPS):
@@ -464,6 +502,7 @@
         sent = 1 if last else lines
         results = call(
             functools.partial(last_step_body if last else step_body, step, count, paired, doubling),
+            f"step{step}",
             [(devices, sent, width)]
             + ([] if last else [(near, TAIL, width)])
             + [(slots, TAIL, width), (full, width)],
@@ -475,7 +514,10 @@
     every = lax.all_to_all(message, AXES, 0, 0)
     return tuple(
         call(
-            functools.partial(end_body, count), [(slots, width), (slots, width)], [VMEM] * (7 + len(histories))
+            functools.partial(end_body, count),
+            "end",
+            [(slots, width), (slots, width)],
+            [VMEM] * (7 + len(histories)),
         )(mask, every, own, own_tails, inverse, start, recycled, *histories)
     )
 

time: 60.7 us -> 55.9 us (0.921)
  blocking collectives: 32.1 us -> 41.7 us
  starting transfers between devices: 11.4 us -> 4.36 us
  waiting for transfers between devices: 9.79 us -> 2.95 us
    all_to_all x0 -> x1, blocking collectives: none -> 14.3 us  [local(): parts = lax.all_to_all(grams, 'dom', 0, 0)]
    all_to_all x1 -> x0, starting transfers between devices: 7.32 us -> none  [local(): parts = lax.all_to_all(grams, AXES, 0, 0)]
    all_to_all x3, blocking collectives: 32.1 us -> 27.4 us  [local(): every = lax.all_to_all(message, AXES, 0, 0)]
    all_to_all x1 -> x0, waiting for transfers between devices: 3.18 us -> none  [local(): parts = lax.all_to_all(grams, AXES, 0, 0)]
    ppermute x4, waiting for transfers between devices: 5.28 us -> 2.95 us  [turn(): return lax.ppermute(value, 'sub', [(i, i ^ bit) for i in range(subs)])]
    ppermute x1, waiting for transfers between devices: 1.33 us -> 0.01 us  [local(): one = lax.ppermute(group, AXES, pairs)]
    pallas_call x6 -> x7, Pallas kernels: 3.88 us -> 3.41 us  [the longest x1 1.69 us: local(): call(functools.partial(factor_body, count, rows, paired, doubling), 'fact...]
  transfers between devices with their start and end apart: 6 -> 5, of which waited for: 5 -> 2; matrix products, arithmetic and copies ran while one was open for 0% -> 0% of each run, Pallas kernels for 3% -> 4%
where the time goes in v7:
time: 55.9 us; the launch traced here: 55.6 us
  blocking collectives  41.7 us (75%)
  Pallas kernels  4.38 us (8%)
  starting transfers between devices  4.36 us (8%)
  waiting for transfers between devices  2.95 us (5%)
  between operations  1.39 us (2%)
  local copies, waits for them, and re-layouts  0.8 us (1%)
    all_to_all x3, blocking collectives, local(): every = lax.all_to_all(message, AXES, 0, 0)  27.4 us
    all_to_all x1, blocking collectives, local(): parts = lax.all_to_all(grams, 'dom', 0, 0)  14.3 us
    ppermute x4, starting transfers between devices, turn(): return lax.ppermute(value, 'sub', [(i, i ^ bit) for i in range(subs)])  3.07 us
    ppermute x4, waiting for transfers between devices, turn(): return lax.ppermute(value, 'sub', [(i, i ^ bit) for i in range(subs)])  2.95 us
    pallas_call x1, Pallas kernels, local(): call(functools.partial(factor_body, count, rows, paired, doubling), 'fact...  1.69 us
    ppermute x1, starting transfers between devices, local(): one = lax.ppermute(group, AXES, pairs)  1.29 us
  transfers between devices with their start and end apart: 5, of which 2 were waited for; matrix products, arithmetic and copies ran while one was open for 0% of the time, Pallas kernels for 4%

profile of v7, /device:TPU:0, one launch (start us, length us, event | category | flops | bytes accessed | tf_op | source)
XLA Modules:
  0.0 55.6 jit_solution(17391644222086607520)
XLA Ops:
  0.6 0.0 copy-start.3
  1.3 0.0 copy-done.3
  1.3 0.0 copy-start.1
  1.3 0.8 %copy-done.1 = f32[40,2,128]{2,1,0:T(2,128)S(1)} copy-done((f32[40,2,128]{2,1,0:T(2,128)S(1)}, f32[40,2,128]{2,1,0:T(2,128)}, u32[]{:S(2)}) %copy-start.1) | copy-done | bytes 40984
  2.1 3.1 %collective-permute-start.1 = (f32[2,48,128]{2,1,0:T(8,128)S(1)}, f32[2,48,128]{2,1,0:T(8,128)S(1)}, u32[]{:S(2)}, u32[]{:S(2)}) collective-permute-start(f32[2,48,128]{2,1,0:T(8,128)S(1)} %get-tuple-element.23.refs_0_.own_ref.refs_1_), channel_id=1, source_target_pairs={{0,2},{1,3},{2,0},{3,1},{4,6},{5,7},{6,4},{7,5},{8,10},{9,11},{10,... | collective-permute-start | bytes 147464 | tf_op jit(solution)/shard_map/outer/ppermute | solution.py:449
  5.2 0.0 collective-permute-start
  5.2 2.1 %collective-permute-done.1.refs_2_ = f32[2,48,128]{2,1,0:T(8,128)S(1)} collective-permute-done((f32[2,48,128]{2,1,0:T(8,128)S(1)}, f32[2,48,128]{2,1,0:T(8,128)S(1)}, u32[]{:S(2)}, u32[]{:S(2)}) %collective-permute-start.1) | collective-permute-done | bytes 49184 | tf_op jit(solution)/shard_map/outer/ppermute | solution.py:449
  7.3 0.0 collective-permute-start.2
  7.3 0.0 collective-permute-done.refs_1_
  7.3 0.3 first_gram.1.held_ref
  7.6 0.9 %collective-permute-done.2.refs_3_.group_ref = f32[2,48,128]{2,1,0:T(8,128)S(1)} collective-permute-done((f32[2,48,128]{2,1,0:T(8,128)S(1)}, f32[2,48,128]{2,1,0:T(8,128)S(1)}, u32[]{:S(2)}, u32[]{:S(2)}) %collective-permute-start.2) | collective-permute-done | bytes 49184 | tf_op jit(solution)/shard_map/corner/ppermute | solution.py:449
  8.5 1.3 %collective-permute-start.3 = (f32[8,48,128]{2,1,0:T(8,128)S(1)}, f32[8,48,128]{2,1,0:T(8,128)S(1)}, u32[]{:S(2)}, u32[]{:S(2)}) collective-permute-start(f32[8,48,128]{2,1,0:T(8,128)S(1)} %join.1.group_ref.refs_3_), channel_id=1, source_target_pairs={{1,5},{3,7},{4,0},{5,9},{6,2},{7,11},{8,4},{9,13},{10,6},{11,15},{... | collective-permute-start | bytes 589832 | tf_op jit(solution)/shard_map/pair/ppermute | solution.py:475
  9.8 0.3 gram.1
  10.1 0.0 copy-start.2
  10.1 0.0 copy-start.4
  10.1 14.3 %all_to_all.20.parts_ref = f32[8,16,128]{2,1,0:T(8,128)S(1)} all-to-all(f32[8,16,128]{2,1,0:T(8,128)S(1)} %gram.1), channel_id=1, replica_groups=mesh['dom'=8,'sub'=4] {'dom'}, dimensions={0} | all-to-all | bytes 131072 | tf_op jit(solution)/shard_map/collect/all_to_all | solution.py:466
  24.4 0.0 collective-permute-done.3.one_ref.refs_2_
  24.4 0.0 collective-permute-start.4
  24.4 0.0 copy-done.2
  24.4 0.0 copy-done.4
  24.4 1.7 %factor.1 = (f32[56,128]{1,0:T(8,128)S(1)}, f32[56,128]{1,0:T(8,128)S(1)}, f32[26,16,128]{2,1,0:T(8,128)S(1)}, f32[2,8,128,128]{3,2,1,0:T(8,128)S(1)}) custom-call(s32[2,8]{1,0:T(2,128)S(1)} %copy-done.2, s32[1,4]{1,0:T(1,128)S(1)} %copy-done.4, f32[2,8,128,128]{3,2,1,0:T(8,128)} %tiles_ref.1, f32[8,16,128]{2,1,0:T(8,128)S(1)} %all_to_all.20.parts_ref), custom_call_target="tpu_custom_call" | custom-call | flops 10000000 | bytes 1048576 | tf_op jit(solution)/shard_map/factor/pallas_call | solution.py:485
  26.1 0.0 collective-permute-done.4.two_ref.refs_4_
  26.1 0.3 start.1
  26.5 9.5 %all_to_all.21.every_ref = f32[32,4,128]{2,1,0:T(4,128)S(1)} all-to-all(f32[32,4,128]{2,1,0:T(4,128)S(1)} %get-tuple-element.31), channel_id=1, replica_groups=mesh['dom'=8,'sub'=4] {'dom','sub'}, dimensions={0} | all-to-all | bytes 131072 | tf_op jit(solution)/shard_map/all_to_all | solution.py:500
  35.9 0.5 step1.1
  36.4 9.1 %all_to_all.22.refs_0_ = f32[32,4,128]{2,1,0:T(4,128)S(1)} all-to-all(f32[32,4,128]{2,1,0:T(4,128)S(1)} %get-tuple-element.35), channel_id=1, replica_groups=mesh['dom'=8,'sub'=4] {'dom','sub'}, dimensions={0} | all-to-all | bytes 131072 | tf_op jit(solution)/shard_map/all_to_all | solution.py:500
  45.5 0.0 copy-start
  45.5 0.5 step2.1
  46.0 8.9 %all_to_all.23.every_ref = f32[32,1,128]{2,1,0:T(1,128)S(1)} all-to-all(f32[32,1,128]{2,1,0:T(1,128)S(1)} %get-tuple-element.38), channel_id=1, replica_groups=mesh['dom'=8,'sub'=4] {'dom','sub'}, dimensions={0} | all-to-all | bytes 32768 | tf_op jit(solution)/shard_map/all_to_all | solution.py:514
  54.9 0.0 copy-done
  54.9 0.7 %end.1 = (f32[2,128]{1,0:T(2,128)}, f32[2,128]{1,0:T(2,128)}) custom-call(f32[8,128]{1,0:T(8,128)S(1)} %get-tuple-element.22.mask_ref.refs_10_, f32[32,1,128]{2,1,0:T(1,128)S(1)} %all_to_all.23.every_ref, f32[2,48,128]{2,1,0:T(8,128)S(1)} %get-tuple-element.23.refs_0_.own_ref.refs_1_, f32[2,8,128]{2,1,0:T(8,128)S(1)} %get-tuple-element.39.tail_ref, ...), custom_call_target="tpu_custom_call" | custom-call | flops 10000000 | bytes 1048576 | tf_op jit(solution)/shard_map/end/pallas_call | solution.py:516
  (2 shorter events, 0.0 us)
Async XLA Ops:
  0.6 0.7 %copy-start.3 = (f32[2,128]{1,0:T(2,128)S(1)}, f32[2,128]{1,0:T(2,128)}, u32[]{:S(2)}) copy-start(f32[2,128]{1,0:T(2,128)} %load_ref.1) | copy-start | bytes 3076
  1.3 0.8 %copy-start.1 = (f32[40,2,128]{2,1,0:T(2,128)S(1)}, f32[40,2,128]{2,1,0:T(2,128)}, u32[]{:S(2)}) copy-start(f32[40,2,128]{2,1,0:T(2,128)} %images_ref.1) | copy-start | bytes 122884
  2.1 5.1 %collective-permute-start.1 = (f32[2,48,128]{2,1,0:T(8,128)S(1)}, f32[2,48,128]{2,1,0:T(8,128)S(1)}, u32[]{:S(2)}, u32[]{:S(2)}) collective-permute-start(f32[2,48,128]{2,1,0:T(8,128)S(1)} %get-tuple-element.23.refs_0_.own_ref.refs_1_), channel_id=1, source_target_pairs={{0,2},{1,3},{2,0},{3,1},{4,6},{5,7},{6,4},{7,5},{8,10},{9,11},{10,... | collective-permute-start | bytes 147464 | tf_op jit(solution)/shard_map/outer/ppermute | solution.py:449
  5.2 2.1 %collective-permute-start = (f32[2,48,128]{2,1,0:T(8,128)S(1)}, f32[2,48,128]{2,1,0:T(8,128)S(1)}, u32[]{:S(2)}, u32[]{:S(2)}) collective-permute-start(f32[2,48,128]{2,1,0:T(8,128)S(1)} %get-tuple-element.23.refs_0_.own_ref.refs_1_), channel_id=1, source_target_pairs={{0,1},{1,0},{2,3},{3,2},{4,5},{5,4},{6,7},{7,6},{8,9},{9,8},{10,11... | collective-permute-start | bytes 147464 | tf_op jit(solution)/shard_map/inner/ppermute | solution.py:449
  7.3 1.2 %collective-permute-start.2 = (f32[2,48,128]{2,1,0:T(8,128)S(1)}, f32[2,48,128]{2,1,0:T(8,128)S(1)}, u32[]{:S(2)}, u32[]{:S(2)}) collective-permute-start(f32[2,48,128]{2,1,0:T(8,128)S(1)} %collective-permute-done.1.refs_2_), channel_id=1, source_target_pairs={{0,1},{1,0},{2,3},{3,2},{4,5},{5,4},{6,7},{7,6},{8,9},{9,8},{10,11... | collective-permute-start | bytes 147464 | tf_op jit(solution)/shard_map/corner/ppermute | solution.py:449
  8.5 15.9 %collective-permute-start.3 = (f32[8,48,128]{2,1,0:T(8,128)S(1)}, f32[8,48,128]{2,1,0:T(8,128)S(1)}, u32[]{:S(2)}, u32[]{:S(2)}) collective-permute-start(f32[8,48,128]{2,1,0:T(8,128)S(1)} %join.1.group_ref.refs_3_), channel_id=1, source_target_pairs={{1,5},{3,7},{4,0},{5,9},{6,2},{7,11},{8,4},{9,13},{10,6},{11,15},{... | collective-permute-start | bytes 589832 | tf_op jit(solution)/shard_map/pair/ppermute | solution.py:475
  10.1 14.3 %copy-start.2 = (s32[2,8]{1,0:T(2,128)S(1)}, s32[2,8]{1,0:T(2,128)}, u32[]{:S(2)}) copy-start(s32[2,8]{1,0:T(2,128)} %columns_ref.1) | copy-start | bytes 196
  10.1 14.3 %copy-start.4 = (s32[1,4]{1,0:T(1,128)S(1)}, s32[1,4]{1,0:T(1,128)}, u32[]{:S(2)}) copy-start(s32[1,4]{1,0:T(1,128)} %ghosts_ref.1) | copy-start | bytes 52
  24.4 1.7 %collective-permute-start.4 = (f32[8,48,128]{2,1,0:T(8,128)S(1)}, f32[8,48,128]{2,1,0:T(8,128)S(1)}, u32[]{:S(2)}, u32[]{:S(2)}) collective-permute-start(f32[8,48,128]{2,1,0:T(8,128)S(1)} %collective-permute-done.3.one_ref.refs_2_), channel_id=1, source_target_pairs={{0,1},{1,0},{2,3},{3,2},{4,5},{5,4},{6,7},{7,6},{8,9},{9,8},{10,11... | collective-permute-start | bytes 589832 | tf_op jit(solution)/shard_map/swap/ppermute | solution.py:449
  45.5 9.4 %copy-start = (f32[40,2,128]{2,1,0:T(2,128)S(1)}, f32[40,2,128]{2,1,0:T(2,128)}, u32[]{:S(2)}) copy-start(f32[40,2,128]{2,1,0:T(2,128)} %recycled_ref.1) | copy-start | bytes 122884

commit v8 on v7

--- a/solution.py
+++ b/solution.py
@@ -222,7 +222,7 @@
 
 def near_peers(subs, paired, doubling):
     me = lax.axis_index("sub")
-    first = (1 - me % 2) * 2 if paired else 0
+    first = (me + lax.axis_index("dom") + 1) % 2 * 2 if paired else 0
     result = []
     for part, swapped in ((first, 0), (1, 0), (2 - first, 1 if paired else 0)):
         result.append((part, [(peer ^ swapped) ^ me if doubling else peer for peer in range(subs)]))
@@ -454,7 +454,7 @@
         with jax.named_scope("outer"):
             outer = turn(own, 2)
         with jax.named_scope("corner"):
-            corner = turn(outer, 1)
+            corner = turn(own, 3)
         (held,) = call(first_gram_body, "first_gram", [(rows, width)], [VMEM] * 3)(own, inner, outer)
         corner, held = lax.optimization_barrier((corner, held))
         (group,) = call(join_body, "join", [(subs * slots, rows, width)], [VMEM] * 4)(own, inner, outer, corner)
@@ -468,7 +468,7 @@
         pairs = []
         for d in range(doms):
             for s in range(subs):
-                to = d + 1 if s % 2 else d - 1
+                to = d + 1 if (s + d) % 2 == 0 else d - 1
                 if 0 <= to < doms:
                     pairs.append((d * subs + s, to * subs + s))
         with jax.named_scope("pair"):

time: 55.9 us -> 55.6 us (level)
  blocking collectives: 41.7 us -> 39 us
  starting transfers between devices: 4.36 us -> 6.66 us
    all_to_all x1, blocking collectives: 14.3 us -> 11.7 us  [local(): parts = lax.all_to_all(grams, 'dom', 0, 0)]
    ppermute x1, starting transfers between devices: 1.29 us -> 3.4 us  [local(): one = lax.ppermute(group, AXES, pairs)]
where the time goes in v8:
time: 55.6 us; the launch traced here: 55.2 us
  blocking collectives  39 us (70%)
  starting transfers between devices  6.66 us (12%)
  Pallas kernels  4.38 us (8%)
  waiting for transfers between devices  2.98 us (5%)
  between operations  1.39 us (2%)
  local copies, waits for them, and re-layouts  0.8 us (1%)
    all_to_all x3, blocking collectives, local(): every = lax.all_to_all(message, AXES, 0, 0)  27.3 us
    all_to_all x1, blocking collectives, local(): parts = lax.all_to_all(grams, 'dom', 0, 0)  11.7 us
    ppermute x1, starting transfers between devices, local(): one = lax.ppermute(group, AXES, pairs)  3.4 us
    ppermute x4, starting transfers between devices, turn(): return lax.ppermute(value, 'sub', [(i, i ^ bit) for i in range(subs)])  3.26 us
    ppermute x4, waiting for transfers between devices, turn(): return lax.ppermute(value, 'sub', [(i, i ^ bit) for i in range(subs)])  2.98 us
    pallas_call x1, Pallas kernels, local(): call(functools.partial(factor_body, count, rows, paired, doubling), 'fact...  1.69 us
  transfers between devices with their start and end apart: 5, of which 2 were waited for; matrix products, arithmetic and copies ran while one was open for 0% of the time, Pallas kernels for 4%

profile of v8, /device:TPU:0, one launch (start us, length us, event | category | flops | bytes accessed | tf_op | source)
XLA Modules:
  0.0 55.2 jit_solution(9269345214158694871)
XLA Ops:
  0.6 0.0 copy-start.3
  1.3 0.0 copy-done.3
  1.3 0.0 copy-start.1
  1.3 0.8 %copy-done.1 = f32[40,2,128]{2,1,0:T(2,128)S(1)} copy-done((f32[40,2,128]{2,1,0:T(2,128)S(1)}, f32[40,2,128]{2,1,0:T(2,128)}, u32[]{:S(2)}) %copy-start.1) | copy-done | bytes 40984
  2.1 3.1 %collective-permute-start.1 = (f32[2,48,128]{2,1,0:T(8,128)S(1)}, f32[2,48,128]{2,1,0:T(8,128)S(1)}, u32[]{:S(2)}, u32[]{:S(2)}) collective-permute-start(f32[2,48,128]{2,1,0:T(8,128)S(1)} %get-tuple-element.23.refs_0_.own_ref.refs_1_), channel_id=1, source_target_pairs={{0,2},{1,3},{2,0},{3,1},{4,6},{5,7},{6,4},{7,5},{8,10},{9,11},{10,... | collective-permute-start | bytes 147464 | tf_op jit(solution)/shard_map/outer/ppermute | solution.py:449
  5.2 0.0 collective-permute-start
  5.2 0.2 collective-permute-start.2
  5.4 1.9 %collective-permute-done.1.refs_2_ = f32[2,48,128]{2,1,0:T(8,128)S(1)} collective-permute-done((f32[2,48,128]{2,1,0:T(8,128)S(1)}, f32[2,48,128]{2,1,0:T(8,128)S(1)}, u32[]{:S(2)}, u32[]{:S(2)}) %collective-permute-start.1) | collective-permute-done | bytes 49184 | tf_op jit(solution)/shard_map/outer/ppermute | solution.py:449
  7.3 0.0 collective-permute-done.refs_1_
  7.3 0.3 first_gram.1.held_ref
  7.6 1.1 %collective-permute-done.2.refs_3_.group_ref = f32[2,48,128]{2,1,0:T(8,128)S(1)} collective-permute-done((f32[2,48,128]{2,1,0:T(8,128)S(1)}, f32[2,48,128]{2,1,0:T(8,128)S(1)}, u32[]{:S(2)}, u32[]{:S(2)}) %collective-permute-start.2) | collective-permute-done | bytes 49184 | tf_op jit(solution)/shard_map/corner/ppermute | solution.py:449
  8.7 3.4 %collective-permute-start.3 = (f32[8,48,128]{2,1,0:T(8,128)S(1)}, f32[8,48,128]{2,1,0:T(8,128)S(1)}, u32[]{:S(2)}, u32[]{:S(2)}) collective-permute-start(f32[8,48,128]{2,1,0:T(8,128)S(1)} %join.1.group_ref.refs_3_), channel_id=1, source_target_pairs={{0,4},{2,6},{4,0},{5,9},{6,2},{7,11},{8,12},{9,5},{10,14},{11,7},{... | collective-permute-start | bytes 589832 | tf_op jit(solution)/shard_map/pair/ppermute | solution.py:475
  12.1 0.3 gram.1
  12.4 0.0 copy-start.2
  12.4 0.0 copy-start.4
  12.4 11.7 %all_to_all.20.parts_ref = f32[8,16,128]{2,1,0:T(8,128)S(1)} all-to-all(f32[8,16,128]{2,1,0:T(8,128)S(1)} %gram.1), channel_id=1, replica_groups=mesh['dom'=8,'sub'=4] {'dom'}, dimensions={0} | all-to-all | bytes 131072 | tf_op jit(solution)/shard_map/collect/all_to_all | solution.py:466
  24.1 0.0 collective-permute-done.3.one_ref.refs_2_
  24.1 0.0 collective-permute-start.4
  24.1 0.0 copy-done.2
  24.1 0.0 copy-done.4
  24.2 1.7 %factor.1 = (f32[56,128]{1,0:T(8,128)S(1)}, f32[56,128]{1,0:T(8,128)S(1)}, f32[26,16,128]{2,1,0:T(8,128)S(1)}, f32[2,8,128,128]{3,2,1,0:T(8,128)S(1)}) custom-call(s32[2,8]{1,0:T(2,128)S(1)} %copy-done.2, s32[1,4]{1,0:T(1,128)S(1)} %copy-done.4, f32[2,8,128,128]{3,2,1,0:T(8,128)} %tiles_ref.1, f32[8,16,128]{2,1,0:T(8,128)S(1)} %all_to_all.20.parts_ref), custom_call_target="tpu_custom_call" | custom-call | flops 10000000 | bytes 1048576 | tf_op jit(solution)/shard_map/factor/pallas_call | solution.py:485
  25.8 0.0 collective-permute-done.4.two_ref.refs_4_
  25.9 0.3 start.1
  26.2 9.3 %all_to_all.21.every_ref = f32[32,4,128]{2,1,0:T(4,128)S(1)} all-to-all(f32[32,4,128]{2,1,0:T(4,128)S(1)} %get-tuple-element.31), channel_id=1, replica_groups=mesh['dom'=8,'sub'=4] {'dom','sub'}, dimensions={0} | all-to-all | bytes 131072 | tf_op jit(solution)/shard_map/all_to_all | solution.py:500
  35.5 0.5 step1.1
  36.0 9.1 %all_to_all.22.refs_0_ = f32[32,4,128]{2,1,0:T(4,128)S(1)} all-to-all(f32[32,4,128]{2,1,0:T(4,128)S(1)} %get-tuple-element.35), channel_id=1, replica_groups=mesh['dom'=8,'sub'=4] {'dom','sub'}, dimensions={0} | all-to-all | bytes 131072 | tf_op jit(solution)/shard_map/all_to_all | solution.py:500
  45.1 0.0 copy-start
  45.1 0.5 step2.1
  45.6 8.9 %all_to_all.23.every_ref = f32[32,1,128]{2,1,0:T(1,128)S(1)} all-to-all(f32[32,1,128]{2,1,0:T(1,128)S(1)} %get-tuple-element.38), channel_id=1, replica_groups=mesh['dom'=8,'sub'=4] {'dom','sub'}, dimensions={0} | all-to-all | bytes 32768 | tf_op jit(solution)/shard_map/all_to_all | solution.py:514
  54.5 0.0 copy-done
  54.5 0.7 %end.1 = (f32[2,128]{1,0:T(2,128)}, f32[2,128]{1,0:T(2,128)}) custom-call(f32[8,128]{1,0:T(8,128)S(1)} %get-tuple-element.22.mask_ref.refs_10_, f32[32,1,128]{2,1,0:T(1,128)S(1)} %all_to_all.23.every_ref, f32[2,48,128]{2,1,0:T(8,128)S(1)} %get-tuple-element.23.refs_0_.own_ref.refs_1_, f32[2,8,128]{2,1,0:T(8,128)S(1)} %get-tuple-element.39.tail_ref, ...), custom_call_target="tpu_custom_call" | custom-call | flops 10000000 | bytes 1048576 | tf_op jit(solution)/shard_map/end/pallas_call | solution.py:516
  (2 shorter events, 0.1 us)
Async XLA Ops:
  0.6 0.7 %copy-start.3 = (f32[2,128]{1,0:T(2,128)S(1)}, f32[2,128]{1,0:T(2,128)}, u32[]{:S(2)}) copy-start(f32[2,128]{1,0:T(2,128)} %load_ref.1) | copy-start | bytes 3076
  1.3 0.8 %copy-start.1 = (f32[40,2,128]{2,1,0:T(2,128)S(1)}, f32[40,2,128]{2,1,0:T(2,128)}, u32[]{:S(2)}) copy-start(f32[40,2,128]{2,1,0:T(2,128)} %images_ref.1) | copy-start | bytes 122884
  2.1 5.1 %collective-permute-start.1 = (f32[2,48,128]{2,1,0:T(8,128)S(1)}, f32[2,48,128]{2,1,0:T(8,128)S(1)}, u32[]{:S(2)}, u32[]{:S(2)}) collective-permute-start(f32[2,48,128]{2,1,0:T(8,128)S(1)} %get-tuple-element.23.refs_0_.own_ref.refs_1_), channel_id=1, source_target_pairs={{0,2},{1,3},{2,0},{3,1},{4,6},{5,7},{6,4},{7,5},{8,10},{9,11},{10,... | collective-permute-start | bytes 147464 | tf_op jit(solution)/shard_map/outer/ppermute | solution.py:449
  5.2 2.1 %collective-permute-start = (f32[2,48,128]{2,1,0:T(8,128)S(1)}, f32[2,48,128]{2,1,0:T(8,128)S(1)}, u32[]{:S(2)}, u32[]{:S(2)}) collective-permute-start(f32[2,48,128]{2,1,0:T(8,128)S(1)} %get-tuple-element.23.refs_0_.own_ref.refs_1_), channel_id=1, source_target_pairs={{0,1},{1,0},{2,3},{3,2},{4,5},{5,4},{6,7},{7,6},{8,9},{9,8},{10,11... | collective-permute-start | bytes 147464 | tf_op jit(solution)/shard_map/inner/ppermute | solution.py:449
  5.2 3.5 %collective-permute-start.2 = (f32[2,48,128]{2,1,0:T(8,128)S(1)}, f32[2,48,128]{2,1,0:T(8,128)S(1)}, u32[]{:S(2)}, u32[]{:S(2)}) collective-permute-start(f32[2,48,128]{2,1,0:T(8,128)S(1)} %get-tuple-element.23.refs_0_.own_ref.refs_1_), channel_id=1, source_target_pairs={{0,3},{1,2},{2,1},{3,0},{4,7},{5,6},{6,5},{7,4},{8,11},{9,10},{10,... | collective-permute-start | bytes 147464 | tf_op jit(solution)/shard_map/corner/ppermute | solution.py:449
  8.7 15.4 %collective-permute-start.3 = (f32[8,48,128]{2,1,0:T(8,128)S(1)}, f32[8,48,128]{2,1,0:T(8,128)S(1)}, u32[]{:S(2)}, u32[]{:S(2)}) collective-permute-start(f32[8,48,128]{2,1,0:T(8,128)S(1)} %join.1.group_ref.refs_3_), channel_id=1, source_target_pairs={{0,4},{2,6},{4,0},{5,9},{6,2},{7,11},{8,12},{9,5},{10,14},{11,7},{... | collective-permute-start | bytes 589832 | tf_op jit(solution)/shard_map/pair/ppermute | solution.py:475
  12.4 11.7 %copy-start.2 = (s32[2,8]{1,0:T(2,128)S(1)}, s32[2,8]{1,0:T(2,128)}, u32[]{:S(2)}) copy-start(s32[2,8]{1,0:T(2,128)} %columns_ref.1) | copy-start | bytes 196
  12.4 11.7 %copy-start.4 = (s32[1,4]{1,0:T(1,128)S(1)}, s32[1,4]{1,0:T(1,128)}, u32[]{:S(2)}) copy-start(s32[1,4]{1,0:T(1,128)} %ghosts_ref.1) | copy-start | bytes 52
  24.1 1.7 %collective-permute-start.4 = (f32[8,48,128]{2,1,0:T(8,128)S(1)}, f32[8,48,128]{2,1,0:T(8,128)S(1)}, u32[]{:S(2)}, u32[]{:S(2)}) collective-permute-start(f32[8,48,128]{2,1,0:T(8,128)S(1)} %collective-permute-done.3.one_ref.refs_2_), channel_id=1, source_target_pairs={{0,1},{1,0},{2,3},{3,2},{4,5},{5,4},{6,7},{7,6},{8,9},{9,8},{10,11... | collective-permute-start | bytes 589832 | tf_op jit(solution)/shard_map/swap/ppermute | solution.py:449
  45.1 9.4 %copy-start = (f32[40,2,128]{2,1,0:T(2,128)S(1)}, f32[40,2,128]{2,1,0:T(2,128)}, u32[]{:S(2)}) copy-start(f32[40,2,128]{2,1,0:T(2,128)} %recycled_ref.1) | copy-start | bytes 122884

commit v9 on v8

--- a/solution.py
+++ b/solution.py
@@ -97,9 +97,10 @@
     refs[-1][...] = gram_of(*refs[:-1])
 
 
-def gram_body(count, held_ref, group_ref, out_ref):
-    rows, width = group_ref.shape[1:]
-    gram = gram_of(group_ref)
+def gram_body(count, held_ref, *refs):
+    parts, out_ref = refs[:-1], refs[-1]
+    rows, width = parts[0].shape[1:]
+    gram = gram_of(*parts)
     if held_ref is not None:
         gram = gram + held_ref[...]
     groups = lane_groups(count, rows, width)
@@ -455,10 +456,12 @@
             outer = turn(own, 2)
         with jax.named_scope("corner"):
             corner = turn(own, 3)
-        (held,) = call(first_gram_body, "first_gram", [(rows, width)], [VMEM] * 3)(own, inner, outer)
-        corner, held = lax.optimization_barrier((corner, held))
+        (held,) = call(first_gram_body, "first_gram", [(rows, width)], [VMEM] * 2)(own, inner)
+        outer, corner, held = lax.optimization_barrier((outer, corner, held))
         (group,) = call(join_body, "join", [(subs * slots, rows, width)], [VMEM] * 4)(own, inner, outer, corner)
-        (grams,) = call(functools.partial(gram_body, count), "gram", [(doms, each, width)], [VMEM] * 2)(held, corner)
+        (grams,) = call(functools.partial(gram_body, count), "gram", [(doms, each, width)], [VMEM] * 3)(
+            held, outer, corner
+        )
     else:
         group = lax.all_gather(own, "sub", axis=0, tiled=True)
         (grams,) = call(functools.partial(whole_gram_body, count), "gram", [(doms, each, width)], [VMEM])(group)

time: 55.6 us -> 56.1 us (level)
  waiting for transfers between devices: 2.98 us -> 3.78 us
    ppermute x4, waiting for transfers between devices: 2.98 us -> 3.78 us  [turn(): return lax.ppermute(value, 'sub', [(i, i ^ bit) for i in range(subs)])]
where the time goes in v9:
time: 56.1 us; the launch traced here: 55.8 us
  blocking collectives  38.8 us (69%)
  starting transfers between devices  6.62 us (12%)
  Pallas kernels  4.38 us (8%)
  waiting for transfers between devices  3.78 us (7%)
  between operations  1.39 us (2%)
  local copies, waits for them, and re-layouts  0.8 us (1%)
    all_to_all x3, blocking collectives, local(): every = lax.all_to_all(message, AXES, 0, 0)  27.1 us
    all_to_all x1, blocking collectives, local(): parts = lax.all_to_all(grams, 'dom', 0, 0)  11.7 us
    ppermute x4, waiting for transfers between devices, turn(): return lax.ppermute(value, 'sub', [(i, i ^ bit) for i in range(subs)])  3.78 us
    ppermute x1, starting transfers between devices, local(): one = lax.ppermute(group, AXES, pairs)  3.4 us
    ppermute x4, starting transfers between devices, turn(): return lax.ppermute(value, 'sub', [(i, i ^ bit) for i in range(subs)])  3.22 us
    pallas_call x1, Pallas kernels, local(): call(functools.partial(factor_body, count, rows, paired, doubling), 'fact...  1.69 us
  transfers between devices with their start and end apart: 5, of which 2 were waited for; matrix products, arithmetic and copies ran while one was open for 0% of the time, Pallas kernels for 4%

profile of v9, /device:TPU:0, one launch (start us, length us, event | category | flops | bytes accessed | tf_op | source)
XLA Modules:
  0.0 55.8 jit_solution(11925257741763775357)
XLA Ops:
  0.6 0.0 copy-start.3
  1.3 0.0 copy-done.3
  1.3 0.0 copy-start.1
  1.3 0.8 %copy-done.1 = f32[40,2,128]{2,1,0:T(2,128)S(1)} copy-done((f32[40,2,128]{2,1,0:T(2,128)S(1)}, f32[40,2,128]{2,1,0:T(2,128)}, u32[]{:S(2)}) %copy-start.1) | copy-done | bytes 40984
  2.1 0.6 %collective-permute-start = (f32[2,48,128]{2,1,0:T(8,128)S(1)}, f32[2,48,128]{2,1,0:T(8,128)S(1)}, u32[]{:S(2)}, u32[]{:S(2)}) collective-permute-start(f32[2,48,128]{2,1,0:T(8,128)S(1)} %get-tuple-element.24.refs_0_.own_ref.refs_1_), channel_id=1, source_target_pairs={{0,1},{1,0},{2,3},{3,2},{4,5},{5,4},{6,7},{7,6},{8,9},{9,8},{10,11... | collective-permute-start | bytes 147464 | tf_op jit(solution)/shard_map/inner/ppermute | solution.py:450
  2.7 2.6 %collective-permute-start.2 = (f32[2,48,128]{2,1,0:T(8,128)S(1)}, f32[2,48,128]{2,1,0:T(8,128)S(1)}, u32[]{:S(2)}, u32[]{:S(2)}) collective-permute-start(f32[2,48,128]{2,1,0:T(8,128)S(1)} %get-tuple-element.24.refs_0_.own_ref.refs_1_), channel_id=1, source_target_pairs={{0,3},{1,2},{2,1},{3,0},{4,7},{5,6},{6,5},{7,4},{8,11},{9,10},{10,... | collective-permute-start | bytes 147464 | tf_op jit(solution)/shard_map/corner/ppermute | solution.py:450
  5.3 0.0 collective-permute-start.1
  5.3 0.0 collective-permute-done.refs_1_
  5.4 0.3 first_gram.1.held_ref
  5.6 1.7 %collective-permute-done.2.refs_3_.refs_1_ = f32[2,48,128]{2,1,0:T(8,128)S(1)} collective-permute-done((f32[2,48,128]{2,1,0:T(8,128)S(1)}, f32[2,48,128]{2,1,0:T(8,128)S(1)}, u32[]{:S(2)}, u32[]{:S(2)}) %collective-permute-start.2) | collective-permute-done | bytes 49184 | tf_op jit(solution)/shard_map/corner/ppermute | solution.py:450
  7.4 2.0 %collective-permute-done.1.refs_2_.refs_0_ = f32[2,48,128]{2,1,0:T(8,128)S(1)} collective-permute-done((f32[2,48,128]{2,1,0:T(8,128)S(1)}, f32[2,48,128]{2,1,0:T(8,128)S(1)}, u32[]{:S(2)}, u32[]{:S(2)}) %collective-permute-start.1) | collective-permute-done | bytes 49184 | tf_op jit(solution)/shard_map/outer/ppermute | solution.py:450
  9.4 3.4 %collective-permute-start.3 = (f32[8,48,128]{2,1,0:T(8,128)S(1)}, f32[8,48,128]{2,1,0:T(8,128)S(1)}, u32[]{:S(2)}, u32[]{:S(2)}) collective-permute-start(f32[8,48,128]{2,1,0:T(8,128)S(1)} %join.1.group_ref.refs_3_), channel_id=1, source_target_pairs={{0,4},{2,6},{4,0},{5,9},{6,2},{7,11},{8,12},{9,5},{10,14},{11,7},{... | collective-permute-start | bytes 589832 | tf_op jit(solution)/shard_map/pair/ppermute | solution.py:478
  12.8 0.3 gram.1
  13.2 0.0 copy-start.2
  13.2 0.0 copy-start.4
  13.2 11.7 %all_to_all.20.parts_ref = f32[8,16,128]{2,1,0:T(8,128)S(1)} all-to-all(f32[8,16,128]{2,1,0:T(8,128)S(1)} %gram.1), channel_id=1, replica_groups=mesh['dom'=8,'sub'=4] {'dom'}, dimensions={0} | all-to-all | bytes 131072 | tf_op jit(solution)/shard_map/collect/all_to_all | solution.py:469
  24.9 0.0 collective-permute-done.3.one_ref.refs_2_
  24.9 0.0 collective-permute-start.4
  24.9 0.0 copy-done.2
  24.9 0.0 copy-done.4
  24.9 1.7 %factor.1 = (f32[56,128]{1,0:T(8,128)S(1)}, f32[56,128]{1,0:T(8,128)S(1)}, f32[26,16,128]{2,1,0:T(8,128)S(1)}, f32[2,8,128,128]{3,2,1,0:T(8,128)S(1)}) custom-call(s32[2,8]{1,0:T(2,128)S(1)} %copy-done.2, s32[1,4]{1,0:T(1,128)S(1)} %copy-done.4, f32[2,8,128,128]{3,2,1,0:T(8,128)} %tiles_ref.1, f32[8,16,128]{2,1,0:T(8,128)S(1)} %all_to_all.20.parts_ref), custom_call_target="tpu_custom_call" | custom-call | flops 10000000 | bytes 1048576 | tf_op jit(solution)/shard_map/factor/pallas_call | solution.py:488
  26.6 0.0 collective-permute-done.4.two_ref.refs_4_
  26.6 0.3 start.1
  27.0 9.1 %all_to_all.21.every_ref = f32[32,4,128]{2,1,0:T(4,128)S(1)} all-to-all(f32[32,4,128]{2,1,0:T(4,128)S(1)} %get-tuple-element.33), channel_id=1, replica_groups=mesh['dom'=8,'sub'=4] {'dom','sub'}, dimensions={0} | all-to-all | bytes 131072 | tf_op jit(solution)/shard_map/all_to_all | solution.py:503
  36.1 0.5 step1.1
  36.6 9.1 %all_to_all.22.refs_0_ = f32[32,4,128]{2,1,0:T(4,128)S(1)} all-to-all(f32[32,4,128]{2,1,0:T(4,128)S(1)} %get-tuple-element.37), channel_id=1, replica_groups=mesh['dom'=8,'sub'=4] {'dom','sub'}, dimensions={0} | all-to-all | bytes 131072 | tf_op jit(solution)/shard_map/all_to_all | solution.py:503
  45.7 0.0 copy-start
  45.7 0.5 step2.1
  46.2 8.9 %all_to_all.23.every_ref = f32[32,1,128]{2,1,0:T(1,128)S(1)} all-to-all(f32[32,1,128]{2,1,0:T(1,128)S(1)} %get-tuple-element.40), channel_id=1, replica_groups=mesh['dom'=8,'sub'=4] {'dom','sub'}, dimensions={0} | all-to-all | bytes 32768 | tf_op jit(solution)/shard_map/all_to_all | solution.py:517
  55.0 0.0 copy-done
  55.0 0.7 %end.1 = (f32[2,128]{1,0:T(2,128)}, f32[2,128]{1,0:T(2,128)}) custom-call(f32[8,128]{1,0:T(8,128)S(1)} %get-tuple-element.23.mask_ref.refs_10_, f32[32,1,128]{2,1,0:T(1,128)S(1)} %all_to_all.23.every_ref, f32[2,48,128]{2,1,0:T(8,128)S(1)} %get-tuple-element.24.refs_0_.own_ref.refs_1_, f32[2,8,128]{2,1,0:T(8,128)S(1)} %get-tuple-element.41.tail_ref, ...), custom_call_target="tpu_custom_call" | custom-call | flops 10000000 | bytes 1048576 | tf_op jit(solution)/shard_map/end/pallas_call | solution.py:519
  (2 shorter events, 0.1 us)
Async XLA Ops:
  0.6 0.7 %copy-start.3 = (f32[2,128]{1,0:T(2,128)S(1)}, f32[2,128]{1,0:T(2,128)}, u32[]{:S(2)}) copy-start(f32[2,128]{1,0:T(2,128)} %load_ref.1) | copy-start | bytes 3076
  1.3 0.8 %copy-start.1 = (f32[40,2,128]{2,1,0:T(2,128)S(1)}, f32[40,2,128]{2,1,0:T(2,128)}, u32[]{:S(2)}) copy-start(f32[40,2,128]{2,1,0:T(2,128)} %images_ref.1) | copy-start | bytes 122884
  2.1 3.2 %collective-permute-start = (f32[2,48,128]{2,1,0:T(8,128)S(1)}, f32[2,48,128]{2,1,0:T(8,128)S(1)}, u32[]{:S(2)}, u32[]{:S(2)}) collective-permute-start(f32[2,48,128]{2,1,0:T(8,128)S(1)} %get-tuple-element.24.refs_0_.own_ref.refs_1_), channel_id=1, source_target_pairs={{0,1},{1,0},{2,3},{3,2},{4,5},{5,4},{6,7},{7,6},{8,9},{9,8},{10,11... | collective-permute-start | bytes 147464 | tf_op jit(solution)/shard_map/inner/ppermute | solution.py:450
  2.7 4.7 %collective-permute-start.2 = (f32[2,48,128]{2,1,0:T(8,128)S(1)}, f32[2,48,128]{2,1,0:T(8,128)S(1)}, u32[]{:S(2)}, u32[]{:S(2)}) collective-permute-start(f32[2,48,128]{2,1,0:T(8,128)S(1)} %get-tuple-element.24.refs_0_.own_ref.refs_1_), channel_id=1, source_target_pairs={{0,3},{1,2},{2,1},{3,0},{4,7},{5,6},{6,5},{7,4},{8,11},{9,10},{10,... | collective-permute-start | bytes 147464 | tf_op jit(solution)/shard_map/corner/ppermute | solution.py:450
  5.3 4.1 %collective-permute-start.1 = (f32[2,48,128]{2,1,0:T(8,128)S(1)}, f32[2,48,128]{2,1,0:T(8,128)S(1)}, u32[]{:S(2)}, u32[]{:S(2)}) collective-permute-start(f32[2,48,128]{2,1,0:T(8,128)S(1)} %get-tuple-element.24.refs_0_.own_ref.refs_1_), channel_id=1, source_target_pairs={{0,2},{1,3},{2,0},{3,1},{4,6},{5,7},{6,4},{7,5},{8,10},{9,11},{10,... | collective-permute-start | bytes 147464 | tf_op jit(solution)/shard_map/outer/ppermute | solution.py:450
  9.4 15.5 %collective-permute-start.3 = (f32[8,48,128]{2,1,0:T(8,128)S(1)}, f32[8,48,128]{2,1,0:T(8,128)S(1)}, u32[]{:S(2)}, u32[]{:S(2)}) collective-permute-start(f32[8,48,128]{2,1,0:T(8,128)S(1)} %join.1.group_ref.refs_3_), channel_id=1, source_target_pairs={{0,4},{2,6},{4,0},{5,9},{6,2},{7,11},{8,12},{9,5},{10,14},{11,7},{... | collective-permute-start | bytes 589832 | tf_op jit(solution)/shard_map/pair/ppermute | solution.py:478
  13.2 11.7 %copy-start.2 = (s32[2,8]{1,0:T(2,128)S(1)}, s32[2,8]{1,0:T(2,128)}, u32[]{:S(2)}) copy-start(s32[2,8]{1,0:T(2,128)} %columns_ref.1) | copy-start | bytes 196
  13.2 11.7 %copy-start.4 = (s32[1,4]{1,0:T(1,128)S(1)}, s32[1,4]{1,0:T(1,128)}, u32[]{:S(2)}) copy-start(s32[1,4]{1,0:T(1,128)} %ghosts_ref.1) | copy-start | bytes 52
  24.9 1.7 %collective-permute-start.4 = (f32[8,48,128]{2,1,0:T(8,128)S(1)}, f32[8,48,128]{2,1,0:T(8,128)S(1)}, u32[]{:S(2)}, u32[]{:S(2)}) collective-permute-start(f32[8,48,128]{2,1,0:T(8,128)S(1)} %collective-permute-done.3.one_ref.refs_2_), channel_id=1, source_target_pairs={{0,1},{1,0},{2,3},{3,2},{4,5},{5,4},{6,7},{7,6},{8,9},{9,8},{10,11... | collective-permute-start | bytes 589832 | tf_op jit(solution)/shard_map/swap/ppermute | solution.py:450
  45.7 9.4 %copy-start = (f32[40,2,128]{2,1,0:T(2,128)S(1)}, f32[40,2,128]{2,1,0:T(2,128)}, u32[]{:S(2)}) copy-start(f32[40,2,128]{2,1,0:T(2,128)} %recycled_ref.1) | copy-start | bytes 122884

commit v10 on v9

--- a/solution.py
+++ b/solution.py
@@ -6,6 +6,7 @@
 from jax.experimental import pallas as pl
 from jax.experimental.pallas import tpu as pltpu
 from jax.sharding import PartitionSpec as P
+
 
 STEPS = 3
 TAIL = 8
@@ -17,10 +18,9 @@
 F32 = jnp.float32
 
 
-def call(body, name, outs, specs, scratch=(), work=10_000_000):
+def call(body, outs, specs, scratch=(), work=10_000_000):
     return pl.pallas_call(
         body,
-        name=name,
         out_shape=[jax.ShapeDtypeStruct(shape, F32) for shape in outs],
         in_specs=specs,
         out_specs=[VMEM] * len(outs),
@@ -283,7 +283,7 @@
 def start_body(
     start_ref, own_ref, one_ref, group_ref, two_ref, tiles_ref, pick_ref, mask_ref, out_ref, tail_ref, own_tail_ref
 ):
-    slots, rows, width = own_ref.shape
+    _, rows, width = own_ref.shape
     blocks = group_ref.shape[0]
     coefficients = start_ref[0:rows, :] * start_ref[rows + 1 : rows + 2, :]
     empty = jnp.zeros((TAIL, width), F32)
@@ -384,7 +384,6 @@
 def end_body(count, mask_ref, every_ref, own_ref, tail_ref, inverse_ref, start_ref, recycled_ref, *rest):
     histories, (solution_ref, residual_ref) = rest[:-2], rest[-2:]
     slots, rows, width = own_ref.shape
-    full = rows + TAIL
     total_row = tree_sum([every_ref[i] for i in range(every_ref.shape[0])])
     projected, norm, _, down = project(total_row, inverse_ref[...], rows, width)
     columns = [history[...] for history in histories]
@@ -437,10 +436,7 @@
     full = rows + TAIL
     per_row = tile_columns.shape[1]
     own, mask = call(
-        pack_body,
-        "pack",
-        [(slots, rows, width), (round_up(slots, 8), width)],
-        [SMEM, VMEM, VMEM],
+        pack_body, [(slots, rows, width), (round_up(slots, 8), width)], [SMEM, VMEM, VMEM]
     )(live_counts, load_vector, images)
     each = rows // lane_groups(count, rows, width)
     paired = subs % 2 == 0
@@ -450,23 +446,17 @@
         return lax.ppermute(value, "sub", [(i, i ^ bit) for i in range(subs)])
 
     if doubling:
-        with jax.named_scope("inner"):
-            inner = turn(own, 1)
-        with jax.named_scope("outer"):
-            outer = turn(own, 2)
-        with jax.named_scope("corner"):
-            corner = turn(own, 3)
-        (held,) = call(first_gram_body, "first_gram", [(rows, width)], [VMEM] * 2)(own, inner)
+        inner = turn(own, 1)
+        outer = turn(own, 2)
+        corner = turn(own, 3)
+        (held,) = call(first_gram_body, [(rows, width)], [VMEM] * 2)(own, inner)
         outer, corner, held = lax.optimization_barrier((outer, corner, held))
-        (group,) = call(join_body, "join", [(subs * slots, rows, width)], [VMEM] * 4)(own, inner, outer, corner)
-        (grams,) = call(functools.partial(gram_body, count), "gram", [(doms, each, width)], [VMEM] * 3)(
-            held, outer, corner
-        )
+        (group,) = call(join_body, [(subs * slots, rows, width)], [VMEM] * 4)(own, inner, outer, corner)
+        (grams,) = call(functools.partial(gram_body, count), [(doms, each, width)], [VMEM] * 3)(held, outer, corner)
     else:
         group = lax.all_gather(own, "sub", axis=0, tiled=True)
-        (grams,) = call(functools.partial(whole_gram_body, count), "gram", [(doms, each, width)], [VMEM])(group)
-    with jax.named_scope("collect"):
-        parts = lax.all_to_all(grams, "dom", 0, 0)
+        (grams,) = call(functools.partial(whole_gram_body, count), [(doms, each, width)], [VMEM])(group)
+    parts = lax.all_to_all(grams, "dom", 0, 0)
     if paired:
         pairs = []
         for d in range(doms):
@@ -474,11 +464,9 @@
                 to = d + 1 if (s + d) % 2 == 0 else d - 1
                 if 0 <= to < doms:
                     pairs.append((d * subs + s, to * subs + s))
-        with jax.named_scope("pair"):
-            one = lax.ppermute(group, AXES, pairs)
+        one = lax.ppermute(group, AXES, pairs)
         one, parts = lax.optimization_barrier((one, parts))
-        with jax.named_scope("swap"):
-            two = turn(one, 1)
+        two = turn(one, 1)
     else:
         up = [(i, i + 1) for i in range(doms - 1)]
         one = lax.ppermute(group, "dom", up)
@@ -487,16 +475,12 @@
     near = 3 * group.shape[0]
     inverse, start, pick, tiles = call(
         functools.partial(factor_body, count, rows, paired, doubling),
-        "factor",
         [(full, width), (full, width), (near + slots, slots * per_row, width), matrix_tiles.shape],
         [VMEM, VMEM, HBM, VMEM],
         [pltpu.SemaphoreType.DMA],
     )(tile_columns, ghost_list, pltpu.with_memory_space_constraint(matrix_tiles, pltpu.HBM), parts)
     message, tails, own_tails = call(
-        start_body,
-        "start",
-        [(devices, lines, width), (near, TAIL, width), (slots, TAIL, width)],
-        [VMEM] * 8,
+        start_body, [(devices, lines, width), (near, TAIL, width), (slots, TAIL, width)], [VMEM] * 8
     )(start, own, one, group, two, tiles, pick, mask)
     histories = []
     for step in range(1, STEPS):
@@ -505,7 +489,6 @@
         sent = 1 if last else lines
         results = call(
             functools.partial(last_step_body if last else step_body, step, count, paired, doubling),
-            f"step{step}",
             [(devices, sent, width)]
             + ([] if last else [(near, TAIL, width)])
             + [(slots, TAIL, width), (full, width)],
@@ -517,10 +500,7 @@
     every = lax.all_to_all(message, AXES, 0, 0)
     return tuple(
         call(
-            functools.partial(end_body, count),
-            "end",
-            [(slots, width), (slots, width)],
-            [VMEM] * (7 + len(histories)),
+            functools.partial(end_body, count), [(slots, width), (slots, width)], [VMEM] * (7 + len(histories))
         )(mask, every, own, own_tails, inverse, start, recycled, *histories)
     )
 

time: 56.1 us -> 56.1 us (level)
  no operation moved by 1% of the time
where the time goes in v10:
time: 56.1 us; the launch traced here: 55.8 us
  blocking collectives  38.8 us (69%)
  starting transfers between devices  6.62 us (12%)
  Pallas kernels  4.38 us (8%)
  waiting for transfers between devices  3.78 us (7%)
  between operations  1.39 us (2%)
  local copies, waits for them, and re-layouts  0.8 us (1%)
    all_to_all x3, blocking collectives, local(): every = lax.all_to_all(message, AXES, 0, 0)  27.1 us
    all_to_all x1, blocking collectives, local(): parts = lax.all_to_all(grams, 'dom', 0, 0)  11.7 us
    ppermute x4, waiting for transfers between devices, turn(): return lax.ppermute(value, 'sub', [(i, i ^ bit) for i in range(subs)])  3.78 us
    ppermute x1, starting transfers between devices, local(): one = lax.ppermute(group, AXES, pairs)  3.4 us
    ppermute x4, starting transfers between devices, turn(): return lax.ppermute(value, 'sub', [(i, i ^ bit) for i in range(subs)])  3.22 us
    pallas_call x1, Pallas kernels, local(): call(functools.partial(factor_body, count, rows, paired, doubling), [(ful...  1.69 us
  transfers between devices with their start and end apart: 5, of which 2 were waited for; matrix products, arithmetic and copies ran while one was open for 0% of the time, Pallas kernels for 4%

profile of v10, /device:TPU:0, one launch (start us, length us, event | category | flops | bytes accessed | tf_op | source)
XLA Modules:
  0.0 55.8 jit_solution(11925257741763775357)
XLA Ops:
  0.6 0.0 copy-start.3
  1.3 0.0 copy-done.3
  1.3 0.0 copy-start.1
  1.3 0.8 %copy-done.1 = f32[40,2,128]{2,1,0:T(2,128)S(1)} copy-done((f32[40,2,128]{2,1,0:T(2,128)S(1)}, f32[40,2,128]{2,1,0:T(2,128)}, u32[]{:S(2)}) %copy-start.1) | copy-done | bytes 40984
  2.1 0.6 %collective-permute-start = (f32[2,48,128]{2,1,0:T(8,128)S(1)}, f32[2,48,128]{2,1,0:T(8,128)S(1)}, u32[]{:S(2)}, u32[]{:S(2)}) collective-permute-start(f32[2,48,128]{2,1,0:T(8,128)S(1)} %get-tuple-element.24.refs_0_.own_ref.refs_1_), channel_id=1, source_target_pairs={{0,1},{1,0},{2,3},{3,2},{4,5},{5,4},{6,7},{7,6},{8,9},{9,8},{10,11... | collective-permute-start | bytes 147464 | tf_op jit(solution)/shard_map/ppermute | solution.py:446
  2.7 2.6 %collective-permute-start.2 = (f32[2,48,128]{2,1,0:T(8,128)S(1)}, f32[2,48,128]{2,1,0:T(8,128)S(1)}, u32[]{:S(2)}, u32[]{:S(2)}) collective-permute-start(f32[2,48,128]{2,1,0:T(8,128)S(1)} %get-tuple-element.24.refs_0_.own_ref.refs_1_), channel_id=1, source_target_pairs={{0,3},{1,2},{2,1},{3,0},{4,7},{5,6},{6,5},{7,4},{8,11},{9,10},{10,... | collective-permute-start | bytes 147464 | tf_op jit(solution)/shard_map/ppermute | solution.py:446
  5.3 0.0 collective-permute-start.1
  5.3 0.0 collective-permute-done.refs_1_
  5.4 0.3 shard_map.87.held_ref
  5.6 1.7 %collective-permute-done.2.refs_3_.refs_1_ = f32[2,48,128]{2,1,0:T(8,128)S(1)} collective-permute-done((f32[2,48,128]{2,1,0:T(8,128)S(1)}, f32[2,48,128]{2,1,0:T(8,128)S(1)}, u32[]{:S(2)}, u32[]{:S(2)}) %collective-permute-start.2) | collective-permute-done | bytes 49184 | tf_op jit(solution)/shard_map/ppermute | solution.py:446
  7.4 2.0 %collective-permute-done.1.refs_2_.refs_0_ = f32[2,48,128]{2,1,0:T(8,128)S(1)} collective-permute-done((f32[2,48,128]{2,1,0:T(8,128)S(1)}, f32[2,48,128]{2,1,0:T(8,128)S(1)}, u32[]{:S(2)}, u32[]{:S(2)}) %collective-permute-start.1) | collective-permute-done | bytes 49184 | tf_op jit(solution)/shard_map/ppermute | solution.py:446
  9.4 3.4 %collective-permute-start.3 = (f32[8,48,128]{2,1,0:T(8,128)S(1)}, f32[8,48,128]{2,1,0:T(8,128)S(1)}, u32[]{:S(2)}, u32[]{:S(2)}) collective-permute-start(f32[8,48,128]{2,1,0:T(8,128)S(1)} %shard_map.88.group_ref.refs_3_), channel_id=1, source_target_pairs={{0,4},{2,6},{4,0},{5,9},{6,2},{7,11},{8,12},{9,5},{10,14},{11,7},{... | collective-permute-start | bytes 589832 | tf_op jit(solution)/shard_map/ppermute | solution.py:467
  12.8 0.3 shard_map.89
  13.2 0.0 copy-start.2
  13.2 0.0 copy-start.4
  13.2 11.7 %all_to_all.20.parts_ref = f32[8,16,128]{2,1,0:T(8,128)S(1)} all-to-all(f32[8,16,128]{2,1,0:T(8,128)S(1)} %shard_map.89), channel_id=1, replica_groups=mesh['dom'=8,'sub'=4] {'dom'}, dimensions={0} | all-to-all | bytes 131072 | tf_op jit(solution)/shard_map/all_to_all | solution.py:459
  24.9 0.0 collective-permute-done.3.one_ref.refs_2_
  24.9 0.0 collective-permute-start.4
  24.9 0.0 copy-done.2
  24.9 0.0 copy-done.4
  24.9 1.7 %shard_map.90 = (f32[56,128]{1,0:T(8,128)S(1)}, f32[56,128]{1,0:T(8,128)S(1)}, f32[26,16,128]{2,1,0:T(8,128)S(1)}, f32[2,8,128,128]{3,2,1,0:T(8,128)S(1)}) custom-call(s32[2,8]{1,0:T(2,128)S(1)} %copy-done.2, s32[1,4]{1,0:T(1,128)S(1)} %copy-done.4, f32[2,8,128,128]{3,2,1,0:T(8,128)} %tiles_ref.1, f32[8,16,128]{2,1,0:T(8,128)S(1)} %all_to_all.20.parts_ref), custom_call_target="tpu_custom_call" | custom-call | flops 10000000 | bytes 1048576 | tf_op jit(solution)/shard_map/pallas_call | solution.py:476
  26.6 0.0 collective-permute-done.4.two_ref.refs_4_
  26.6 0.3 shard_map.91
  27.0 9.1 %all_to_all.21.every_ref = f32[32,4,128]{2,1,0:T(4,128)S(1)} all-to-all(f32[32,4,128]{2,1,0:T(4,128)S(1)} %get-tuple-element.33), channel_id=1, replica_groups=mesh['dom'=8,'sub'=4] {'dom','sub'}, dimensions={0} | all-to-all | bytes 131072 | tf_op jit(solution)/shard_map/all_to_all | solution.py:487
  36.1 0.5 shard_map.92
  36.6 9.1 %all_to_all.22.refs_0_ = f32[32,4,128]{2,1,0:T(4,128)S(1)} all-to-all(f32[32,4,128]{2,1,0:T(4,128)S(1)} %get-tuple-element.37), channel_id=1, replica_groups=mesh['dom'=8,'sub'=4] {'dom','sub'}, dimensions={0} | all-to-all | bytes 131072 | tf_op jit(solution)/shard_map/all_to_all | solution.py:487
  45.7 0.0 copy-start
  45.7 0.5 shard_map.93
  46.2 8.9 %all_to_all.23.every_ref = f32[32,1,128]{2,1,0:T(1,128)S(1)} all-to-all(f32[32,1,128]{2,1,0:T(1,128)S(1)} %get-tuple-element.40), channel_id=1, replica_groups=mesh['dom'=8,'sub'=4] {'dom','sub'}, dimensions={0} | all-to-all | bytes 32768 | tf_op jit(solution)/shard_map/all_to_all | solution.py:500
  55.0 0.0 copy-done
  55.0 0.7 %shard_map.94 = (f32[2,128]{1,0:T(2,128)}, f32[2,128]{1,0:T(2,128)}) custom-call(f32[8,128]{1,0:T(8,128)S(1)} %get-tuple-element.23.mask_ref.refs_10_, f32[32,1,128]{2,1,0:T(1,128)S(1)} %all_to_all.23.every_ref, f32[2,48,128]{2,1,0:T(8,128)S(1)} %get-tuple-element.24.refs_0_.own_ref.refs_1_, f32[2,8,128]{2,1,0:T(8,128)S(1)} %get-tuple-element.41.tail_ref, ...), custom_call_target="tpu_custom_call" | custom-call | flops 10000000 | bytes 1048576 | tf_op jit(solution)/shard_map/pallas_call | solution.py:502
  (2 shorter events, 0.1 us)
Async XLA Ops:
  0.6 0.7 %copy-start.3 = (f32[2,128]{1,0:T(2,128)S(1)}, f32[2,128]{1,0:T(2,128)}, u32[]{:S(2)}) copy-start(f32[2,128]{1,0:T(2,128)} %load_ref.1) | copy-start | bytes 3076
  1.3 0.8 %copy-start.1 = (f32[40,2,128]{2,1,0:T(2,128)S(1)}, f32[40,2,128]{2,1,0:T(2,128)}, u32[]{:S(2)}) copy-start(f32[40,2,128]{2,1,0:T(2,128)} %images_ref.1) | copy-start | bytes 122884
  2.1 3.2 %collective-permute-start = (f32[2,48,128]{2,1,0:T(8,128)S(1)}, f32[2,48,128]{2,1,0:T(8,128)S(1)}, u32[]{:S(2)}, u32[]{:S(2)}) collective-permute-start(f32[2,48,128]{2,1,0:T(8,128)S(1)} %get-tuple-element.24.refs_0_.own_ref.refs_1_), channel_id=1, source_target_pairs={{0,1},{1,0},{2,3},{3,2},{4,5},{5,4},{6,7},{7,6},{8,9},{9,8},{10,11... | collective-permute-start | bytes 147464 | tf_op jit(solution)/shard_map/ppermute | solution.py:446
  2.7 4.7 %collective-permute-start.2 = (f32[2,48,128]{2,1,0:T(8,128)S(1)}, f32[2,48,128]{2,1,0:T(8,128)S(1)}, u32[]{:S(2)}, u32[]{:S(2)}) collective-permute-start(f32[2,48,128]{2,1,0:T(8,128)S(1)} %get-tuple-element.24.refs_0_.own_ref.refs_1_), channel_id=1, source_target_pairs={{0,3},{1,2},{2,1},{3,0},{4,7},{5,6},{6,5},{7,4},{8,11},{9,10},{10,... | collective-permute-start | bytes 147464 | tf_op jit(solution)/shard_map/ppermute | solution.py:446
  5.3 4.1 %collective-permute-start.1 = (f32[2,48,128]{2,1,0:T(8,128)S(1)}, f32[2,48,128]{2,1,0:T(8,128)S(1)}, u32[]{:S(2)}, u32[]{:S(2)}) collective-permute-start(f32[2,48,128]{2,1,0:T(8,128)S(1)} %get-tuple-element.24.refs_0_.own_ref.refs_1_), channel_id=1, source_target_pairs={{0,2},{1,3},{2,0},{3,1},{4,6},{5,7},{6,4},{7,5},{8,10},{9,11},{10,... | collective-permute-start | bytes 147464 | tf_op jit(solution)/shard_map/ppermute | solution.py:446
  9.4 15.5 %collective-permute-start.3 = (f32[8,48,128]{2,1,0:T(8,128)S(1)}, f32[8,48,128]{2,1,0:T(8,128)S(1)}, u32[]{:S(2)}, u32[]{:S(2)}) collective-permute-start(f32[8,48,128]{2,1,0:T(8,128)S(1)} %shard_map.88.group_ref.refs_3_), channel_id=1, source_target_pairs={{0,4},{2,6},{4,0},{5,9},{6,2},{7,11},{8,12},{9,5},{10,14},{11,7},{... | collective-permute-start | bytes 589832 | tf_op jit(solution)/shard_map/ppermute | solution.py:467
  13.2 11.7 %copy-start.2 = (s32[2,8]{1,0:T(2,128)S(1)}, s32[2,8]{1,0:T(2,128)}, u32[]{:S(2)}) copy-start(s32[2,8]{1,0:T(2,128)} %columns_ref.1) | copy-start | bytes 196
  13.2 11.7 %copy-start.4 = (s32[1,4]{1,0:T(1,128)S(1)}, s32[1,4]{1,0:T(1,128)}, u32[]{:S(2)}) copy-start(s32[1,4]{1,0:T(1,128)} %ghosts_ref.1) | copy-start | bytes 52
  24.9 1.7 %collective-permute-start.4 = (f32[8,48,128]{2,1,0:T(8,128)S(1)}, f32[8,48,128]{2,1,0:T(8,128)S(1)}, u32[]{:S(2)}, u32[]{:S(2)}) collective-permute-start(f32[8,48,128]{2,1,0:T(8,128)S(1)} %collective-permute-done.3.one_ref.refs_2_), channel_id=1, source_target_pairs={{0,1},{1,0},{2,3},{3,2},{4,5},{5,4},{6,7},{7,6},{8,9},{9,8},{10,11... | collective-permute-start | bytes 589832 | tf_op jit(solution)/shard_map/ppermute | solution.py:446
  45.7 9.4 %copy-start = (f32[40,2,128]{2,1,0:T(2,128)S(1)}, f32[40,2,128]{2,1,0:T(2,128)}, u32[]{:S(2)}) copy-start(f32[40,2,128]{2,1,0:T(2,128)} %recycled_ref.1) | copy-start | bytes 122884

commit v11 on v10

--- a/solution.py
+++ b/solution.py
@@ -230,11 +230,7 @@
     return result
 
 
-def factor_body(
-    count, rows, paired, doubling, columns_ref, ghosts_ref, tiles_ref, parts_ref, inverse_ref, start_ref, pick_ref, here_ref, sem
-):
-    move = pltpu.make_async_copy(tiles_ref, here_ref, sem)
-    move.start()
+def sweep_parts(count, rows, parts_ref, inverse_ref, start_ref):
     width = parts_ref.shape[2]
     groups = lane_groups(count, rows, width)
     lanes = width // groups
@@ -258,6 +254,36 @@
     start = jnp.where(down < count, -swept[:, count : count + 1], jnp.where(down == count, 1.0, 0.0))
     start_ref[0:rows, :] = start
     start_ref[rows : rows + TAIL, :] = jnp.where(tail_down == 0, squared * inverse_norm, inverse_norm)
+
+
+def odd_core():
+    return lax.axis_index("sub") % 2 == 1
+
+
+def early_body(count, rows, columns_ref, ghosts_ref, parts_ref, inverse_ref, start_ref):
+    @pl.when(odd_core())
+    def _():
+        sweep_parts(count, rows, parts_ref, inverse_ref, start_ref)
+
+
+def factor_body(
+    count, rows, paired, doubling, columns_ref, ghosts_ref, tiles_ref, parts_ref, *refs,
+):
+    early_refs, (inverse_ref, start_ref, pick_ref, here_ref, sem) = refs[:-5], refs[-5:]
+    move = pltpu.make_async_copy(tiles_ref, here_ref, sem)
+    move.start()
+    width = parts_ref.shape[2]
+    if early_refs:
+        @pl.when(odd_core())
+        def _():
+            inverse_ref[...] = early_refs[0][...]
+            start_ref[...] = early_refs[1][...]
+
+        @pl.when(jnp.logical_not(odd_core()))
+        def _():
+            sweep_parts(count, rows, parts_ref, inverse_ref, start_ref)
+    else:
+        sweep_parts(count, rows, parts_ref, inverse_ref, start_ref)
     slots, per_row = columns_ref.shape
     blocks = (pick_ref.shape[0] - slots) // 3
     places = [
@@ -465,20 +491,24 @@
                 if 0 <= to < doms:
                     pairs.append((d * subs + s, to * subs + s))
         one = lax.ppermute(group, AXES, pairs)
-        one, parts = lax.optimization_barrier((one, parts))
+        early = call(functools.partial(early_body, count, rows), [(full, width)] * 2, [VMEM] * 3)(
+            tile_columns, ghost_list, parts
+        )
+        one, parts, early = lax.optimization_barrier((one, parts, early))
         two = turn(one, 1)
     else:
         up = [(i, i + 1) for i in range(doms - 1)]
         one = lax.ppermute(group, "dom", up)
         two = lax.ppermute(group, "dom", [(j, i) for i, j in up])
+        early = []
     lines = round_up(slots + 1, 4)
     near = 3 * group.shape[0]
     inverse, start, pick, tiles = call(
         functools.partial(factor_body, count, rows, paired, doubling),
         [(full, width), (full, width), (near + slots, slots * per_row, width), matrix_tiles.shape],
-        [VMEM, VMEM, HBM, VMEM],
+        [VMEM, VMEM, HBM, VMEM] + [VMEM] * len(early),
         [pltpu.SemaphoreType.DMA],
-    )(tile_columns, ghost_list, pltpu.with_memory_space_constraint(matrix_tiles, pltpu.HBM), parts)
+    )(tile_columns, ghost_list, pltpu.with_memory_space_constraint(matrix_tiles, pltpu.HBM), parts, *early)
     message, tails, own_tails = call(
         start_body, [(devices, lines, width), (near, TAIL, width), (slots, TAIL, width)], [VMEM] * 8
     )(start, own, one, group, two, tiles, pick, mask)

time: 56.1 us -> 56.5 us (level)
  transfers between devices with their start and end apart: 5 -> 5, of which waited for: 2 -> 2; matrix products, arithmetic and copies ran while one was open for 0% -> 0% of each run, Pallas kernels for 4% -> 5%
where the time goes in v11:
time: 56.5 us; the launch traced here: 56.1 us
  blocking collectives  38.8 us (69%)
  starting transfers between devices  6.69 us (12%)
  Pallas kernels  4.67 us (8%)
  waiting for transfers between devices  3.78 us (7%)
  between operations  1.39 us (2%)
  local copies, waits for them, and re-layouts  0.8 us (1%)
    all_to_all x3, blocking collectives, local(): every = lax.all_to_all(message, AXES, 0, 0)  27.1 us
    all_to_all x1, blocking collectives, local(): parts = lax.all_to_all(grams, 'dom', 0, 0)  11.7 us
    ppermute x4, waiting for transfers between devices, turn(): return lax.ppermute(value, 'sub', [(i, i ^ bit) for i in range(subs)])  3.78 us
    ppermute x1, starting transfers between devices, local(): one = lax.ppermute(group, AXES, pairs)  3.4 us
    ppermute x4, starting transfers between devices, turn(): return lax.ppermute(value, 'sub', [(i, i ^ bit) for i in range(subs)])  3.29 us
    pallas_call x1, Pallas kernels, local(): call(functools.partial(factor_body, count, rows, paired, doubling), [(ful...  1.98 us
  transfers between devices with their start and end apart: 5, of which 2 were waited for; matrix products, arithmetic and copies ran while one was open for 0% of the time, Pallas kernels for 5%

profile of v11, /device:TPU:0, one launch (start us, length us, event | category | flops | bytes accessed | tf_op | source)
XLA Modules:
  0.0 56.1 jit_solution(3819967951584233755)
XLA Ops:
  0.6 0.0 copy-start.4
  1.3 0.0 copy-done.4
  1.3 0.0 copy-start.1
  1.3 0.8 %copy-done.1 = f32[40,2,128]{2,1,0:T(2,128)S(1)} copy-done((f32[40,2,128]{2,1,0:T(2,128)S(1)}, f32[40,2,128]{2,1,0:T(2,128)}, u32[]{:S(2)}) %copy-start.1) | copy-done | bytes 40984
  2.1 0.6 collective-permute-start
  2.7 2.6 %collective-permute-start.2 = (f32[2,48,128]{2,1,0:T(8,128)S(1)}, f32[2,48,128]{2,1,0:T(8,128)S(1)}, u32[]{:S(2)}, u32[]{:S(2)}) collective-permute-start(f32[2,48,128]{2,1,0:T(8,128)S(1)} %get-tuple-element.28.refs_0_.own_ref.refs_1_), channel_id=1, source_target_pairs={{0,3},{1,2},{2,1},{3,0},{4,7},{5,6},{6,5},{7,4},{8,11},{9,10},{10,... | collective-permute-start | bytes 147464 | tf_op jit(solution)/shard_map/ppermute | solution.py:472
  5.3 0.0 collective-permute-start.1
  5.3 0.0 collective-permute-done.refs_1_
  5.4 0.3 shard_map.87.held_ref
  5.6 1.7 %collective-permute-done.2.refs_3_.refs_1_ = f32[2,48,128]{2,1,0:T(8,128)S(1)} collective-permute-done((f32[2,48,128]{2,1,0:T(8,128)S(1)}, f32[2,48,128]{2,1,0:T(8,128)S(1)}, u32[]{:S(2)}, u32[]{:S(2)}) %collective-permute-start.2) | collective-permute-done | bytes 49184 | tf_op jit(solution)/shard_map/ppermute | solution.py:472
  7.4 2.0 %collective-permute-done.1.refs_2_.refs_0_ = f32[2,48,128]{2,1,0:T(8,128)S(1)} collective-permute-done((f32[2,48,128]{2,1,0:T(8,128)S(1)}, f32[2,48,128]{2,1,0:T(8,128)S(1)}, u32[]{:S(2)}, u32[]{:S(2)}) %collective-permute-start.1) | collective-permute-done | bytes 49184 | tf_op jit(solution)/shard_map/ppermute | solution.py:472
  9.4 3.4 %collective-permute-start.3 = (f32[8,48,128]{2,1,0:T(8,128)S(1)}, f32[8,48,128]{2,1,0:T(8,128)S(1)}, u32[]{:S(2)}, u32[]{:S(2)}) collective-permute-start(f32[8,48,128]{2,1,0:T(8,128)S(1)} %shard_map.88.group_ref.refs_3_), channel_id=1, source_target_pairs={{0,4},{2,6},{4,0},{5,9},{6,2},{7,11},{8,12},{9,5},{10,14},{11,7},{... | collective-permute-start | bytes 589832 | tf_op jit(solution)/shard_map/ppermute | solution.py:493
  12.8 0.3 shard_map.89
  13.2 0.0 copy-start.2
  13.2 0.0 copy-start.3
  13.2 11.7 %all_to_all.20.parts_ref = f32[8,16,128]{2,1,0:T(8,128)S(1)} all-to-all(f32[8,16,128]{2,1,0:T(8,128)S(1)} %shard_map.89), channel_id=1, replica_groups=mesh['dom'=8,'sub'=4] {'dom'}, dimensions={0} | all-to-all | bytes 131072 | tf_op jit(solution)/shard_map/all_to_all | solution.py:485
  24.9 0.0 copy-done.2
  24.9 0.0 copy-done.3
  24.9 0.0 collective-permute-done.3.one_ref.refs_2_
  24.9 0.1 collective-permute-start.4
  25.0 2.0 %shard_map.91 = (f32[56,128]{1,0:T(8,128)S(1)}, f32[56,128]{1,0:T(8,128)S(1)}, f32[26,16,128]{2,1,0:T(8,128)S(1)}, f32[2,8,128,128]{3,2,1,0:T(8,128)S(1)}) custom-call(s32[2,8]{1,0:T(2,128)S(1)} %copy-done.2, s32[1,4]{1,0:T(1,128)S(1)} %copy-done.3, f32[2,8,128,128]{3,2,1,0:T(8,128)} %tiles_ref.1, f32[8,16,128]{2,1,0:T(8,128)S(1)} %all_to_all.20.parts_ref, ...), custom_call_target="tpu_custom_call" | custom-call | flops 10000000 | bytes 1048576 | tf_op jit(solution)/shard_map/pallas_call | solution.py:506
  27.0 0.0 collective-permute-done.4.two_ref.refs_4_
  27.0 0.3 shard_map.92
  27.3 9.1 %all_to_all.21.every_ref = f32[32,4,128]{2,1,0:T(4,128)S(1)} all-to-all(f32[32,4,128]{2,1,0:T(4,128)S(1)} %get-tuple-element.41), channel_id=1, replica_groups=mesh['dom'=8,'sub'=4] {'dom','sub'}, dimensions={0} | all-to-all | bytes 131072 | tf_op jit(solution)/shard_map/all_to_all | solution.py:517
  36.4 0.5 shard_map.93
  36.9 9.1 %all_to_all.22.refs_0_ = f32[32,4,128]{2,1,0:T(4,128)S(1)} all-to-all(f32[32,4,128]{2,1,0:T(4,128)S(1)} %get-tuple-element.45), channel_id=1, replica_groups=mesh['dom'=8,'sub'=4] {'dom','sub'}, dimensions={0} | all-to-all | bytes 131072 | tf_op jit(solution)/shard_map/all_to_all | solution.py:517
  46.0 0.0 copy-start
  46.0 0.5 shard_map.94
  46.5 8.9 %all_to_all.23.every_ref = f32[32,1,128]{2,1,0:T(1,128)S(1)} all-to-all(f32[32,1,128]{2,1,0:T(1,128)S(1)} %get-tuple-element.48), channel_id=1, replica_groups=mesh['dom'=8,'sub'=4] {'dom','sub'}, dimensions={0} | all-to-all | bytes 32768 | tf_op jit(solution)/shard_map/all_to_all | solution.py:530
  55.4 0.0 copy-done
  55.4 0.7 %shard_map.95 = (f32[2,128]{1,0:T(2,128)}, f32[2,128]{1,0:T(2,128)}) custom-call(f32[8,128]{1,0:T(8,128)S(1)} %get-tuple-element.27.mask_ref.refs_10_, f32[32,1,128]{2,1,0:T(1,128)S(1)} %all_to_all.23.every_ref, f32[2,48,128]{2,1,0:T(8,128)S(1)} %get-tuple-element.28.refs_0_.own_ref.refs_1_, f32[2,8,128]{2,1,0:T(8,128)S(1)} %get-tuple-element.49.tail_ref, ...), custom_call_target="tpu_custom_call" | custom-call | flops 10000000 | bytes 1048576 | tf_op jit(solution)/shard_map/pallas_call | solution.py:532
  (3 shorter events, 0.1 us)
Async XLA Ops:
  0.6 0.7 %copy-start.4 = (f32[2,128]{1,0:T(2,128)S(1)}, f32[2,128]{1,0:T(2,128)}, u32[]{:S(2)}) copy-start(f32[2,128]{1,0:T(2,128)} %load_ref.1) | copy-start | bytes 3076
  1.3 0.8 %copy-start.1 = (f32[40,2,128]{2,1,0:T(2,128)S(1)}, f32[40,2,128]{2,1,0:T(2,128)}, u32[]{:S(2)}) copy-start(f32[40,2,128]{2,1,0:T(2,128)} %images_ref.1) | copy-start | bytes 122884
  2.1 3.2 %collective-permute-start = (f32[2,48,128]{2,1,0:T(8,128)S(1)}, f32[2,48,128]{2,1,0:T(8,128)S(1)}, u32[]{:S(2)}, u32[]{:S(2)}) collective-permute-start(f32[2,48,128]{2,1,0:T(8,128)S(1)} %get-tuple-element.28.refs_0_.own_ref.refs_1_), channel_id=1, source_target_pairs={{0,1},{1,0},{2,3},{3,2},{4,5},{5,4},{6,7},{7,6},{8,9},{9,8},{10,11... | collective-permute-start | bytes 147464 | tf_op jit(solution)/shard_map/ppermute | solution.py:472
  2.7 4.7 %collective-permute-start.2 = (f32[2,48,128]{2,1,0:T(8,128)S(1)}, f32[2,48,128]{2,1,0:T(8,128)S(1)}, u32[]{:S(2)}, u32[]{:S(2)}) collective-permute-start(f32[2,48,128]{2,1,0:T(8,128)S(1)} %get-tuple-element.28.refs_0_.own_ref.refs_1_), channel_id=1, source_target_pairs={{0,3},{1,2},{2,1},{3,0},{4,7},{5,6},{6,5},{7,4},{8,11},{9,10},{10,... | collective-permute-start | bytes 147464 | tf_op jit(solution)/shard_map/ppermute | solution.py:472
  5.3 4.1 %collective-permute-start.1 = (f32[2,48,128]{2,1,0:T(8,128)S(1)}, f32[2,48,128]{2,1,0:T(8,128)S(1)}, u32[]{:S(2)}, u32[]{:S(2)}) collective-permute-start(f32[2,48,128]{2,1,0:T(8,128)S(1)} %get-tuple-element.28.refs_0_.own_ref.refs_1_), channel_id=1, source_target_pairs={{0,2},{1,3},{2,0},{3,1},{4,6},{5,7},{6,4},{7,5},{8,10},{9,11},{10,... | collective-permute-start | bytes 147464 | tf_op jit(solution)/shard_map/ppermute | solution.py:472
  9.4 15.5 %collective-permute-start.3 = (f32[8,48,128]{2,1,0:T(8,128)S(1)}, f32[8,48,128]{2,1,0:T(8,128)S(1)}, u32[]{:S(2)}, u32[]{:S(2)}) collective-permute-start(f32[8,48,128]{2,1,0:T(8,128)S(1)} %shard_map.88.group_ref.refs_3_), channel_id=1, source_target_pairs={{0,4},{2,6},{4,0},{5,9},{6,2},{7,11},{8,12},{9,5},{10,14},{11,7},{... | collective-permute-start | bytes 589832 | tf_op jit(solution)/shard_map/ppermute | solution.py:493
  13.2 11.7 %copy-start.2 = (s32[2,8]{1,0:T(2,128)S(1)}, s32[2,8]{1,0:T(2,128)}, u32[]{:S(2)}) copy-start(s32[2,8]{1,0:T(2,128)} %columns_ref.3) | copy-start | bytes 196
  13.2 11.7 %copy-start.3 = (s32[1,4]{1,0:T(1,128)S(1)}, s32[1,4]{1,0:T(1,128)}, u32[]{:S(2)}) copy-start(s32[1,4]{1,0:T(1,128)} %ghosts_ref.3) | copy-start | bytes 52
  24.9 2.1 %collective-permute-start.4 = (f32[8,48,128]{2,1,0:T(8,128)S(1)}, f32[8,48,128]{2,1,0:T(8,128)S(1)}, u32[]{:S(2)}, u32[]{:S(2)}) collective-permute-start(f32[8,48,128]{2,1,0:T(8,128)S(1)} %collective-permute-done.3.one_ref.refs_2_), channel_id=1, source_target_pairs={{0,1},{1,0},{2,3},{3,2},{4,5},{5,4},{6,7},{7,6},{8,9},{9,8},{10,11... | collective-permute-start | bytes 589832 | tf_op jit(solution)/shard_map/ppermute | solution.py:472
  46.0 9.4 %copy-start = (f32[40,2,128]{2,1,0:T(2,128)S(1)}, f32[40,2,128]{2,1,0:T(2,128)}, u32[]{:S(2)}) copy-start(f32[40,2,128]{2,1,0:T(2,128)} %recycled_ref.1) | copy-start | bytes 122884
